TPU v7x, 16 devices: a whole 2x2x2 slice. The times are simulated.
16 devices in a mesh: w: 4 (over z, y), h: 4 (over x, core).
Axes of the slice: x: 2, y: 2, z: 2, core: 2. Of those that a mesh axis runs over, the one named last changes fastest.
Arguments:
- image: bfloat16 [1, 96, 192, 640], P(None, 'h', 'w')
- w_first: bfloat16 [3, 3, 640, 640], replicated
- w_down: bfloat16 [3, 3, 640, 640], replicated
- grad_out: bfloat16 [1, 48, 96, 640], P(None, 'h', 'w')
Outputs:
- output 1: bfloat16 [1, 48, 96, 640], P(None, 'h', 'w')
- output 2: bfloat16 [1, 96, 192, 640], P(None, 'h', 'w')
- output 3: float32 [3, 3, 640, 640], replicated
- output 4: float32 [3, 3, 640, 640], replicated
All inputs are finite; a program needn't handle non-finite values.
Results may differ from a plain program's by a relative error of at most 0.0115483.
Values are sent between devices in bfloat16 or wider.
A program may use at most 1 GiB of HBM per device.

v0:
```python
import jax
import jax.numpy as jnp
from jax import lax
from jax.sharding import PartitionSpec as P

IMAGE_DIMS = ('NHWC', 'HWIO', 'NHWC')
BACK_DIMS = ('NHWC', 'HWOI', 'NHWC')
WGRAD_DIMS = ('CHWN', 'IHWO', 'HWNC')


def gelu_tanh(values):
    return jax.nn.gelu(values, approximate=True)


def conv_valid(lhs_in, kernel, stride):
    return lax.conv_general_dilated(lhs_in, kernel, (stride, stride), 'VALID', dimension_numbers=IMAGE_DIMS, preferred_element_type=jnp.float32)


def conv_back(grad_in, kernel, dilation, padding):
    return lax.conv_general_dilated(grad_in, jnp.flip(kernel, (0, 1)), (1, 1), padding, lhs_dilation=(dilation, dilation), dimension_numbers=BACK_DIMS, preferred_element_type=jnp.float32)


def weight_grad(lhs_in, grad_in, dilation, padding):
    return lax.conv_general_dilated(lhs_in, grad_in, (1, 1), padding, rhs_dilation=(dilation, dilation), dimension_numbers=WGRAD_DIMS, preferred_element_type=jnp.float32)


def solution(mesh):
    axis_len = {'h': mesh.shape['h'], 'w': mesh.shape['w']}

    def from_prev(tile_edge, axis_name):
        return lax.ppermute(tile_edge, axis_name, [(src_idx, src_idx + 1) for src_idx in range(axis_len[axis_name] - 1)])

    def from_next(tile_edge, axis_name):
        return lax.ppermute(tile_edge, axis_name, [(src_idx + 1, src_idx) for src_idx in range(axis_len[axis_name] - 1)])

    def extend(tile_in, axis_pos, axis_name, depth_lo, depth_hi):
        size_in = tile_in.shape[axis_pos]
        pieces = [tile_in]
        if depth_lo > 0:
            pieces = [from_prev(lax.slice_in_dim(tile_in, size_in - depth_lo, size_in, axis=axis_pos), axis_name)] + pieces
        if depth_hi > 0:
            pieces = pieces + [from_next(lax.slice_in_dim(tile_in, 0, depth_hi, axis=axis_pos), axis_name)]
        return jnp.concatenate(pieces, axis=axis_pos)

    def with_halo(tile_in, depth_lo, depth_hi):
        rows_ext = extend(tile_in, 1, 'h', depth_lo, depth_hi)
        return extend(rows_ext, 2, 'w', depth_lo, depth_hi)

    def block_step(image, w_first, w_down, grad_out):
        image_ext = with_halo(image, 1, 1)
        pre_act = conv_valid(image_ext, w_first, 1).astype(jnp.bfloat16)
        gelu_out, gelu_vjp = jax.vjp(gelu_tanh, pre_act.astype(jnp.float32))
        hidden = gelu_out.astype(jnp.bfloat16)
        hidden_ext = with_halo(hidden, 0, 1)
        block_out = conv_valid(hidden_ext, w_down, 2).astype(jnp.bfloat16)
        grad_ext = with_halo(grad_out, 1, 0)
        grad_hidden = conv_back(grad_ext, w_down, 2, ((0, 1), (0, 1)))
        grad_w_down = weight_grad(hidden_ext, grad_out, 2, ((0, 0), (0, 0)))
        grad_pre = gelu_vjp(grad_hidden)[0].astype(jnp.bfloat16)
        grad_pre_ext = with_halo(grad_pre, 1, 1)
        grad_image = conv_back(grad_pre_ext, w_first, 1, ((0, 0), (0, 0))).astype(jnp.bfloat16)
        grad_w_first = weight_grad(image_ext, grad_pre, 1, ((0, 0), (0, 0)))
        grad_w_first, grad_w_down = lax.psum((grad_w_first, grad_w_down), ('w', 'h'))
        return block_out, grad_image, grad_w_first, grad_w_down

    img_spec = P(None, 'h', 'w', None)
    return jax.shard_map(block_step, mesh=mesh, in_specs=(img_spec, P(), P(), img_spec), out_specs=(img_spec, img_spec, P(), P()), check_vma=False)
```

profile of v0, /device:TPU:0, one launch (start us, length us, event | category | flops | bytes accessed | tf_op | source)
XLA Modules:
  0.0 528.9 jit_solution(13843140099290386462)
XLA Ops:
  7.2 0.9 slice.71
  8.1 2.7 collective-permute-start.6
  10.8 0.9 fusion.64
  11.8 4.5 collective-permute-start
  16.4 1.3 collective-permute-start.1
  17.8 1.6 constant_dynamic-update-slice_fusion.4
  19.5 3.4 collective-permute-start.7
  23.1 2.7 constant_dynamic-update-slice_fusion.1
  26.0 3.4 collective-permute-start.2
  29.5 1.3 collective-permute-start.3
  30.8 2.1 pad_maximum_fusion.12
  32.9 3.1 collective-permute-done.3
  35.9 8.4 %pad_maximum_fusion = bf16[1,26,50,640]{3,0,2,1:T(2,128)(2,1)S(1)} fusion(bf16[1,26,1,640]{3,0,2,1:T(2,128)(2,1)S(1)} %collective-permute-done.3, bf16[1,26,48,640]{3,0,2,1:T(2,128)(2,1)S(1)} %constant_dynamic-update-slice_fusion, bf16[1,26,1,640]{3,0,2,1:T(2,128)(2,1)S(1)} %collective-permute-done.2), kind=kLoop, calls=%fused_computation.15 | loop fusion | flops 1664000 | bytes 3328000 | tf_op jit(solution)/shard_map/concatenate | solution.py:43
  44.4 1.7 copy-done
  46.1 0.3 copy.103
  46.4 1.4 pad
  47.8 2.6 reshape.10
  50.8 0.3 copy-done.14
  51.1 17.7 %add_multiply_fusion = (f32[24,8,7,640]{3,1,2,0:T(8,128)S(1)}, f32[24,8,7,640]{3,1,2,0:T(8,128)}, f32[24,8,7,640]{3,1,2,0:T(8,128)S(1)}, bf16[24,8,7,640]{3,1,2,0:T(8,128)(2,1)S(1)}, bf16[24,8,7,640]{3,1,2,0:T(8,128)(2,1)}) fusion(bf16[3,3,640,640]{3,2,1,0:T(8,128)(2,1)} %param.5, bf16[26,1,7,2,640]{4,2,3,0,1:T(8,128)(2,1)S(1)} %slice.64, ...), kind=kOutput, calls=%fused_computation.17 | convolution fusion | flops 9929134080 | bytes 23465016 | tf_op jit(solution)/shard_map/conv_general_dilated | solution.py:16
  69.0 0.7 copy.31
  69.7 1.8 slice.73
  71.5 1.2 slice_bitcast_fusion.1
  72.7 0.7 reshape.64
  73.4 1.7 slice.67
  75.1 1.5 collective-permute-start.4
  76.6 2.6 copy.35
  79.4 0.7 copy.37
  80.3 1.6 copy-done.9
  82.4 0.8 slice-done.1
  83.2 1.0 copy-done.7
  84.3 33.0 %fusion.14 = bf16[1,24,48,640]{3,0,2,1:T(2,128)(2,1)} fusion(f32[24,1,48,640]{3,0,2,1:T(8,128)S(1)} %slice.76, f32[24,1,48,640]{3,0,2,1:T(8,128)S(1)} %slice.75, f32[24,1,48,640]{3,0,2,1:T(8,128)S(1)} %slice.74, f32[24,1,48,640]{3,0,2,1:T(8,128)S(1)} %copy-done.7, bf16[3,3,640,640]{3,2,1,0:T(8,128)(2,1)S(1)} %bitcast.111, ...), kind=kOutput, calls=%fused_computation.31 | convolution fusion | flops 2130739200 | bytes 21059840 | tf_op jit(solution)/shard_map/conv_general_dilated | solution.py:20
  117.3 2.3 copy_dynamic-update-slice_fusion
  119.6 1.0 constant_dynamic-update-slice_fusion.3
  120.7 1.6 copy-done.5
  122.2 0.7 slice.68
  122.9 1.3 collective-permute-start.5
  124.2 57.4 %fusion.65 = f32[3,3,640,640]{3,2,1,0:T(8,128)} fusion(bf16[1,26,50,640]{3,0,2,1:T(2,128)(2,1)S(1)} %copy-done.1, bf16[1,24,48,640]{3,0,2,1:T(2,128)(2,1)} %fusion.14), kind=kOutput, calls=%fused_computation.88 | convolution fusion | flops 8493465600 | bytes 17884160 | tf_op jit(solution)/shard_map/conv_general_dilated | solution.py:24
  181.7 6.3 %pad_maximum_fusion.2 = bf16[1,25,49,640]{3,0,2,1:T(2,128)(2,1)S(1)} fusion(bf16[1,25,1,640]{3,0,2,1:T(2,128)(2,1)} %collective-permute-done.5, bf16[1,25,48,640]{3,0,2,1:T(2,128)(2,1)} %copy-done.5), kind=kLoop, calls=%fused_computation.18 | loop fusion | flops 784000 | bytes 3136000 | tf_op jit(solution)/shard_map/concatenate | solution.py:43
  187.9 1.6 copy-done.3
  189.6 19.5 %fusion.60 = f32[3,3,640,640]{3,2,1,0:T(8,128)} fusion(bf16[1,25,49,640]{3,0,2,1:T(2,128)(2,1)S(1)} %pad_maximum_fusion.2, bf16[1,12,24,640]{3,2,1,0:T(8,128)(2,1)S(1)} %copy-done.13), kind=kOutput, calls=%fused_computation.83 | convolution fusion | flops 2123366400 | bytes 16682240 | tf_op jit(solution)/shard_map/conv_general_dilated | solution.py:24
  209.1 1.8 copy-done.2
  211.2 3.2 collective-permute-start.8
  214.4 1.3 collective-permute-start.9
  215.7 3.2 collective-permute-done.9
  218.9 0.8 pad_maximum_fusion.9
  219.7 5.4 %collective-permute-start.10 = (bf16[1,26,1,640]{3,0,2,1:T(2,128)(2,1)}, bf16[1,26,1,640]{3,0,2,1:T(2,128)(2,1)}, u32[]{:S(2)}, u32[]{:S(2)}) collective-permute-start(bf16[1,26,1,640]{3,0,2,1:T(2,128)(2,1)} %get-tuple-element.10), channel_id=1, source_target_pairs={{0,4},{4,8},{8,12},{1,5},{5,9},{9,13},{2,6},{6,10},{10,14},{3,7},{... | collective-permute-start | bytes 99848 | tf_op jit(solution)/shard_map/ppermute | solution.py:31
  225.1 1.5 collective-permute-start.11
  226.6 0.3 copy.104
  226.9 0.3 pad_bitcast_fusion
  227.2 0.4 copy.27
  227.7 1.0 slice-done.2
  228.8 1.1 slice-done.3
  229.9 3.7 fusion.43
  233.7 0.9 reshape.21
  234.6 1.8 slice_bitcast_fusion.2
  236.4 13.3 %pad_maximum_fusion.1 = bf16[1,26,50,640]{3,0,2,1:T(2,128)(2,1)S(1)} fusion(bf16[1,26,1,640]{3,0,2,1:T(2,128)(2,1)} %collective-permute-done.11, bf16[1,1,48,640]{3,0,2,1:T(2,128)(2,1)} %copy-done.12, bf16[1,24,48,640]{3,0,2,1:T(2,128)(2,1)S(1)} %copy-done.2, bf16[1,1,48,640]{3,0,2,1:T(2,128)(2,1)} %copy-done.11, ...), kind=kLoop, calls=%fused_computation.16 | loop fusion | flops 3328000 | bytes 3328000 | tf_op jit(solution)/shard_map/concatenate | solution.py:43
  249.7 0.3 copy.102
  250.0 1.4 pad.4
  251.4 2.6 reshape.24
  254.7 15.0 %select_convert_fusion = bf16[24,8,7,640]{3,1,2,0:T(8,128)(2,1)S(1)} fusion(pred[8,7]{0,1:T(8,128)(4,1)S(1)} %copy-done.15, bf16[3,3,640,640]{3,2,1,0:T(8,128)(2,1)} %param.5, bf16[26,1,7,2,640]{4,2,3,0,1:T(8,128)(2,1)S(1)} %slice.79, bf16[26,1,8,7,640]{4,2,3,0,1:T(8,128)(2,1)S(1)} %copy.40), kind=kOutput, calls=%fused_computation.11 | convolution fusion | flops 9917952000 | bytes 11422776 | tf_op jit(solution)/shard_map/conv_general_dilated | solution.py:20
  270.0 1.3 copy.43
  271.3 227.2 %all-reduce.3.cloned.1.call-done = (f32[3,3,640,640]{3,2,1,0:T(8,128)}, f32[3,3,640,640]{3,2,1,0:T(8,128)}) async-done(((f32[3,3,640,640]{3,2,1,0:T(8,128)}, f32[3,3,640,640]{3,2,1,0:T(8,128)}), (f32[3,3,640,640]{3,2,1,0:T(8,128)}, f32[3,3,640,640]{3,2,1,0:T(8,128)})) %all-reduce.3.cloned.1.call-update) | async-done | bytes 29491216 | tf_op jit(solution)/shard_map/psum | solution.py:63
  498.5 11.6 %copy.111 = f32[3,3,640,640]{3,2,1,0:T(8,128)} copy(f32[3,3,640,640]{3,2,1,0:T(8,128)} %get-tuple-element.25) | data formatting | bytes 29491200
  510.2 11.6 %copy.112 = f32[3,3,640,640]{3,2,1,0:T(8,128)} copy(f32[3,3,640,640]{3,2,1,0:T(8,128)} %get-tuple-element.26) | data formatting | bytes 29491200
  (70 shorter events, 4.1 us)
Async XLA Ops:
  7.2 15.9 %copy-start.8 = (bf16[1,24,48,640]{3,2,1,0:T(8,128)(2,1)S(1)}, bf16[1,24,48,640]{3,2,1,0:T(8,128)(2,1)}, u32[]{:S(2)}) copy-start(bf16[1,24,48,640]{3,2,1,0:T(8,128)(2,1)} %param.4) | copy-start | bytes 4423684
  7.2 491.4 %all-reduce.3.cloned.1.call-start = ((), (), s32[]{:S(2)}) async-start(), calls=%async_computation | async-start | bytes 58982400 | tf_op jit(solution)/shard_map/psum | solution.py:63
  8.1 9.6 %collective-permute-start.6 = (bf16[1,1,24,640]{3,0,2,1:T(2,128)(2,1)S(1)}, bf16[1,1,24,640]{3,0,2,1:T(2,128)(2,1)S(1)}, u32[]{:S(2)}, u32[]{:S(2)}) collective-permute-start(bf16[1,1,24,640]{3,0,2,1:T(2,128)(2,1)S(1)} %copy.97), channel_id=1, source_target_pairs={{0,1},{1,2},{2,3},{4,5},{5,6},{6,7},{8,9},{9,10},{10,11},{12,13},{... | collective-permute-start | bytes 92168 | tf_op jit(solution)/shard_map/ppermute | solution.py:31
  11.8 11.1 %collective-permute-start = (bf16[1,1,48,640]{3,0,2,1:T(2,128)(2,1)S(1)}, bf16[1,1,48,640]{3,0,2,1:T(2,128)(2,1)S(1)}, u32[]{:S(2)}, u32[]{:S(2)}) collective-permute-start(bf16[1,1,48,640]{3,0,2,1:T(2,128)(2,1)S(1)} %copy.95), channel_id=1, source_target_pairs={{0,1},{1,2},{2,3},{4,5},{5,6},{6,7},{8,9},{9,10},{10,11},{12,13},{... | collective-permute-start | bytes 184328 | tf_op jit(solution)/shard_map/ppermute | solution.py:31
  16.4 9.3 %collective-permute-start.1 = (bf16[1,1,48,640]{3,0,2,1:T(2,128)(2,1)S(1)}, bf16[1,1,48,640]{3,0,2,1:T(2,128)(2,1)S(1)}, u32[]{:S(2)}, u32[]{:S(2)}) collective-permute-start(bf16[1,1,48,640]{3,0,2,1:T(2,128)(2,1)S(1)} %copy.96), channel_id=1, source_target_pairs={{1,0},{2,1},{3,2},{5,4},{6,5},{7,6},{9,8},{10,9},{11,10},{13,12},{... | collective-permute-start | bytes 184328 | tf_op jit(solution)/shard_map/ppermute | solution.py:34
  19.5 11.3 %collective-permute-start.7 = (bf16[1,13,1,640]{3,0,2,1:T(2,128)(2,1)S(1)}, bf16[1,13,1,640]{3,0,2,1:T(2,128)(2,1)S(1)}, u32[]{:S(2)}, u32[]{:S(2)}) collective-permute-start(bf16[1,13,1,640]{3,0,2,1:T(2,128)(2,1)S(1)} %slice.72), channel_id=1, source_target_pairs={{0,4},{4,8},{8,12},{1,5},{5,9},{9,13},{2,6},{6,10},{10,14},{3,7},{... | collective-permute-start | bytes 49928 | tf_op jit(solution)/shard_map/ppermute | solution.py:31
  26.0 6.8 %collective-permute-start.2 = (bf16[1,26,1,640]{3,0,2,1:T(2,128)(2,1)S(1)}, bf16[1,26,1,640]{3,0,2,1:T(2,128)(2,1)S(1)}, u32[]{:S(2)}, u32[]{:S(2)}) collective-permute-start(bf16[1,26,1,640]{3,0,2,1:T(2,128)(2,1)S(1)} %get-tuple-element.12), channel_id=1, source_target_pairs={{0,4},{4,8},{8,12},{1,5},{5,9},{9,13},{2,6},{6,10},{10,14},{3,7},{... | collective-permute-start | bytes 99848 | tf_op jit(solution)/shard_map/ppermute | solution.py:31
  29.5 6.5 %collective-permute-start.3 = (bf16[1,26,1,640]{3,0,2,1:T(2,128)(2,1)S(1)}, bf16[1,26,1,640]{3,0,2,1:T(2,128)(2,1)S(1)}, u32[]{:S(2)}, u32[]{:S(2)}) collective-permute-start(bf16[1,26,1,640]{3,0,2,1:T(2,128)(2,1)S(1)} %get-tuple-element.13), channel_id=1, source_target_pairs={{4,0},{8,4},{12,8},{5,1},{9,5},{13,9},{6,2},{10,6},{14,10},{7,3},{... | collective-permute-start | bytes 99848 | tf_op jit(solution)/shard_map/ppermute | solution.py:34
  44.4 1.7 copy-start
  50.4 0.7 copy-start.14
  75.1 44.5 %collective-permute-start.4 = (bf16[1,1,48,640]{3,0,2,1:T(2,128)(2,1)}, bf16[1,1,48,640]{3,0,2,1:T(2,128)(2,1)}, u32[]{:S(2)}, u32[]{:S(2)}) collective-permute-start(bf16[1,1,48,640]{3,0,2,1:T(2,128)(2,1)} %slice.67), channel_id=1, source_target_pairs={{1,0},{2,1},{3,2},{5,4},{6,5},{7,6},{9,8},{10,9},{11,10},{13,12},{... | collective-permute-start | bytes 184328 | tf_op jit(solution)/shard_map/ppermute | solution.py:34
  79.4 2.9 slice-start
  80.1 1.8 copy-start.9
  80.1 3.0 slice-start.1
  82.1 2.0 copy-start.7
  82.1 2.2 copy-start.10
  84.3 33.0 %copy-start.6 = (bf16[1,24,48,640]{3,1,2,0:T(8,128)(2,1)S(1)}, bf16[1,24,48,640]{3,1,2,0:T(8,128)(2,1)}, u32[]{:S(2)}) copy-start(bf16[1,24,48,640]{3,1,2,0:T(8,128)(2,1)} %slice_bitcast_fusion.1) | copy-start | bytes 4423684
  117.3 6.9 %copy-start.1 = (bf16[1,26,50,640]{3,0,2,1:T(2,128)(2,1)S(1)}, bf16[1,26,50,640]{3,0,2,1:T(2,128)(2,1)}, u32[]{:S(2)}) copy-start(bf16[1,26,50,640]{3,0,2,1:T(2,128)(2,1)} %copy-done) | copy-start | bytes 4992004
  120.6 1.6 copy-start.5
  122.9 58.7 %collective-permute-start.5 = (bf16[1,25,1,640]{3,0,2,1:T(2,128)(2,1)}, bf16[1,25,1,640]{3,0,2,1:T(2,128)(2,1)}, u32[]{:S(2)}, u32[]{:S(2)}) collective-permute-start(bf16[1,25,1,640]{3,0,2,1:T(2,128)(2,1)} %slice.68), channel_id=1, source_target_pairs={{4,0},{8,4},{12,8},{5,1},{9,5},{13,9},{6,2},{10,6},{14,10},{7,3},{... | collective-permute-start | bytes 96008 | tf_op jit(solution)/shard_map/ppermute | solution.py:34
  181.6 7.9 %copy-start.13 = (bf16[1,12,24,640]{3,2,1,0:T(8,128)(2,1)S(1)}, bf16[1,12,24,640]{3,2,1,0:T(8,128)(2,1)}, u32[]{:S(2)}) copy-start(bf16[1,12,24,640]{3,2,1,0:T(8,128)(2,1)} %param.7) | copy-start | bytes 1105924
  187.9 1.6 copy-start.3
  209.1 1.8 copy-start.2
  210.9 15.6 %copy-start.4 = (bf16[1,25,49,640]{3,0,2,1:T(2,128)(2,1)S(1)}, bf16[1,25,49,640]{3,0,2,1:T(2,128)(2,1)}, u32[]{:S(2)}) copy-start(bf16[1,25,49,640]{3,0,2,1:T(2,128)(2,1)} %copy-done.3) | copy-start | bytes 4704004
  211.2 4.5 collective-permute-start.8
  214.4 4.5 collective-permute-start.9
  215.7 9.4 %copy-start.11 = (bf16[1,1,48,640]{3,0,2,1:T(2,128)(2,1)}, bf16[1,1,48,640]{3,0,2,1:T(2,128)(2,1)S(1)}, u32[]{:S(2)}) copy-start(bf16[1,1,48,640]{3,0,2,1:T(2,128)(2,1)S(1)} %collective-permute-done.8) | copy-start | bytes 184324
  218.9 6.2 %copy-start.12 = (bf16[1,1,48,640]{3,0,2,1:T(2,128)(2,1)}, bf16[1,1,48,640]{3,0,2,1:T(2,128)(2,1)S(1)}, u32[]{:S(2)}) copy-start(bf16[1,1,48,640]{3,0,2,1:T(2,128)(2,1)S(1)} %collective-permute-done.9) | copy-start | bytes 184324
  219.7 16.7 %collective-permute-start.10 = (bf16[1,26,1,640]{3,0,2,1:T(2,128)(2,1)}, bf16[1,26,1,640]{3,0,2,1:T(2,128)(2,1)}, u32[]{:S(2)}, u32[]{:S(2)}) collective-permute-start(bf16[1,26,1,640]{3,0,2,1:T(2,128)(2,1)} %get-tuple-element.10), channel_id=1, source_target_pairs={{0,4},{4,8},{8,12},{1,5},{5,9},{9,13},{2,6},{6,10},{10,14},{3,7},{... | collective-permute-start | bytes 99848 | tf_op jit(solution)/shard_map/ppermute | solution.py:31
  225.1 11.3 %collective-permute-start.11 = (bf16[1,26,1,640]{3,0,2,1:T(2,128)(2,1)S(1)}, bf16[1,26,1,640]{3,0,2,1:T(2,128)(2,1)}, u32[]{:S(2)}, u32[]{:S(2)}) collective-permute-start(bf16[1,26,1,640]{3,0,2,1:T(2,128)(2,1)S(1)} %get-tuple-element.11), channel_id=1, source_target_pairs={{4,0},{8,4},{12,8},{5,1},{9,5},{13,9},{6,2},{10,6},{14,10},{7,3},{... | collective-permute-start | bytes 99848 | tf_op jit(solution)/shard_map/ppermute | solution.py:34
  226.6 2.2 slice-start.2
  226.9 2.9 slice-start.3
  227.2 2.6 copy-start.16
  254.0 0.7 copy-start.15
Sparse Core Ops, SparseCore 0:
  209.2 289.2 all-reduce.2
where the time goes:
time: 535 us; the launch traced here: 529 us
  waiting for transfers between devices  234 us (44%)
  matrix products  146 us (27%)
  local copies, waits for them, and re-layouts  72.7 us (14%)
  other arithmetic  30.9 us (6%)
  starting transfers between devices  30.7 us (6%)
  between operations  14.9 us (3%)
    psum x1, waiting for transfers between devices, block_step(): lax.psum((grad_w_first, grad_w_down), ('w', 'h'))  227 us
    conv_general_dilated x2, matrix products, weight_grad(): lax.conv_general_dilated(lhs_in, grad_in, (1, 1), padding, rhs_dilation=(...  76.9 us
    conv_general_dilated x2, matrix products, conv_back(): lax.conv_general_dilated(grad_in, jnp.flip(kernel, (0, 1)), (1, 1), paddi...  47.9 us
    unnamed x55, local copies, waits for them, and re-layouts  43.9 us
    concatenate x3, other arithmetic, extend(): return jnp.concatenate(pieces, axis=axis_pos)  28 us
    ppermute x6, starting transfers between devices, from_prev(): lax.ppermute(tile_edge, axis_name, [(src_idx, src_idx + 1) for src_idx in...  22.6 us
    conv_general_dilated x2, matrix products, conv_valid(): lax.conv_general_dilated(lhs_in, kernel, (stride, stride), 'VALID', dimen...  21.4 us
  transfers between devices with their start and end apart: 13, of which 3 were waited for; matrix products, arithmetic and copies ran while one was open for 28% of the time, Pallas kernels for 0%

commit v1 on v0

v1 whole, which is shorter than its diff:
```python
import jax
import jax.numpy as jnp
from jax import lax
from jax.sharding import PartitionSpec as P
from jax.experimental import pallas as pl
from jax.experimental.pallas import tpu as pltpu

MESH = pl.DeviceIdType.MESH
F32, BF16 = jnp.float32, jnp.bfloat16
C = 640
ROWS, COLS = 24, 48
OUT_R, OUT_C = 12, 24
PIX, OPIX = ROWS * COLS, OUT_R * OUT_C
HALF = 320
MIB = 2 ** 20
ORDERS = (('x', 'y', 'z'), ('y', 'z', 'x'), ('z', 'x', 'y'))
R1, R2, R3, A1, A2, A3A, A3B, DA, DB, DC, LA, LB, LC = range(13)


def gelu_tanh(values):
    return jax.nn.gelu(values, approximate=True)


def dot(lhs, rhs):
    return lax.dot_general(lhs, rhs, (((1,), (0,)), ((), ())), preferred_element_type=F32)


def dot_rhs_t(lhs, rhs):
    return lax.dot_general(lhs, rhs, (((1,), (1,)), ((), ())), preferred_element_type=F32)


def dot_lhs_t(lhs, rhs):
    return lax.dot_general(lhs, rhs, (((0,), (0,)), ((), ())), preferred_element_type=F32)


VM = pl.BlockSpec(memory_space=pltpu.VMEM)
ANY = pl.BlockSpec(memory_space=pl.ANY)


def shift_columns(ext_ref, out_ref):
    def one_row(r, _):
        for c in range(3):
            out_ref[c, pl.ds(pl.multiple_of(r * COLS, COLS), COLS), :] = ext_ref[r, c:c + COLS, :]
        return 0
    lax.fori_loop(0, ROWS + 2, one_row, 0)


def conv_first_kernel(ext_ref, w_ref, a_ref, z_ref, cat, sa, sz):
    step = pl.program_id(0)

    @pl.when(step == 0)
    def _():
        def one_row(r, _):
            for c in range(3):
                cat[pl.ds(pl.multiple_of(r * COLS, COLS), COLS), c * C:(c + 1) * C] = ext_ref[r, c:c + COLS, :]
            return 0
        lax.fori_loop(0, ROWS + 2, one_row, 0)

    block = 8 * COLS
    acc = None
    for a in range(3):
        rows = pl.ds(pl.multiple_of(step * block + a * COLS, COLS), block)
        part = dot(cat[rows, :], w_ref[a])
        acc = part if acc is None else acc + part
    pre = acc.astype(BF16).astype(F32)
    act = gelu_tanh(pre).astype(BF16).astype(F32)
    for lane in range(5):
        sa[lane] = pre[:, lane * 128:(lane + 1) * 128]
        sz[lane] = act[:, lane * 128:(lane + 1) * 128]
    for r in range(8):
        for cp in range(2):
            for lane in range(5):
                rows, lanes = pl.ds(r * COLS + cp, OUT_C, stride=2), pl.ds(lane * 128, 128)
                a_ref[r % 2, cp, r // 2, :, lanes] = sa[lane, rows, :]
                z_ref[r % 2, cp, r // 2, :, lanes] = sz[lane, rows, :]


def conv_first(image_ext, w_first):
    shape = jax.ShapeDtypeStruct((2, 2, OUT_R, OUT_C, C), F32)
    spec = pl.BlockSpec((2, 2, 4, OUT_C, C), lambda i: (0, 0, i, 0, 0))
    return pl.pallas_call(
        conv_first_kernel, grid=(3,), out_shape=[shape, shape],
        in_specs=[pl.BlockSpec(image_ext.shape, lambda i: (0, 0, 0)), pl.BlockSpec((3, 3 * C, C), lambda i: (0, 0, 0))],
        out_specs=[spec, spec],
        scratch_shapes=[pltpu.VMEM(((ROWS + 2) * COLS, 3 * C), BF16), pltpu.VMEM((5, 8 * COLS, 128), F32), pltpu.VMEM((5, 8 * COLS, 128), F32)],
        compiler_params=pltpu.CompilerParams(vmem_limit_bytes=56 * MIB),
        cost_estimate=pl.CostEstimate(flops=2 * PIX * 9 * C * C, bytes_accessed=16 * MIB, transcendentals=PIX * C),
    )(image_ext, w_first.reshape(3, 3 * C, C))


def weight_down_kernel(z_ref, zp_ref, g_ref, gp_ref, out_ref, taps, gs):
    core = lax.axis_index('h') % 2
    for src, (zr, gr) in enumerate(((z_ref, g_ref), (zp_ref, gp_ref))):
        gs[src * OPIX:(src + 1) * OPIX, :] = gr[1:, 1:, :].reshape(OPIX, C).astype(BF16)
        for t in range(9):
            a, c = t // 3, t % 3
            tap = zr[a % 2, c % 2, a // 2:a // 2 + OUT_R, c // 2:c // 2 + OUT_C, :]
            taps[t, src * OPIX:(src + 1) * OPIX, :] = tap.reshape(OPIX, C).astype(BF16)

    def one(j, _):
        res = dot_lhs_t(taps[4 * core + j], gs[...])
        out_ref[2 * j] = res[:HALF]
        out_ref[2 * j + 1] = res[HALF:]
        return 0
    lax.fori_loop(0, 5, one, 0)


def weight_down(z_own, z_pair, g_own, g_pair):
    return pl.pallas_call(
        weight_down_kernel, out_shape=jax.ShapeDtypeStruct((10, HALF, C), F32), in_specs=[VM] * 4, out_specs=VM,
        scratch_shapes=[pltpu.VMEM((9, 2 * OPIX, C), BF16), pltpu.VMEM((2 * OPIX, C), BF16)],
        compiler_params=pltpu.CompilerParams(vmem_limit_bytes=56 * MIB),
        cost_estimate=pl.CostEstimate(flops=2 * OPIX * 9 * C * C, bytes_accessed=16 * MIB, transcendentals=0),
    )(z_own, z_pair, g_own, g_pair)


def conv_down_kernel(z_ref, w_ref, y_ref, acc):
    for t in range(9):
        a, c = t // 3, t % 3
        tap = z_ref[a % 2, c % 2, a // 2:a // 2 + OUT_R, c // 2:c // 2 + OUT_C, :].reshape(OPIX, C).astype(BF16)
        part = dot(tap, w_ref[t])
        acc[...] = part if t == 0 else acc[...] + part
    y_ref[...] = acc[...].astype(BF16)


def conv_down(z_own, w_down):
    return pl.pallas_call(
        conv_down_kernel, out_shape=jax.ShapeDtypeStruct((OPIX, C), BF16), in_specs=[VM] * 2, out_specs=VM,
        scratch_shapes=[pltpu.VMEM((OPIX, C), F32)],
        compiler_params=pltpu.CompilerParams(vmem_limit_bytes=56 * MIB),
        cost_estimate=pl.CostEstimate(flops=2 * OPIX * 9 * C * C, bytes_accessed=12 * MIB, transcendentals=0),
    )(z_own, w_down)


def grad_pre_kernel(g_ref, a_ref, w_ref, out_ref, gs, sd):
    for di in range(2):
        for dj in range(2):
            gs[di, dj] = g_ref[di:di + OUT_R, dj:dj + OUT_C, :].reshape(OPIX, C).astype(BF16)
    for rp in range(2):
        for cp in range(2):
            acc = None
            for a in ((0, 2), (1,))[rp]:
                for c in ((0, 2), (1,))[cp]:
                    part = dot_rhs_t(gs[1 - a // 2, 1 - c // 2], w_ref[3 * a + c])
                    acc = part if acc is None else acc + part
            pre = a_ref[rp, cp].reshape(OPIX, C)
            grad = jax.vjp(gelu_tanh, pre)[1](acc)[0].astype(BF16).astype(F32)
            for i in range(OUT_R):
                for lane in range(5):
                    rows = pl.ds((2 * i + rp) * COLS + cp, OUT_C, stride=2)
                    sd[lane, rows, :] = grad[i * OUT_C:(i + 1) * OUT_C, lane * 128:(lane + 1) * 128]
    for lane in range(5):
        out_ref[:, lane * 128:(lane + 1) * 128] = sd[lane].astype(BF16)


def grad_pre_call(g_ext, a_own, w_down):
    return pl.pallas_call(
        grad_pre_kernel, out_shape=jax.ShapeDtypeStruct((PIX, C), BF16), in_specs=[VM] * 3, out_specs=VM,
        scratch_shapes=[pltpu.VMEM((2, 2, OPIX, C), BF16), pltpu.VMEM((5, PIX, 128), F32)],
        compiler_params=pltpu.CompilerParams(vmem_limit_bytes=56 * MIB),
        cost_estimate=pl.CostEstimate(flops=2 * OPIX * 9 * C * C, bytes_accessed=12 * MIB, transcendentals=PIX * C),
    )(g_ext, a_own, w_down)


def weight_first_kernel(x_ref, xp_ref, d_ref, dp_ref, out_ref, xs):
    core = lax.axis_index('h') % 2
    for src, ref in enumerate((x_ref, xp_ref)):
        shift_columns(ref, xs.at[src])

    def one(j, _):
        t = 4 * core + j
        a, c = t // 3, t % 3
        rows = pl.ds(pl.multiple_of(a * COLS, COLS), PIX)
        res = dot_lhs_t(xs[0, c, rows, :], d_ref[...]) + dot_lhs_t(xs[1, c, rows, :], dp_ref[...])
        out_ref[2 * j] = res[:HALF]
        out_ref[2 * j + 1] = res[HALF:]
        return 0
    lax.fori_loop(0, 5, one, 0)


def weight_first(x_own, x_pair, d_own, d_pair):
    return pl.pallas_call(
        weight_first_kernel, out_shape=jax.ShapeDtypeStruct((10, HALF, C), F32), in_specs=[VM] * 4, out_specs=VM,
        scratch_shapes=[pltpu.VMEM((2, 3, (ROWS + 2) * COLS, C), BF16)],
        compiler_params=pltpu.CompilerParams(vmem_limit_bytes=56 * MIB),
        cost_estimate=pl.CostEstimate(flops=2 * PIX * 9 * C * C, bytes_accessed=16 * MIB, transcendentals=0),
    )(x_own, x_pair, d_own, d_pair)


def grad_image_kernel(d_ref, w_ref, out_ref, ds, acc):
    shift_columns(d_ref, ds)
    block = 8 * COLS

    def one(i, _):
        for t in range(9):
            a, c = t // 3, t % 3
            rows = pl.ds(pl.multiple_of(i * block + (2 - a) * COLS, COLS), block)
            part = dot_rhs_t(ds[2 - c, rows, :], w_ref[t])
            acc[...] = part if t == 0 else acc[...] + part
        out_ref[pl.ds(pl.multiple_of(i * block, block), block), :] = acc[...].astype(BF16)
        return 0
    lax.fori_loop(0, 3, one, 0)


def grad_image_call(d_ext, w_first):
    return pl.pallas_call(
        grad_image_kernel, out_shape=jax.ShapeDtypeStruct((PIX, C), BF16), in_specs=[VM] * 2, out_specs=VM,
        scratch_shapes=[pltpu.VMEM((3, (ROWS + 2) * COLS, C), BF16), pltpu.VMEM((8 * COLS, C), F32)],
        compiler_params=pltpu.CompilerParams(vmem_limit_bytes=56 * MIB),
        cost_estimate=pl.CostEstimate(flops=2 * PIX * 9 * C * C, bytes_accessed=16 * MIB, transcendentals=0),
    )(d_ext, w_first)


def place():
    w, h = lax.axis_index('w'), lax.axis_index('h')
    bit = {'x': h // 2, 'c': h % 2, 'y': w % 2, 'z': w // 2}
    dev = {'x': (w, (h + 2) % 4), 'c': (w, h + 1 - 2 * (h % 2)), 'y': (w + 1 - 2 * (w % 2), h), 'z': ((w + 2) % 4, h)}
    return bit, dev


class Reducer:
    def __init__(self, index, own, land, out, sems, grants, bit, dev):
        self.index, self.own, self.land, self.out, self.sems, self.grants, self.bit, self.dev = index, own, land, out, sems, grants, bit, dev

    def starts(self, third):
        b = [self.bit[axis] for axis in ORDERS[third]]
        base2 = b[0] * 160
        base3 = base2 + b[1] * 80
        return b, base2, base3, base3 + b[2] * 40

    def copy(self, third, kind):
        b, base2, base3, base4 = self.starts(third)
        core = self.bit['c']
        far = (1 - b[0]) * 160
        src, size, axis = {
            R1: (far, 160, 0), R2: (base2 + (1 - b[1]) * 80, 80, 1), R3: (base3 + (1 - b[2]) * 40, 40, 2),
            A1: (base4, 40, 2), A2: (base3, 80, 1), A3A: (base3, 80, 0), A3B: (base2 + (1 - b[1]) * 80, 80, 0),
            DA: (base2, 160, 'c'), DB: (far + b[1] * 80, 80, 'c'), DC: (far + (1 - b[1]) * 80, 80, 'c'),
            LA: (base2, 160, None), LB: (far + b[1] * 80, 80, None), LC: (far + (1 - b[1]) * 80, 80, None),
        }[kind]
        rows = pl.ds(pl.multiple_of(src, 8), size)
        source = self.own.at[pl.ds(core + 3 * third, 3), rows]
        send, recv = (s.at[self.index, third, kind] for s in self.sems)
        if kind <= R3:
            target = self.land.at[pl.ds(3 * third, 3), pl.ds((0, 160, 240)[kind], size)]
        elif kind <= A3B:
            target = source
        else:
            target = self.out.at[pl.ds(9 * core + 3 * third, 3), rows]
        if axis is None:
            return pltpu.make_async_copy(source, target, recv)
        peer = self.dev[axis if axis == 'c' else ORDERS[third][axis]]
        return pltpu.make_async_remote_copy(src_ref=source, dst_ref=target, send_sem=send, recv_sem=recv, device_id=peer, device_id_type=MESH)

    def add(self, third, kind):
        _, base2, base3, base4 = self.starts(third)
        keep, size = ((base2, 160), (base3, 80), (base4, 40))[kind]
        land_at = (0, 160, 240)[kind]
        steps = size // 40

        def body(j, _):
            unit, row = 3 * third + j // steps, (j % steps) * 40
            rows = pl.ds(pl.multiple_of(keep + row, 8), 40)
            where = self.bit['c'] + unit
            self.own[where, rows, :] += self.land[unit, pl.ds(pl.multiple_of(land_at + row, 8), 40), :]
            return 0
        lax.fori_loop(0, 3 * steps, body, 0)

    def begin(self):
        for third in range(3):
            self.copy(third, R1).start()

    def move(self, wait_for, then, add=False):
        for third in range(3):
            self.copy(third, wait_for).wait()
            if add:
                pl.semaphore_signal(self.grants.at[self.index, third, wait_for], inc=1, device_id=self.dev[ORDERS[third][wait_for]], device_id_type=MESH)
                self.add(third, wait_for)
            for kind in then:
                if kind in (A1, A2, A3A):
                    pl.semaphore_wait(self.grants.at[self.index, third, {A1: R3, A2: R2, A3A: R1}[kind]], 1)
                self.copy(third, kind).start()

    def finish(self):
        for kind in (DA, DB, DC, LA, LB, LC):
            self.move(kind, ())


def reduce_kernel(p_down, p_first, o_down, o_first, own_d, own_f, land_d, land_f, local_sems, send_sems, recv_sems, grants):
    bit, dev = place()
    loads = [pltpu.make_async_copy(p, o, local_sems.at[i]) for i, (p, o) in enumerate(((p_down, own_d), (p_first, own_f)))]
    for load in loads:
        load.start()
    barrier = pltpu.get_barrier_semaphore()
    for axis in 'xyzc':
        pl.semaphore_signal(barrier, inc=1, device_id=dev[axis], device_id_type=MESH)
    pl.semaphore_wait(barrier, 4)
    sems = (send_sems, recv_sems)
    both = [Reducer(0, own_d, land_d, o_down, sems, grants, bit, dev), Reducer(1, own_f, land_f, o_first, sems, grants, bit, dev)]
    for load, one in zip(loads, both):
        load.wait()
        one.begin()
    for kind in (R1, R2, R3):
        for one in both:
            one.move(kind, (kind + 1,), add=True)
    for one in both:
        one.move(A1, (A2, A3A))
    for one in both:
        one.move(A2, (A3B, DA, LA))
    for one in both:
        one.move(A3A, (DB, LB))
    for one in both:
        one.move(A3B, (DC, LC))
    for one in both:
        one.finish()


def reduce_all(p_down, p_first):
    shape = jax.ShapeDtypeStruct((18, HALF, C), F32)
    return pl.pallas_call(
        reduce_kernel, out_shape=[shape, shape], in_specs=[ANY] * 2, out_specs=[ANY] * 2,
        scratch_shapes=[pltpu.VMEM((10, HALF, C), F32)] * 2 + [pltpu.VMEM((9, 280, C), F32)] * 2
        + [pltpu.SemaphoreType.DMA((2,)), pltpu.SemaphoreType.DMA((2, 3, 13)), pltpu.SemaphoreType.DMA((2, 3, 13)), pltpu.SemaphoreType.REGULAR((2, 3, 3))],
        compiler_params=pltpu.CompilerParams(collective_id=1, has_side_effects=True, vmem_limit_bytes=56 * MIB),
        cost_estimate=pl.CostEstimate(flops=2 * PIX * 90 * C * C, bytes_accessed=64 * MIB, transcendentals=0),
    )(p_down, p_first)


def settle_kernel(in_a, in_b, out_a, out_b, buf, load_sems, store_sems):
    loads, stores = [], []
    for i, (src, dst) in enumerate(((in_a, out_a), (in_b, out_b))):
        for part in range(9):
            span = pl.ds(2 * part, 2)
            loads.append(pltpu.make_async_copy(src.at[span], buf.at[i, span], load_sems.at[i, part]))
            stores.append(pltpu.make_async_copy(buf.at[i, span], dst.at[span], store_sems.at[i, part]))
    for load in loads:
        load.start()
    for load, store in zip(loads, stores):
        load.wait()
        store.start()
    for store in stores:
        store.wait()


def settle(sum_a, sum_b):
    shape = jax.ShapeDtypeStruct((18, HALF, C), F32)
    return pl.pallas_call(
        settle_kernel, out_shape=[shape, shape], in_specs=[ANY] * 2, out_specs=[ANY] * 2,
        scratch_shapes=[pltpu.VMEM((2, 18, HALF, C), F32), pltpu.SemaphoreType.DMA((2, 9)), pltpu.SemaphoreType.DMA((2, 9))],
        compiler_params=pltpu.CompilerParams(vmem_limit_bytes=56 * MIB),
    )(sum_a, sum_b)


def solution(mesh):
    axis_len = {'h': mesh.shape['h'], 'w': mesh.shape['w']}

    def from_prev(edge, axis):
        return lax.ppermute(edge, axis, [(i, i + 1) for i in range(axis_len[axis] - 1)])

    def from_next(edge, axis):
        return lax.ppermute(edge, axis, [(i + 1, i) for i in range(axis_len[axis] - 1)])

    def swap_core(value):
        return lax.ppermute(value, 'h', [(i, i ^ 1) for i in range(axis_len['h'])])

    def frame(tile):
        rows = jnp.concatenate([from_prev(tile[-1:], 'h'), tile, from_next(tile[:1], 'h')], 0)
        return jnp.concatenate([from_prev(rows[:, -1:], 'w'), rows, from_next(rows[:, :1], 'w')], 1)

    def block_step(image, w_first, w_down, grad_out):
        image, grad_out = image[0], grad_out[0]
        x_own = frame(image)
        g_rows = jnp.concatenate([from_prev(grad_out[-1:], 'h'), grad_out], 0)
        g_own = jnp.concatenate([from_prev(g_rows[:, -1:], 'w'), g_rows], 1)
        x_pair, g_pair = swap_core(x_own), swap_core(g_own)
        a_own, z_tile = conv_first(x_own, w_first)
        z_rows = jnp.concatenate([z_tile, jnp.pad(from_next(z_tile[:1, :, :1], 'h'), ((0, 1),) + ((0, 0),) * 4)], 2)
        z_own = jnp.concatenate([z_rows, jnp.pad(from_next(z_rows[:, :1, :, :1], 'w'), ((0, 0), (0, 1)) + ((0, 0),) * 3)], 3)
        z_pair = swap_core(z_own)
        g_f32, gp_f32 = g_own.astype(F32), g_pair.astype(F32)
        p_down = weight_down(z_own, z_pair, g_f32, gp_f32)
        w_taps = w_down.reshape(9, C, C)
        grad_pre = grad_pre_call(g_f32, a_own, w_taps)
        d_pair = swap_core(grad_pre)
        p_first = weight_first(x_own, x_pair, grad_pre, d_pair)
        block_out = conv_down(z_own, w_taps)
        grad_image = grad_image_call(frame(grad_pre.reshape(ROWS, COLS, C)), w_first.reshape(9, C, C))
        grad_w_down, grad_w_first = settle(*reduce_all(p_down, p_first))
        return (block_out.reshape(1, OUT_R, OUT_C, C), grad_image.reshape(1, ROWS, COLS, C),
                grad_w_first.reshape(3, 3, C, C), grad_w_down.reshape(3, 3, C, C))

    img_spec = P(None, 'h', 'w', None)
    return jax.shard_map(block_step, mesh=mesh, in_specs=(img_spec, P(), P(), img_spec), out_specs=(img_spec, img_spec, P(), P()), check_vma=False)
```

time: 535 us -> 386 us (0.72); the launches traced: 529 us -> 385 us
  Pallas kernels: 0 us -> 305 us
  waiting for transfers between devices: 234 us -> 26.8 us
  matrix products: 146 us -> 0 us
  local copies, waits for them, and re-layouts: 72.7 us -> 9.34 us
  other arithmetic: 30.9 us -> 11.2 us
  between operations: 14.9 us -> 1.02 us
    pallas_call x0 -> x8, Pallas kernels: none -> 305 us  [the longest x1 195 us: reduce_all(): pl.pallas_call(reduce_kernel, out_shape=[shape, shape], in_specs=[ANY] *...]
    psum x1 -> x0, waiting for transfers between devices: 227 us -> none  [block_step(): lax.psum((grad_w_first, grad_w_down), ('w', 'h'))]
    conv_general_dilated x6 -> x0, matrix products: 146 us -> none  [the longest x2 76.9 us: weight_grad(): lax.conv_general_dilated(lhs_in, grad_in, (1, 1), padding, rhs_dilation=(...]
    unnamed x55 -> x8, local copies, waits for them, and re-layouts: 43.9 us -> 0.02 us
    ppermute x12 -> x16, waiting for transfers between devices: 6.27 us -> 26.8 us  [the longest x6 20.7 us: from_next(): lax.ppermute(edge, axis, [(i + 1, i) for i in range(axis_len[axis] - 1)])]
    concatenate x3 -> x6, other arithmetic: 28 us -> 8.87 us  [the longest x2 6.12 us: frame(): jnp.concatenate([from_prev(rows[:, -1:], 'w'), rows, from_next(rows[:, :1...]
    conv_general_dilated x9 -> x0, local copies, waits for them, and re-layouts: 6.68 us -> none  [the longest x6 3.73 us: conv_valid(): lax.conv_general_dilated(lhs_in, kernel, (stride, stride), 'VALID', dimen...]
    convert_element_type x13 -> x1, local copies, waits for them, and re-layouts: 7.44 us -> 1.17 us  [block_step(): g_f32, gp_f32 = (g_own.astype(F32), g_pair.astype(F32))]
  transfers between devices with their start and end apart: 13 -> 16, of which waited for: 3 -> 10; matrix products, arithmetic and copies ran while one was open for 28% -> 2% of each run, Pallas kernels for 0% -> 15%
where the time goes in v1:
time: 386 us; the launch traced here: 385 us
  Pallas kernels  305 us (79%)
  starting transfers between devices  32.1 us (8%)
  waiting for transfers between devices  26.8 us (7%)
  other arithmetic  11.2 us (3%)
  local copies, waits for them, and re-layouts  9.34 us (2%)
    pallas_call x1, Pallas kernels, reduce_all(): pl.pallas_call(reduce_kernel, out_shape=[shape, shape], in_specs=[ANY] *...  195 us
    pallas_call x1, Pallas kernels, weight_first(): pl.pallas_call(weight_first_kernel, out_shape=jax.ShapeDtypeStruct((10, H...  21.5 us
    ppermute x6, waiting for transfers between devices, from_next(): lax.ppermute(edge, axis, [(i + 1, i) for i in range(axis_len[axis] - 1)])  20.7 us
    pallas_call x1, Pallas kernels, settle(): pl.pallas_call(settle_kernel, out_shape=[shape, shape], in_specs=[ANY] *...  20.6 us
    ppermute x6, starting transfers between devices, from_prev(): lax.ppermute(edge, axis, [(i, i + 1) for i in range(axis_len[axis] - 1)])  19 us
    pallas_call x1, Pallas kernels, grad_image_call(): pl.pallas_call(grad_image_kernel, out_shape=jax.ShapeDtypeStruct((PIX, C)...  18.3 us
    pallas_call x1, Pallas kernels, conv_first(): pl.pallas_call(conv_first_kernel, grid=(3,), out_shape=[shape, shape], in...  18.2 us
    pallas_call x1, Pallas kernels, weight_down(): pl.pallas_call(weight_down_kernel, out_shape=jax.ShapeDtypeStruct((10, HA...  13 us
  transfers between devices with their start and end apart: 16, of which 10 were waited for; matrix products, arithmetic and copies ran while one was open for 2% of the time, Pallas kernels for 15%

profile of v1, /device:TPU:0, one launch (start us, length us, event | category | flops | bytes accessed | tf_op | source)
XLA Modules:
  0.0 385.3 jit_solution(15635565083860670802)
XLA Ops:
  0.6 0.9 slice_bitcast_fusion.3
  1.5 2.7 collective-permute-start
  4.2 1.3 collective-permute-start.1
  5.5 0.0 collective-permute-done
  5.5 3.9 %collective-permute-done.1 = bf16[1,48,640]{2,1,0:T(8,128)(2,1)S(1)} collective-permute-done((bf16[1,48,640]{2,1,0:T(8,128)(2,1)S(1)}, bf16[1,48,640]{2,1,0:T(8,128)(2,1)S(1)}, u32[]{:S(2)}, u32[]{:S(2)}) %collective-permute-start.1) | collective-permute-done | bytes 61472 | tf_op jit(solution)/shard_map/ppermute | solution.py:361
  9.4 1.2 pad_maximum_fusion.8
  10.6 3.4 collective-permute-start.2
  14.0 1.3 collective-permute-start.3
  15.3 0.6 collective-permute-done.2
  15.9 4.5 %collective-permute-done.3 = bf16[26,1,640]{2,1,0:T(2,128)(2,1)S(1)} collective-permute-done((bf16[26,1,640]{2,1,0:T(2,128)(2,1)S(1)}, bf16[26,1,640]{2,1,0:T(2,128)(2,1)S(1)}, u32[]{:S(2)}, u32[]{:S(2)}) %collective-permute-start.3) | collective-permute-done | bytes 33312 | tf_op jit(solution)/shard_map/ppermute | solution.py:361
  20.4 3.8 pad_maximum_fusion.ext_ref.x_ref
  24.2 18.2 %shard_map.75 = (f32[2,2,12,24,640]{4,3,2,1,0:T(8,128)}, f32[2,2,12,24,640]{4,3,2,1,0:T(8,128)}) custom-call(bf16[26,50,640]{2,1,0:T(8,128)(2,1)} %pad_maximum_fusion.ext_ref.x_ref, bf16[3,1920,640]{2,1,0:T(8,128)(2,1)} %bitcast.31), custom_call_target="tpu_custom_call" | custom-call | flops 8493465600 | bytes 16777216 | tf_op jit(solution)/shard_map/pallas_call | solution.py:81
  42.4 0.0 copy-start.2
  42.4 1.1 slice.57
  43.5 1.3 collective-permute-start.4
  44.8 2.7 collective-permute-done.4
  47.5 1.1 pad_maximum_fusion.5
  48.5 1.3 collective-permute-start.5
  49.8 5.3 %collective-permute-done.5 = f32[2,1,13,1,640]{4,3,2,1,0:T(1,128)S(1)} collective-permute-done((f32[2,1,13,1,640]{4,3,2,1,0:T(1,128)S(1)}, f32[2,1,13,1,640]{4,3,2,1,0:T(1,128)S(1)}, u32[]{:S(2)}, u32[]{:S(2)}) %collective-permute-start.5) | collective-permute-done | bytes 66592 | tf_op jit(solution)/shard_map/ppermute | solution.py:361
  55.1 0.0 copy-done.2
  55.1 0.5 select_maximum_fusion.z_ref
  55.6 0.0 copy-start
  55.6 0.0 copy-start.3
  55.6 2.6 copy.12
  58.3 0.0 copy-done
  58.3 2.6 collective-permute-start.12
  60.9 0.0 copy-done.3
  60.9 1.9 collective-permute-start.6
  62.9 3.6 collective-permute-done.6
  66.6 4.7 %collective-permute-start.7 = (bf16[13,1,640]{2,1,0:T(2,128)(2,1)S(1)}, bf16[13,1,640]{2,1,0:T(2,128)(2,1)S(1)}, u32[]{:S(2)}, u32[]{:S(2)}) collective-permute-start(bf16[13,1,640]{2,1,0:T(2,128)(2,1)S(1)} %pad_maximum_fusion.9), channel_id=1, source_target_pairs={{0,4},{4,8},{8,12},{1,5},{5,9},{9,13},{2,6},{6,10},{10,14},{3,7},{... | collective-permute-start | bytes 49928 | tf_op jit(solution)/shard_map/ppermute | solution.py:358
  71.3 1.4 collective-permute-done.7
  72.7 1.2 maximum_maximum_fusion
  73.8 0.0 collective-permute-start.14
  73.9 10.0 %shard_map.77.d_ref = bf16[1152,640]{1,0:T(8,128)(2,1)} custom-call(f32[13,25,640]{2,1,0:T(8,128)} %get-tuple-element.25.g_ref, f32[2,2,12,24,640]{4,3,2,1,0:T(8,128)} %get-tuple-element.11.a_ref, bf16[9,640,640]{2,1,0:T(8,128)(2,1)} %bitcast.20), custom_call_target="tpu_custom_call" | custom-call | flops 2123366400 | bytes 12582912 | tf_op jit(solution)/shard_map/pallas_call | solution.py:157
  83.9 0.0 copy-start.1
  83.9 0.5 collective-permute-start.15
  84.4 0.9 slice_bitcast_fusion.1
  85.2 2.0 collective-permute-start.8
  87.3 1.3 collective-permute-start.9
  88.6 0.0 collective-permute-done.8
  88.6 2.3 collective-permute-done.9
  90.8 1.2 pad_maximum_fusion.4
  92.0 4.2 %collective-permute-start.10 = (bf16[26,1,640]{2,1,0:T(2,128)(2,1)S(1)}, bf16[26,1,640]{2,1,0:T(2,128)(2,1)S(1)}, u32[]{:S(2)}, u32[]{:S(2)}) collective-permute-start(bf16[26,1,640]{2,1,0:T(2,128)(2,1)S(1)} %get-tuple-element.16), channel_id=1, source_target_pairs={{0,4},{4,8},{8,12},{1,5},{5,9},{9,13},{2,6},{6,10},{10,14},{3,7},{... | collective-permute-start | bytes 99848 | tf_op jit(solution)/shard_map/ppermute | solution.py:358
  96.3 1.3 collective-permute-start.11
  97.6 0.1 copy.13
  97.7 0.4 collective-permute-done.10
  98.1 2.2 collective-permute-start.13
  100.4 2.1 collective-permute-done.11
  102.4 0.0 copy-done.1
  102.4 2.3 pad_maximum_fusion.1.d_ref
  104.8 18.3 %shard_map.78 = bf16[1152,640]{1,0:T(8,128)(2,1)} custom-call(bf16[26,50,640]{2,1,0:T(8,128)(2,1)} %pad_maximum_fusion.1.d_ref, bf16[9,640,640]{2,1,0:T(8,128)(2,1)} %bitcast.32), custom_call_target="tpu_custom_call" | custom-call | flops 8493465600 | bytes 16777216 | tf_op jit(solution)/shard_map/pallas_call | solution.py:206
  123.1 8.2 %shard_map.76 = bf16[288,640]{1,0:T(8,128)(2,1)} custom-call(f32[2,2,13,25,640]{4,3,2,1,0:T(8,128)} %copy-done, bf16[9,640,640]{2,1,0:T(8,128)(2,1)} %bitcast.21), custom_call_target="tpu_custom_call" | custom-call | flops 2123366400 | bytes 12582912 | tf_op jit(solution)/shard_map/pallas_call | solution.py:127
  131.3 0.0 collective-permute-done.13
  131.3 1.2 copy.15.gp_ref
  132.5 0.0 collective-permute-done.15.dp_ref
  132.5 0.0 collective-permute-done.14.xp_ref
  132.5 21.5 %shard_map.80.p_first = f32[10,320,640]{2,1,0:T(8,128)} custom-call(bf16[26,50,640]{2,1,0:T(8,128)(2,1)} %pad_maximum_fusion.ext_ref.x_ref, bf16[26,50,640]{2,1,0:T(8,128)(2,1)} %collective-permute-done.14.xp_ref, bf16[1152,640]{1,0:T(8,128)(2,1)} %shard_map.77.d_ref, bf16[1152,640]{1,0:T(8,128)(2,1)} %collective-permute-done.15.dp_ref), custom_call_target="tpu_custom_call" | custom-call | flops 8493465600 | bytes 16777216 | tf_op jit(solution)/shard_map/pallas_call | solution.py:182
  154.0 0.0 collective-permute-done.12
  154.0 2.5 copy.14.zp_ref
  156.6 13.0 %shard_map.79.p_down = f32[10,320,640]{2,1,0:T(8,128)} custom-call(f32[2,2,13,25,640]{4,3,2,1,0:T(8,128)} %copy-done, f32[2,2,13,25,640]{4,3,2,1,0:T(8,128)} %copy.14.zp_ref, f32[13,25,640]{2,1,0:T(8,128)} %get-tuple-element.25.g_ref, f32[13,25,640]{2,1,0:T(8,128)} %copy.15.gp_ref), custom_call_target="tpu_custom_call" | custom-call | flops 2123366400 | bytes 16777216 | tf_op jit(solution)/shard_map/pallas_call | solution.py:109
  169.5 195.1 %shard_map.81 = (f32[18,320,640]{2,1,0:T(8,128)}, f32[18,320,640]{2,1,0:T(8,128)}) custom-call(f32[10,320,640]{2,1,0:T(8,128)} %shard_map.79.p_down, f32[10,320,640]{2,1,0:T(8,128)} %shard_map.80.p_first), custom_call_target="tpu_custom_call" | custom-call | flops 84934656000 | bytes 67108864 | tf_op jit(solution)/shard_map/pallas_call | solution.py:320
  364.6 20.6 %shard_map.82 = (f32[18,320,640]{2,1,0:T(8,128)}, f32[18,320,640]{2,1,0:T(8,128)}) custom-call(f32[18,320,640]{2,1,0:T(8,128)} %get-tuple-element.12.in_a, f32[18,320,640]{2,1,0:T(8,128)} %get-tuple-element.13.in_b), custom_call_target="tpu_custom_call" | custom-call | tf_op jit(solution)/shard_map/pallas_call | solution.py:347
  (3 shorter events, 0.1 us)
Async XLA Ops:
  1.5 4.0 %collective-permute-start = (bf16[1,48,640]{2,1,0:T(8,128)(2,1)S(1)}, bf16[1,48,640]{2,1,0:T(8,128)(2,1)S(1)}, u32[]{:S(2)}, u32[]{:S(2)}) collective-permute-start(bf16[1,48,640]{2,1,0:T(8,128)(2,1)S(1)} %get-tuple-element.22), channel_id=1, source_target_pairs={{0,1},{1,2},{2,3},{4,5},{5,6},{6,7},{8,9},{9,10},{10,11},{12,13},{... | collective-permute-start | bytes 184328 | tf_op jit(solution)/shard_map/ppermute | solution.py:358
  4.2 5.2 %collective-permute-start.1 = (bf16[1,48,640]{2,1,0:T(8,128)(2,1)S(1)}, bf16[1,48,640]{2,1,0:T(8,128)(2,1)S(1)}, u32[]{:S(2)}, u32[]{:S(2)}) collective-permute-start(bf16[1,48,640]{2,1,0:T(8,128)(2,1)S(1)} %get-tuple-element.23), channel_id=1, source_target_pairs={{1,0},{2,1},{3,2},{5,4},{6,5},{7,6},{9,8},{10,9},{11,10},{13,12},{... | collective-permute-start | bytes 184328 | tf_op jit(solution)/shard_map/ppermute | solution.py:361
  10.6 5.3 %collective-permute-start.2 = (bf16[26,1,640]{2,1,0:T(2,128)(2,1)S(1)}, bf16[26,1,640]{2,1,0:T(2,128)(2,1)S(1)}, u32[]{:S(2)}, u32[]{:S(2)}) collective-permute-start(bf16[26,1,640]{2,1,0:T(2,128)(2,1)S(1)} %get-tuple-element.18), channel_id=1, source_target_pairs={{0,4},{4,8},{8,12},{1,5},{5,9},{9,13},{2,6},{6,10},{10,14},{3,7},{... | collective-permute-start | bytes 99848 | tf_op jit(solution)/shard_map/ppermute | solution.py:358
  14.0 6.4 %collective-permute-start.3 = (bf16[26,1,640]{2,1,0:T(2,128)(2,1)S(1)}, bf16[26,1,640]{2,1,0:T(2,128)(2,1)S(1)}, u32[]{:S(2)}, u32[]{:S(2)}) collective-permute-start(bf16[26,1,640]{2,1,0:T(2,128)(2,1)S(1)} %get-tuple-element.19), channel_id=1, source_target_pairs={{4,0},{8,4},{12,8},{5,1},{9,5},{13,9},{6,2},{10,6},{14,10},{7,3},{... | collective-permute-start | bytes 99848 | tf_op jit(solution)/shard_map/ppermute | solution.py:361
  42.4 12.7 %copy-start.2 = (f32[2,2,12,24,640]{4,3,2,1,0:T(8,128)S(1)}, f32[2,2,12,24,640]{4,3,2,1,0:T(8,128)}, u32[]{:S(2)}) copy-start(f32[2,2,12,24,640]{4,3,2,1,0:T(8,128)} %get-tuple-element.10) | copy-start | bytes 8847364
  43.5 4.0 %collective-permute-start.4 = (f32[1,2,1,24,640]{4,3,2,1,0:T(8,128)S(1)}, f32[1,2,1,24,640]{4,3,2,1,0:T(8,128)S(1)}, u32[]{:S(2)}, u32[]{:S(2)}) collective-permute-start(f32[1,2,1,24,640]{4,3,2,1,0:T(8,128)S(1)} %slice.57), channel_id=1, source_target_pairs={{1,0},{2,1},{3,2},{5,4},{6,5},{7,6},{9,8},{10,9},{11,10},{13,12},{... | collective-permute-start | bytes 368648 | tf_op jit(solution)/shard_map/ppermute | solution.py:361
  48.5 6.6 %collective-permute-start.5 = (f32[2,1,13,1,640]{4,3,2,1,0:T(1,128)S(1)}, f32[2,1,13,1,640]{4,3,2,1,0:T(1,128)S(1)}, u32[]{:S(2)}, u32[]{:S(2)}) collective-permute-start(f32[2,1,13,1,640]{4,3,2,1,0:T(1,128)S(1)} %pad_maximum_fusion.5), channel_id=1, source_target_pairs={{4,0},{8,4},{12,8},{5,1},{9,5},{13,9},{6,2},{10,6},{14,10},{7,3},{... | collective-permute-start | bytes 199688 | tf_op jit(solution)/shard_map/ppermute | solution.py:361
  55.6 2.7 copy-start
  55.6 5.3 %copy-start.3 = (bf16[1,12,24,640]{3,2,1,0:T(8,128)(2,1)S(1)}, bf16[1,12,24,640]{3,2,1,0:T(8,128)(2,1)}, u32[]{:S(2)}) copy-start(bf16[1,12,24,640]{3,2,1,0:T(8,128)(2,1)} %param.7) | copy-start | bytes 1105924
  58.3 95.7 %collective-permute-start.12 = (f32[2,2,13,25,640]{4,1,3,2,0:T(2,128)S(1)}, f32[2,2,13,25,640]{4,1,3,2,0:T(2,128)S(1)}, u32[]{:S(2)}, u32[]{:S(2)}) collective-permute-start(f32[2,2,13,25,640]{4,1,3,2,0:T(2,128)S(1)} %copy.12), channel_id=1, source_target_pairs={{0,1},{1,0},{2,3},{3,2},{4,5},{5,4},{6,7},{7,6},{8,9},{9,8},{10,11... | collective-permute-start | bytes 9984008 | tf_op jit(solution)/shard_map/ppermute | solution.py:364
  60.9 5.6 %collective-permute-start.6 = (bf16[1,24,640]{2,1,0:T(8,128)(2,1)S(1)}, bf16[1,24,640]{2,1,0:T(8,128)(2,1)S(1)}, u32[]{:S(2)}, u32[]{:S(2)}) collective-permute-start(bf16[1,24,640]{2,1,0:T(8,128)(2,1)S(1)} %slice_bitcast_fusion.4), channel_id=1, source_target_pairs={{0,1},{1,2},{2,3},{4,5},{5,6},{6,7},{8,9},{9,10},{10,11},{12,13},{... | collective-permute-start | bytes 92168 | tf_op jit(solution)/shard_map/ppermute | solution.py:358
  66.6 6.1 %collective-permute-start.7 = (bf16[13,1,640]{2,1,0:T(2,128)(2,1)S(1)}, bf16[13,1,640]{2,1,0:T(2,128)(2,1)S(1)}, u32[]{:S(2)}, u32[]{:S(2)}) collective-permute-start(bf16[13,1,640]{2,1,0:T(2,128)(2,1)S(1)} %pad_maximum_fusion.9), channel_id=1, source_target_pairs={{0,4},{4,8},{8,12},{1,5},{5,9},{9,13},{2,6},{6,10},{10,14},{3,7},{... | collective-permute-start | bytes 49928 | tf_op jit(solution)/shard_map/ppermute | solution.py:358
  73.8 58.6 %collective-permute-start.14 = (bf16[26,50,640]{2,1,0:T(8,128)(2,1)}, bf16[26,50,640]{2,1,0:T(8,128)(2,1)}, u32[]{:S(2)}, u32[]{:S(2)}) collective-permute-start(bf16[26,50,640]{2,1,0:T(8,128)(2,1)} %pad_maximum_fusion.ext_ref.x_ref), channel_id=1, source_target_pairs={{0,1},{1,0},{2,3},{3,2},{4,5},{5,4},{6,7},{7,6},{8,9},{9,8},{10,11... | collective-permute-start | bytes 4992008 | tf_op jit(solution)/shard_map/ppermute | solution.py:364
  83.9 18.6 %copy-start.1 = (bf16[1152,640]{1,0:T(8,128)(2,1)S(1)}, bf16[1152,640]{1,0:T(8,128)(2,1)}, u32[]{:S(2)}) copy-start(bf16[1152,640]{1,0:T(8,128)(2,1)} %shard_map.77.d_ref) | copy-start | bytes 4423684
  83.9 48.6 %collective-permute-start.15 = (bf16[1152,640]{1,0:T(8,128)(2,1)}, bf16[1152,640]{1,0:T(8,128)(2,1)}, u32[]{:S(2)}, u32[]{:S(2)}) collective-permute-start(bf16[1152,640]{1,0:T(8,128)(2,1)} %shard_map.77.d_ref), channel_id=1, source_target_pairs={{0,1},{1,0},{2,3},{3,2},{4,5},{5,4},{6,7},{7,6},{8,9},{9,8},{10,11... | collective-permute-start | bytes 4423688 | tf_op jit(solution)/shard_map/ppermute | solution.py:364
  85.2 3.3 collective-permute-start.8
  87.3 3.6 collective-permute-start.9
  92.0 6.1 %collective-permute-start.10 = (bf16[26,1,640]{2,1,0:T(2,128)(2,1)S(1)}, bf16[26,1,640]{2,1,0:T(2,128)(2,1)S(1)}, u32[]{:S(2)}, u32[]{:S(2)}) collective-permute-start(bf16[26,1,640]{2,1,0:T(2,128)(2,1)S(1)} %get-tuple-element.16), channel_id=1, source_target_pairs={{0,4},{4,8},{8,12},{1,5},{5,9},{9,13},{2,6},{6,10},{10,14},{3,7},{... | collective-permute-start | bytes 99848 | tf_op jit(solution)/shard_map/ppermute | solution.py:358
  96.3 6.2 %collective-permute-start.11 = (bf16[26,1,640]{2,1,0:T(2,128)(2,1)S(1)}, bf16[26,1,640]{2,1,0:T(2,128)(2,1)S(1)}, u32[]{:S(2)}, u32[]{:S(2)}) collective-permute-start(bf16[26,1,640]{2,1,0:T(2,128)(2,1)S(1)} %get-tuple-element.17), channel_id=1, source_target_pairs={{4,0},{8,4},{12,8},{5,1},{9,5},{13,9},{6,2},{10,6},{14,10},{7,3},{... | collective-permute-start | bytes 99848 | tf_op jit(solution)/shard_map/ppermute | solution.py:361
  98.1 33.1 %collective-permute-start.13 = (bf16[13,25,640]{2,0,1:T(8,128)(2,1)S(1)}, bf16[13,25,640]{2,0,1:T(8,128)(2,1)S(1)}, u32[]{:S(2)}, u32[]{:S(2)}) collective-permute-start(bf16[13,25,640]{2,0,1:T(8,128)(2,1)S(1)} %copy.13), channel_id=1, source_target_pairs={{0,1},{1,0},{2,3},{3,2},{4,5},{5,4},{6,7},{7,6},{8,9},{9,8},{10,11... | collective-permute-start | bytes 1248008 | tf_op jit(solution)/shard_map/ppermute | solution.py:364

commit v2 on v1

--- a/solution.py
+++ b/solution.py
@@ -88,14 +88,16 @@
     )(image_ext, w_first.reshape(3, 3 * C, C))
 
 
-def weight_down_kernel(z_ref, zp_ref, g_ref, gp_ref, out_ref, taps, gs):
+def weight_down_kernel(z_ref, zp_ref, g_ref, gp_ref, out_ref, tap_ref, taps, gs):
     core = lax.axis_index('h') % 2
     for src, (zr, gr) in enumerate(((z_ref, g_ref), (zp_ref, gp_ref))):
         gs[src * OPIX:(src + 1) * OPIX, :] = gr[1:, 1:, :].reshape(OPIX, C).astype(BF16)
         for t in range(9):
             a, c = t // 3, t % 3
-            tap = zr[a % 2, c % 2, a // 2:a // 2 + OUT_R, c // 2:c // 2 + OUT_C, :]
-            taps[t, src * OPIX:(src + 1) * OPIX, :] = tap.reshape(OPIX, C).astype(BF16)
+            tap = zr[a % 2, c % 2, a // 2:a // 2 + OUT_R, c // 2:c // 2 + OUT_C, :].reshape(OPIX, C).astype(BF16)
+            taps[t, src * OPIX:(src + 1) * OPIX, :] = tap
+            if src == 0:
+                tap_ref[t] = tap
 
     def one(j, _):
         res = dot_lhs_t(taps[4 * core + j], gs[...])
@@ -107,108 +109,11 @@
 
 def weight_down(z_own, z_pair, g_own, g_pair):
     return pl.pallas_call(
-        weight_down_kernel, out_shape=jax.ShapeDtypeStruct((10, HALF, C), F32), in_specs=[VM] * 4, out_specs=VM,
+        weight_down_kernel, out_shape=[jax.ShapeDtypeStruct((10, HALF, C), F32), jax.ShapeDtypeStruct((9, OPIX, C), BF16)], in_specs=[VM] * 4, out_specs=[VM] * 2,
         scratch_shapes=[pltpu.VMEM((9, 2 * OPIX, C), BF16), pltpu.VMEM((2 * OPIX, C), BF16)],
         compiler_params=pltpu.CompilerParams(vmem_limit_bytes=56 * MIB),
         cost_estimate=pl.CostEstimate(flops=2 * OPIX * 9 * C * C, bytes_accessed=16 * MIB, transcendentals=0),
     )(z_own, z_pair, g_own, g_pair)
-
-
-def conv_down_kernel(z_ref, w_ref, y_ref, acc):
-    for t in range(9):
-        a, c = t // 3, t % 3
-        tap = z_ref[a % 2, c % 2, a // 2:a // 2 + OUT_R, c // 2:c // 2 + OUT_C, :].reshape(OPIX, C).astype(BF16)
-        part = dot(tap, w_ref[t])
-        acc[...] = part if t == 0 else acc[...] + part
-    y_ref[...] = acc[...].astype(BF16)
-
-
-def conv_down(z_own, w_down):
-    return pl.pallas_call(
-        conv_down_kernel, out_shape=jax.ShapeDtypeStruct((OPIX, C), BF16), in_specs=[VM] * 2, out_specs=VM,
-        scratch_shapes=[pltpu.VMEM((OPIX, C), F32)],
-        compiler_params=pltpu.CompilerParams(vmem_limit_bytes=56 * MIB),
-        cost_estimate=pl.CostEstimate(flops=2 * OPIX * 9 * C * C, bytes_accessed=12 * MIB, transcendentals=0),
-    )(z_own, w_down)
-
-
-def grad_pre_kernel(g_ref, a_ref, w_ref, out_ref, gs, sd):
-    for di in range(2):
-        for dj in range(2):
-            gs[di, dj] = g_ref[di:di + OUT_R, dj:dj + OUT_C, :].reshape(OPIX, C).astype(BF16)
-    for rp in range(2):
-        for cp in range(2):
-            acc = None
-            for a in ((0, 2), (1,))[rp]:
-                for c in ((0, 2), (1,))[cp]:
-                    part = dot_rhs_t(gs[1 - a // 2, 1 - c // 2], w_ref[3 * a + c])
-                    acc = part if acc is None else acc + part
-            pre = a_ref[rp, cp].reshape(OPIX, C)
-            grad = jax.vjp(gelu_tanh, pre)[1](acc)[0].astype(BF16).astype(F32)
-            for i in range(OUT_R):
-                for lane in range(5):
-                    rows = pl.ds((2 * i + rp) * COLS + cp, OUT_C, stride=2)
-                    sd[lane, rows, :] = grad[i * OUT_C:(i + 1) * OUT_C, lane * 128:(lane + 1) * 128]
-    for lane in range(5):
-        out_ref[:, lane * 128:(lane + 1) * 128] = sd[lane].astype(BF16)
-
-
-def grad_pre_call(g_ext, a_own, w_down):
-    return pl.pallas_call(
-        grad_pre_kernel, out_shape=jax.ShapeDtypeStruct((PIX, C), BF16), in_specs=[VM] * 3, out_specs=VM,
-        scratch_shapes=[pltpu.VMEM((2, 2, OPIX, C), BF16), pltpu.VMEM((5, PIX, 128), F32)],
-        compiler_params=pltpu.CompilerParams(vmem_limit_bytes=56 * MIB),
-        cost_estimate=pl.CostEstimate(flops=2 * OPIX * 9 * C * C, bytes_accessed=12 * MIB, transcendentals=PIX * C),
-    )(g_ext, a_own, w_down)
-
-
-def weight_first_kernel(x_ref, xp_ref, d_ref, dp_ref, out_ref, xs):
-    core = lax.axis_index('h') % 2
-    for src, ref in enumerate((x_ref, xp_ref)):
-        shift_columns(ref, xs.at[src])
-
-    def one(j, _):
-        t = 4 * core + j
-        a, c = t // 3, t % 3
-        rows = pl.ds(pl.multiple_of(a * COLS, COLS), PIX)
-        res = dot_lhs_t(xs[0, c, rows, :], d_ref[...]) + dot_lhs_t(xs[1, c, rows, :], dp_ref[...])
-        out_ref[2 * j] = res[:HALF]
-        out_ref[2 * j + 1] = res[HALF:]
-        return 0
-    lax.fori_loop(0, 5, one, 0)
-
-
-def weight_first(x_own, x_pair, d_own, d_pair):
-    return pl.pallas_call(
-        weight_first_kernel, out_shape=jax.ShapeDtypeStruct((10, HALF, C), F32), in_specs=[VM] * 4, out_specs=VM,
-        scratch_shapes=[pltpu.VMEM((2, 3, (ROWS + 2) * COLS, C), BF16)],
-        compiler_params=pltpu.CompilerParams(vmem_limit_bytes=56 * MIB),
-        cost_estimate=pl.CostEstimate(flops=2 * PIX * 9 * C * C, bytes_accessed=16 * MIB, transcendentals=0),
-    )(x_own, x_pair, d_own, d_pair)
-
-
-def grad_image_kernel(d_ref, w_ref, out_ref, ds, acc):
-    shift_columns(d_ref, ds)
-    block = 8 * COLS
-
-    def one(i, _):
-        for t in range(9):
-            a, c = t // 3, t % 3
-            rows = pl.ds(pl.multiple_of(i * block + (2 - a) * COLS, COLS), block)
-            part = dot_rhs_t(ds[2 - c, rows, :], w_ref[t])
-            acc[...] = part if t == 0 else acc[...] + part
-        out_ref[pl.ds(pl.multiple_of(i * block, block), block), :] = acc[...].astype(BF16)
-        return 0
-    lax.fori_loop(0, 3, one, 0)
-
-
-def grad_image_call(d_ext, w_first):
-    return pl.pallas_call(
-        grad_image_kernel, out_shape=jax.ShapeDtypeStruct((PIX, C), BF16), in_specs=[VM] * 2, out_specs=VM,
-        scratch_shapes=[pltpu.VMEM((3, (ROWS + 2) * COLS, C), BF16), pltpu.VMEM((8 * COLS, C), F32)],
-        compiler_params=pltpu.CompilerParams(vmem_limit_bytes=56 * MIB),
-        cost_estimate=pl.CostEstimate(flops=2 * PIX * 9 * C * C, bytes_accessed=16 * MIB, transcendentals=0),
-    )(d_ext, w_first)
 
 
 def place():
@@ -286,44 +191,197 @@
             self.move(kind, ())
 
 
-def reduce_kernel(p_down, p_first, o_down, o_first, own_d, own_f, land_d, land_f, local_sems, send_sems, recv_sems, grants):
+NEAR = [(dw, dh) for dw in (-1, 0, 1) for dh in (-1, 0, 1) if (dw, dh) != (0, 0)]
+EDGE = 8
+
+
+def lane(k):
+    return pl.ds(k * 128, 128)
+
+
+def back_kernel(p_down, taps_in, g_in, a_in, w_down, w_first, x_in, xp_in, y_out, dx_out, o_down, o_first,
+                own_d, own_f, land_d, land_f, wbuf, xs, ext, taps, g_ext, da, da_pair, grid, acc,
+                row_send, col_send, cor_send, row_land, col_land, cor_land,
+                load_sems, pair_sems, near_sems, out_sems, send_sems, recv_sems, grants):
     bit, dev = place()
-    loads = [pltpu.make_async_copy(p, o, local_sems.at[i]) for i, (p, o) in enumerate(((p_down, own_d), (p_first, own_f)))]
-    for load in loads:
-        load.start()
+    w, h = lax.axis_index('w'), lax.axis_index('h')
+    core = bit['c']
+    flat_a = own_f.at[pl.ds(0, 4), pl.ds(0, OPIX)]
+    loads = {}
+    for i, (name, src, dst) in enumerate((('p', p_down, own_d), ('w', w_down, wbuf), ('g', g_in, g_ext), ('a', a_in, flat_a),
+                                          ('x', x_in, ext), ('t', taps_in, taps))):
+        loads[name] = pltpu.make_async_copy(src, dst, load_sems.at[i])
+        loads[name].start()
     barrier = pltpu.get_barrier_semaphore()
     for axis in 'xyzc':
         pl.semaphore_signal(barrier, inc=1, device_id=dev[axis], device_id_type=MESH)
-    pl.semaphore_wait(barrier, 4)
+    for dw, dh in NEAR:
+        pl.semaphore_signal(barrier, inc=1, device_id=((w + dw + 4) % 4, (h + dh + 4) % 4), device_id_type=MESH)
+    pl.semaphore_wait(barrier, 12)
     sems = (send_sems, recv_sems)
-    both = [Reducer(0, own_d, land_d, o_down, sems, grants, bit, dev), Reducer(1, own_f, land_f, o_first, sems, grants, bit, dev)]
-    for load, one in zip(loads, both):
-        load.wait()
-        one.begin()
-    for kind in (R1, R2, R3):
-        for one in both:
-            one.move(kind, (kind + 1,), add=True)
-    for one in both:
-        one.move(A1, (A2, A3A))
-    for one in both:
-        one.move(A2, (A3B, DA, LA))
-    for one in both:
-        one.move(A3A, (DB, LB))
-    for one in both:
-        one.move(A3B, (DC, LC))
+    down = Reducer(0, own_d, land_d, o_down, sems, grants, bit, dev)
+    first = Reducer(1, own_f, land_f, o_first, sems, grants, bit, dev)
+    both = (down, first)
+    loads['p'].wait()
+    down.begin()
+
+    loads['g'].wait()
+    for di in range(2):
+        for dj in range(2):
+            at = (2 * di + dj) * OPIX
+            xs[1, 0, at:at + OPIX, :] = g_ext[di:di + OUT_R, dj:dj + OUT_C, :].reshape(OPIX, C).astype(BF16)
+    loads['a'].wait()
+    loads['w'].wait()
+    for rp in range(2):
+        for cp in range(2):
+            total = None
+            for a in ((0, 2), (1,))[rp]:
+                for c in ((0, 2), (1,))[cp]:
+                    at = (2 * (1 - a // 2) + 1 - c // 2) * OPIX
+                    part = dot_rhs_t(xs[1, 0, at:at + OPIX, :], wbuf[3 * a + c])
+                    total = part if total is None else total + part
+            pre = own_f[2 * rp + cp, 0:OPIX, :]
+            grad = jax.vjp(gelu_tanh, pre)[1](total)[0].astype(BF16).astype(F32)
+            for i in range(OUT_R):
+                for k in range(5):
+                    grid[k, 2 * i + rp + 1, pl.ds(EDGE + cp, OUT_C, stride=2), :] = grad[i * OUT_C:(i + 1) * OUT_C, k * 128:(k + 1) * 128]
+
+    def pack(r, _):
+        for k in range(5):
+            da[pl.ds(pl.multiple_of(r * COLS, COLS), COLS), lane(k)] = grid[k, r + 1, EDGE:EDGE + COLS, :].astype(BF16)
+        return 0
+    lax.fori_loop(0, ROWS, pack, 0)
+    share = pltpu.make_async_remote_copy(src_ref=da, dst_ref=da_pair, send_sem=pair_sems.at[0], recv_sem=pair_sems.at[1], device_id=dev['c'], device_id_type=MESH)
+    share.start()
+
+    last_r, last_c = ROWS, EDGE + COLS - 1
+    for k in range(5):
+        for side, r in enumerate((1, last_r)):
+            row_send[side, :, lane(k)] = grid[k, r, EDGE:EDGE + COLS, :]
+        for side, c in enumerate((EDGE, last_c)):
+            for r in range(ROWS):
+                col_send[side, r:r + 1, lane(k)] = grid[k, r + 1, c:c + 1, :]
+            for vert, r in enumerate((1, last_r)):
+                cor_send[2 * vert + side, :, lane(k)] = jnp.broadcast_to(grid[k, r, c:c + 1, :], (8, 128))
+    borders = []
+    for i, (dw, dh) in enumerate(NEAR):
+        if dw == 0:
+            src, dst = row_send.at[(dh + 1) // 2], row_land.at[(1 - dh) // 2]
+        elif dh == 0:
+            src, dst = col_send.at[(dw + 1) // 2], col_land.at[(1 - dw) // 2]
+        else:
+            src = cor_send.at[2 * ((dh + 1) // 2) + (dw + 1) // 2]
+            dst = cor_land.at[2 * ((1 - dh) // 2) + (1 - dw) // 2]
+        peer = ((w + dw + 4) % 4, (h + dh + 4) % 4)
+        copy = pltpu.make_async_remote_copy(src_ref=src, dst_ref=dst, send_sem=near_sems.at[0, i], recv_sem=near_sems.at[1, i], device_id=peer, device_id_type=MESH)
+        copy.start()
+        borders.append(copy)
+
+    loads['x'].wait()
+    shift_columns(ext, xs.at[0])
+    pair_load = pltpu.make_async_copy(xp_in, ext, load_sems.at[6])
+    pair_load.start()
+
+    loads['t'].wait()
+    for t in range(9):
+        part = dot(taps[t], wbuf[t])
+        acc[0:OPIX, :] = part if t == 0 else acc[0:OPIX, :] + part
+    y_stage = taps.at[0]
+    y_stage[...] = acc[0:OPIX, :].astype(BF16)
+    y_copy = pltpu.make_async_copy(y_stage, y_out, out_sems.at[0])
+    y_copy.start()
+    w_copy = pltpu.make_async_copy(w_first, wbuf, load_sems.at[7])
+    w_copy.start()
+
+    pair_load.wait()
+    shift_columns(ext, xs.at[1])
+    share.wait()
+
+    def first_tap(j, _):
+        t = 4 * core + j
+        a, c = t // 3, t % 3
+        rows = pl.ds(pl.multiple_of(a * COLS, COLS), PIX)
+        res = dot_lhs_t(xs[0, c, rows, :], da[...]) + dot_lhs_t(xs[1, c, rows, :], da_pair[...])
+        own_f[2 * j] = res[:HALF]
+        own_f[2 * j + 1] = res[HALF:]
+        return 0
+    lax.fori_loop(0, 4, first_tap, 0)
+    down.move(R1, (R2,), add=True)
+    first_tap(4, 0)
+    first.begin()
+
+    for copy in borders:
+        copy.wait()
+    for side, edge in enumerate((h == 0, h == 3)):
+        for k in range(5):
+            grid[k, side * (ROWS + 1), EDGE:EDGE + COLS, :] = jnp.where(edge, 0.0, row_land[side, :, lane(k)])
+    for side, edge in enumerate((w == 0, w == 3)):
+        c = (EDGE - 1, EDGE + COLS)[side]
+        for k in range(5):
+            for r in range(ROWS):
+                grid[k, r + 1, c:c + 1, :] = jnp.where(edge, 0.0, col_land[side, r:r + 1, lane(k)])
+            for vert, far in enumerate((h == 0, h == 3)):
+                grid[k, vert * (ROWS + 1), c:c + 1, :] = jnp.where(jnp.logical_or(edge, far), 0.0, cor_land[2 * vert + side, 0:1, lane(k)])
+
+    def spread(r, _):
+        for c in range(3):
+            for k in range(5):
+                xs[0, c, pl.ds(pl.multiple_of(r * COLS, COLS), COLS), lane(k)] = grid[k, r, EDGE - 1 + c:EDGE - 1 + c + COLS, :].astype(BF16)
+        return 0
+    lax.fori_loop(0, ROWS + 2, spread, 0)
+    w_copy.wait()
+    block = 8 * COLS
+
+    def image_rows(i, _):
+        for t in range(9):
+            a, c = t // 3, t % 3
+            rows = pl.ds(pl.multiple_of(i * block + (2 - a) * COLS, COLS), block)
+            part = dot_rhs_t(xs[0, 2 - c, rows, :], wbuf[t])
+            acc[...] = part if t == 0 else acc[...] + part
+        da_pair[pl.ds(pl.multiple_of(i * block, block), block), :] = acc[...].astype(BF16)
+        return 0
+    lax.fori_loop(0, 3, image_rows, 0)
+    dx_copy = pltpu.make_async_copy(da_pair, dx_out, out_sems.at[1])
+    dx_copy.start()
+
+    down.move(R2, (R3,), add=True)
+    first.move(R1, (R2,), add=True)
+    down.move(R3, (A1,), add=True)
+    first.move(R2, (R3,), add=True)
+    down.move(A1, (A2, A3A))
+    first.move(R3, (A1,), add=True)
+    down.move(A2, (A3B, DA, LA))
+    first.move(A1, (A2, A3A))
+    down.move(A3A, (DB, LB))
+    first.move(A2, (A3B, DA, LA))
+    down.move(A3B, (DC, LC))
+    first.move(A3A, (DB, LB))
+    first.move(A3B, (DC, LC))
+    y_copy.wait()
+    dx_copy.wait()
     for one in both:
         one.finish()
 
 
-def reduce_all(p_down, p_first):
-    shape = jax.ShapeDtypeStruct((18, HALF, C), F32)
+def back_call(p_down, taps, g_ext, a_own, w_down, w_first, x_own, x_pair):
+    total = jax.ShapeDtypeStruct((18, HALF, C), F32)
+    line = ((ROWS + 2) * COLS, C)
+    dma = pltpu.SemaphoreType.DMA
     return pl.pallas_call(
-        reduce_kernel, out_shape=[shape, shape], in_specs=[ANY] * 2, out_specs=[ANY] * 2,
+        back_kernel,
+        out_shape=[jax.ShapeDtypeStruct((OPIX, C), BF16), jax.ShapeDtypeStruct((PIX, C), BF16), total, total],
+        in_specs=[ANY] * 8, out_specs=[ANY] * 4,
         scratch_shapes=[pltpu.VMEM((10, HALF, C), F32)] * 2 + [pltpu.VMEM((9, 280, C), F32)] * 2
-        + [pltpu.SemaphoreType.DMA((2,)), pltpu.SemaphoreType.DMA((2, 3, 13)), pltpu.SemaphoreType.DMA((2, 3, 13)), pltpu.SemaphoreType.REGULAR((2, 3, 3))],
-        compiler_params=pltpu.CompilerParams(collective_id=1, has_side_effects=True, vmem_limit_bytes=56 * MIB),
+        + [pltpu.VMEM((9, C, C), BF16), pltpu.VMEM((2, 3) + line, BF16)]
+        + [pltpu.VMEM((ROWS + 2, COLS + 2, C), BF16)]
+        + [pltpu.VMEM((9, OPIX, C), BF16), pltpu.VMEM((OUT_R + 1, OUT_C + 1, C), F32)]
+        + [pltpu.VMEM((PIX, C), BF16)] * 2
+        + [pltpu.VMEM((5, ROWS + 2, COLS + 2 * EDGE, 128), F32), pltpu.VMEM((8 * COLS, C), F32)]
+        + [pltpu.VMEM((2, COLS, C), F32), pltpu.VMEM((2, ROWS, C), F32), pltpu.VMEM((4, 8, C), F32)] * 2
+        + [dma((8,)), dma((2,)), dma((2, 8)), dma((2,)), dma((2, 3, 13)), dma((2, 3, 13)), pltpu.SemaphoreType.REGULAR((2, 3, 3))],
+        compiler_params=pltpu.CompilerParams(collective_id=1, has_side_effects=True, vmem_limit_bytes=67043328),
         cost_estimate=pl.CostEstimate(flops=2 * PIX * 90 * C * C, bytes_accessed=64 * MIB, transcendentals=0),
-    )(p_down, p_first)
+    )(p_down, taps, g_ext, a_own, w_down, w_first, x_own, x_pair)
 
 
 def settle_kernel(in_a, in_b, out_a, out_b, buf, load_sems, store_sems):
@@ -378,14 +436,10 @@
         z_own = jnp.concatenate([z_rows, jnp.pad(from_next(z_rows[:, :1, :, :1], 'w'), ((0, 0), (0, 1)) + ((0, 0),) * 3)], 3)
         z_pair = swap_core(z_own)
         g_f32, gp_f32 = g_own.astype(F32), g_pair.astype(F32)
-        p_down = weight_down(z_own, z_pair, g_f32, gp_f32)
-        w_taps = w_down.reshape(9, C, C)
-        grad_pre = grad_pre_call(g_f32, a_own, w_taps)
-        d_pair = swap_core(grad_pre)
-        p_first = weight_first(x_own, x_pair, grad_pre, d_pair)
-        block_out = conv_down(z_own, w_taps)
-        grad_image = grad_image_call(frame(grad_pre.reshape(ROWS, COLS, C)), w_first.reshape(9, C, C))
-        grad_w_down, grad_w_first = settle(*reduce_all(p_down, p_first))
+        p_down, taps = weight_down(z_own, z_pair, g_f32, gp_f32)
+        block_out, grad_image, sum_down, sum_first = back_call(
+            p_down, taps, g_f32, a_own.reshape(4, OPIX, C), w_down.reshape(9, C, C), w_first.reshape(9, C, C), x_own, x_pair)
+        grad_w_down, grad_w_first = settle(sum_down, sum_first)
         return (block_out.reshape(1, OUT_R, OUT_C, C), grad_image.reshape(1, ROWS, COLS, C),
                 grad_w_first.reshape(3, 3, C, C), grad_w_down.reshape(3, 3, C, C))
 

time: 386 us -> 320 us (0.83)
  Pallas kernels: 305 us -> 252 us
  starting transfers between devices: 32.1 us -> 20.9 us
    pallas_call x6 -> x2, Pallas kernels: 266 us -> 213 us  [the longest x1 200 us: back_call(): pl.pallas_call(back_kernel, out_shape=[jax.ShapeDtypeStruct((OPIX, C), BF...]
    ppermute x6 -> x4, starting transfers between devices: 19 us -> 12.9 us  [from_prev(): lax.ppermute(edge, axis, [(i, i + 1) for i in range(axis_len[axis] - 1)])]
    ppermute x6 -> x4, waiting for transfers between devices: 20.7 us -> 16.4 us  [from_next(): lax.ppermute(edge, axis, [(i + 1, i) for i in range(axis_len[axis] - 1)])]
    ppermute x6 -> x4, starting transfers between devices: 7.75 us -> 5.16 us  [from_next(): lax.ppermute(edge, axis, [(i + 1, i) for i in range(axis_len[axis] - 1)])]
    ppermute x6 -> x4, waiting for transfers between devices: 6.08 us -> 8.01 us  [from_prev(): lax.ppermute(edge, axis, [(i, i + 1) for i in range(axis_len[axis] - 1)])]
  transfers between devices with their start and end apart: 16 -> 11, of which waited for: 10 -> 8; matrix products, arithmetic and copies ran while one was open for 2% -> 2% of each run, Pallas kernels for 15% -> 4%
where the time goes in v2:
time: 320 us; the launch traced here: 319 us
  Pallas kernels  252 us (79%)
  waiting for transfers between devices  26.3 us (8%)
  starting transfers between devices  20.9 us (7%)
  local copies, waits for them, and re-layouts  11.5 us (4%)
  other arithmetic  7.7 us (2%)
    pallas_call x1, Pallas kernels, back_call(): pl.pallas_call(back_kernel, out_shape=[jax.ShapeDtypeStruct((OPIX, C), BF...  200 us
    pallas_call x1, Pallas kernels, settle(): pl.pallas_call(settle_kernel, out_shape=[shape, shape], in_specs=[ANY] *...  20.7 us
    pallas_call x1, Pallas kernels, conv_first(): pl.pallas_call(conv_first_kernel, grid=(3,), out_shape=[shape, shape], in...  18.2 us
    ppermute x4, waiting for transfers between devices, from_next(): lax.ppermute(edge, axis, [(i + 1, i) for i in range(axis_len[axis] - 1)])  16.4 us
    pallas_call x1, Pallas kernels, weight_down(): pl.pallas_call(weight_down_kernel, out_shape=[jax.ShapeDtypeStruct((10, H...  13.5 us
    ppermute x4, starting transfers between devices, from_prev(): lax.ppermute(edge, axis, [(i, i + 1) for i in range(axis_len[axis] - 1)])  12.9 us
    ppermute x4, waiting for transfers between devices, from_prev(): lax.ppermute(edge, axis, [(i, i + 1) for i in range(axis_len[axis] - 1)])  8.01 us
  transfers between devices with their start and end apart: 11, of which 8 were waited for; matrix products, arithmetic and copies ran while one was open for 2% of the time, Pallas kernels for 4%

profile of v2, /device:TPU:0, one launch (start us, length us, event | category | flops | bytes accessed | tf_op | source)
XLA Modules:
  0.0 319.5 jit_solution(11992253376376959079)
XLA Ops:
  0.6 0.9 slice_bitcast_fusion.1
  1.5 2.7 collective-permute-start
  4.2 1.3 collective-permute-start.1
  5.5 0.0 collective-permute-done
  5.5 3.9 %collective-permute-done.1 = bf16[1,48,640]{2,1,0:T(8,128)(2,1)S(1)} collective-permute-done((bf16[1,48,640]{2,1,0:T(8,128)(2,1)S(1)}, bf16[1,48,640]{2,1,0:T(8,128)(2,1)S(1)}, u32[]{:S(2)}, u32[]{:S(2)}) %collective-permute-start.1) | collective-permute-done | bytes 61472 | tf_op jit(solution)/shard_map/ppermute | solution.py:419
  9.4 1.2 pad_maximum_fusion.4
  10.6 3.4 %collective-permute-start.2 = (bf16[26,1,640]{2,1,0:T(2,128)(2,1)S(1)}, bf16[26,1,640]{2,1,0:T(2,128)(2,1)S(1)}, u32[]{:S(2)}, u32[]{:S(2)}) collective-permute-start(bf16[26,1,640]{2,1,0:T(2,128)(2,1)S(1)} %get-tuple-element.24), channel_id=1, source_target_pairs={{0,4},{4,8},{8,12},{1,5},{5,9},{9,13},{2,6},{6,10},{10,14},{3,7},{... | collective-permute-start | bytes 99848 | tf_op jit(solution)/shard_map/ppermute | solution.py:416
  14.0 1.3 collective-permute-start.3
  15.3 0.6 collective-permute-done.2
  15.9 4.5 %collective-permute-done.3 = bf16[26,1,640]{2,1,0:T(2,128)(2,1)S(1)} collective-permute-done((bf16[26,1,640]{2,1,0:T(2,128)(2,1)S(1)}, bf16[26,1,640]{2,1,0:T(2,128)(2,1)S(1)}, u32[]{:S(2)}, u32[]{:S(2)}) %collective-permute-start.3) | collective-permute-done | bytes 33312 | tf_op jit(solution)/shard_map/ppermute | solution.py:419
  20.4 3.8 %pad_maximum_fusion.ext_ref.x_in = bf16[26,50,640]{2,1,0:T(8,128)(2,1)} fusion(bf16[26,1,640]{2,1,0:T(2,128)(2,1)S(1)} %collective-permute-done.3, bf16[1,48,640]{2,1,0:T(8,128)(2,1)S(1)} %collective-permute-done.1, bf16[24,48,640]{2,1,0:T(8,128)(2,1)} %bitcast.17, bf16[1,48,640]{2,1,0:T(8,128)(2,1)S(1)} %collective-permute-done, ...), kind=kLoop, calls=%fused_computation.2 | loop fusion | flops 8320000 | bytes 3328000 | tf_op jit(solution)/shard_map/concatenate | solution.py:426
  24.2 18.2 %shard_map.75 = (f32[2,2,12,24,640]{4,3,2,1,0:T(8,128)}, f32[2,2,12,24,640]{4,3,2,1,0:T(8,128)}) custom-call(bf16[26,50,640]{2,1,0:T(8,128)(2,1)} %pad_maximum_fusion.ext_ref.x_in, bf16[3,1920,640]{2,1,0:T(8,128)(2,1)} %bitcast.24), custom_call_target="tpu_custom_call" | custom-call | flops 8493465600 | bytes 16777216 | tf_op jit(solution)/shard_map/pallas_call | solution.py:81
  42.4 0.0 copy-start.1
  42.4 1.1 slice.39
  43.5 1.3 collective-permute-start.4
  44.8 2.7 collective-permute-done.4
  47.5 1.1 pad_maximum_fusion.1
  48.5 1.3 collective-permute-start.5
  49.8 5.3 %collective-permute-done.5 = f32[2,1,13,1,640]{4,3,2,1,0:T(1,128)S(1)} collective-permute-done((f32[2,1,13,1,640]{4,3,2,1,0:T(1,128)S(1)}, f32[2,1,13,1,640]{4,3,2,1,0:T(1,128)S(1)}, u32[]{:S(2)}, u32[]{:S(2)}) %collective-permute-start.5) | collective-permute-done | bytes 66592 | tf_op jit(solution)/shard_map/ppermute | solution.py:419
  55.1 0.0 copy-done.1
  55.1 0.5 select_maximum_fusion.z_ref
  55.6 0.0 copy-start
  55.6 0.0 copy-start.2
  55.6 0.0 copy-start.3
  55.6 2.6 copy.12
  58.3 0.0 copy-done
  58.3 2.6 collective-permute-start.6
  60.9 0.0 copy-done.2
  60.9 0.2 collective-permute-start.10
  61.1 0.0 copy-done.3
  61.1 2.2 collective-permute-start.7
  63.4 5.8 %collective-permute-done.7 = bf16[1,24,640]{2,1,0:T(8,128)(2,1)S(1)} collective-permute-done((bf16[1,24,640]{2,1,0:T(8,128)(2,1)S(1)}, bf16[1,24,640]{2,1,0:T(8,128)(2,1)S(1)}, u32[]{:S(2)}, u32[]{:S(2)}) %collective-permute-start.7) | collective-permute-done | bytes 30752 | tf_op jit(solution)/shard_map/ppermute | solution.py:416
  69.2 4.5 %collective-permute-start.8 = (bf16[13,1,640]{2,1,0:T(2,128)(2,1)S(1)}, bf16[13,1,640]{2,1,0:T(2,128)(2,1)S(1)}, u32[]{:S(2)}, u32[]{:S(2)}) collective-permute-start(bf16[13,1,640]{2,1,0:T(2,128)(2,1)S(1)} %pad_maximum_fusion.5), channel_id=1, source_target_pairs={{0,4},{4,8},{8,12},{1,5},{5,9},{9,13},{2,6},{6,10},{10,14},{3,7},{... | collective-permute-start | bytes 49928 | tf_op jit(solution)/shard_map/ppermute | solution.py:416
  73.8 1.6 collective-permute-done.8
  75.4 1.2 maximum_maximum_fusion
  76.5 0.1 copy.13
  76.7 0.0 collective-permute-start.9
  76.7 1.9 collective-permute-done.9
  78.6 1.1 copy.15.gp_ref
  79.8 0.0 collective-permute-done.6
  79.8 2.5 copy.14.zp_ref
  82.2 13.5 %shard_map.76 = (f32[10,320,640]{2,1,0:T(8,128)}, bf16[9,288,640]{2,1,0:T(8,128)(2,1)}) custom-call(f32[2,2,13,25,640]{4,3,2,1,0:T(8,128)} %copy-done, f32[2,2,13,25,640]{4,3,2,1,0:T(8,128)} %copy.14.zp_ref, f32[13,25,640]{2,1,0:T(8,128)} %get-tuple-element.29.g_ref.g_in, f32[13,25,640]{2,1,0:T(8,128)} %copy.15.gp_ref), custom_call_target="tpu_custom_call" | custom-call | flops 2123366400 | bytes 16777216 | tf_op jit(solution)/shard_map/pallas_call | solution.py:111
  95.7 0.0 collective-permute-done.10.xp_in
  95.7 0.0 copy-start.6
  95.7 1.2 copy-done.6
  96.9 199.9 %shard_map.77 = (bf16[288,640]{1,0:T(8,128)(2,1)}, bf16[1152,640]{1,0:T(8,128)(2,1)}, f32[18,320,640]{2,1,0:T(8,128)}, f32[18,320,640]{2,1,0:T(8,128)}) custom-call(f32[10,320,640]{2,1,0:T(8,128)} %get-tuple-element.15.p_down, bf16[9,288,640]{2,1,0:T(8,128)(2,1)} %get-tuple-element.16.taps_in, f32[13,25,640]{2,1,0:T(8,128)} %get-tuple-element.29.g_ref.g_in, ...), custom_call_target="tpu_custom_call" | custom-call | flops 84934656000 | bytes 67108864 | tf_op jit(solution)/shard_map/pallas_call | solution.py:370
  296.9 0.0 copy-start.5
  296.9 0.0 copy-start.4
  296.9 20.7 %shard_map.78 = (f32[18,320,640]{2,1,0:T(8,128)}, f32[18,320,640]{2,1,0:T(8,128)}) custom-call(f32[18,320,640]{2,1,0:T(8,128)} %get-tuple-element.20.in_a, f32[18,320,640]{2,1,0:T(8,128)} %get-tuple-element.21.in_b), custom_call_target="tpu_custom_call" | custom-call | tf_op jit(solution)/shard_map/pallas_call | solution.py:405
  317.6 0.0 copy-done.5
  317.6 0.7 copy.18
  318.3 0.0 copy-done.4
  318.3 1.1 copy.19
  (3 shorter events, 0.1 us)
Async XLA Ops:
  1.5 4.0 %collective-permute-start = (bf16[1,48,640]{2,1,0:T(8,128)(2,1)S(1)}, bf16[1,48,640]{2,1,0:T(8,128)(2,1)S(1)}, u32[]{:S(2)}, u32[]{:S(2)}) collective-permute-start(bf16[1,48,640]{2,1,0:T(8,128)(2,1)S(1)} %get-tuple-element.26), channel_id=1, source_target_pairs={{0,1},{1,2},{2,3},{4,5},{5,6},{6,7},{8,9},{9,10},{10,11},{12,13},{... | collective-permute-start | bytes 184328 | tf_op jit(solution)/shard_map/ppermute | solution.py:416
  4.2 5.2 %collective-permute-start.1 = (bf16[1,48,640]{2,1,0:T(8,128)(2,1)S(1)}, bf16[1,48,640]{2,1,0:T(8,128)(2,1)S(1)}, u32[]{:S(2)}, u32[]{:S(2)}) collective-permute-start(bf16[1,48,640]{2,1,0:T(8,128)(2,1)S(1)} %get-tuple-element.27), channel_id=1, source_target_pairs={{1,0},{2,1},{3,2},{5,4},{6,5},{7,6},{9,8},{10,9},{11,10},{13,12},{... | collective-permute-start | bytes 184328 | tf_op jit(solution)/shard_map/ppermute | solution.py:419
  10.6 5.3 %collective-permute-start.2 = (bf16[26,1,640]{2,1,0:T(2,128)(2,1)S(1)}, bf16[26,1,640]{2,1,0:T(2,128)(2,1)S(1)}, u32[]{:S(2)}, u32[]{:S(2)}) collective-permute-start(bf16[26,1,640]{2,1,0:T(2,128)(2,1)S(1)} %get-tuple-element.24), channel_id=1, source_target_pairs={{0,4},{4,8},{8,12},{1,5},{5,9},{9,13},{2,6},{6,10},{10,14},{3,7},{... | collective-permute-start | bytes 99848 | tf_op jit(solution)/shard_map/ppermute | solution.py:416
  14.0 6.4 %collective-permute-start.3 = (bf16[26,1,640]{2,1,0:T(2,128)(2,1)S(1)}, bf16[26,1,640]{2,1,0:T(2,128)(2,1)S(1)}, u32[]{:S(2)}, u32[]{:S(2)}) collective-permute-start(bf16[26,1,640]{2,1,0:T(2,128)(2,1)S(1)} %get-tuple-element.25), channel_id=1, source_target_pairs={{4,0},{8,4},{12,8},{5,1},{9,5},{13,9},{6,2},{10,6},{14,10},{7,3},{... | collective-permute-start | bytes 99848 | tf_op jit(solution)/shard_map/ppermute | solution.py:419
  42.4 12.7 %copy-start.1 = (f32[2,2,12,24,640]{4,3,2,1,0:T(8,128)S(1)}, f32[2,2,12,24,640]{4,3,2,1,0:T(8,128)}, u32[]{:S(2)}) copy-start(f32[2,2,12,24,640]{4,3,2,1,0:T(8,128)} %get-tuple-element.14) | copy-start | bytes 8847364
  43.5 4.0 %collective-permute-start.4 = (f32[1,2,1,24,640]{4,3,2,1,0:T(8,128)S(1)}, f32[1,2,1,24,640]{4,3,2,1,0:T(8,128)S(1)}, u32[]{:S(2)}, u32[]{:S(2)}) collective-permute-start(f32[1,2,1,24,640]{4,3,2,1,0:T(8,128)S(1)} %slice.39), channel_id=1, source_target_pairs={{1,0},{2,1},{3,2},{5,4},{6,5},{7,6},{9,8},{10,9},{11,10},{13,12},{... | collective-permute-start | bytes 368648 | tf_op jit(solution)/shard_map/ppermute | solution.py:419
  48.5 6.6 %collective-permute-start.5 = (f32[2,1,13,1,640]{4,3,2,1,0:T(1,128)S(1)}, f32[2,1,13,1,640]{4,3,2,1,0:T(1,128)S(1)}, u32[]{:S(2)}, u32[]{:S(2)}) collective-permute-start(f32[2,1,13,1,640]{4,3,2,1,0:T(1,128)S(1)} %pad_maximum_fusion.1), channel_id=1, source_target_pairs={{4,0},{8,4},{12,8},{5,1},{9,5},{13,9},{6,2},{10,6},{14,10},{7,3},{... | collective-permute-start | bytes 199688 | tf_op jit(solution)/shard_map/ppermute | solution.py:419
  55.6 2.7 copy-start
  55.6 5.3 %copy-start.2 = (bf16[26,50,640]{2,1,0:T(8,128)(2,1)S(1)}, bf16[26,50,640]{2,1,0:T(8,128)(2,1)}, u32[]{:S(2)}) copy-start(bf16[26,50,640]{2,1,0:T(8,128)(2,1)} %pad_maximum_fusion.ext_ref.x_in) | copy-start | bytes 4992004
  55.6 5.5 %copy-start.3 = (bf16[1,12,24,640]{3,2,1,0:T(8,128)(2,1)S(1)}, bf16[1,12,24,640]{3,2,1,0:T(8,128)(2,1)}, u32[]{:S(2)}) copy-start(bf16[1,12,24,640]{3,2,1,0:T(8,128)(2,1)} %param.7) | copy-start | bytes 1105924
  58.3 21.4 %collective-permute-start.6 = (f32[2,2,13,25,640]{4,1,3,2,0:T(2,128)S(1)}, f32[2,2,13,25,640]{4,1,3,2,0:T(2,128)S(1)}, u32[]{:S(2)}, u32[]{:S(2)}) collective-permute-start(f32[2,2,13,25,640]{4,1,3,2,0:T(2,128)S(1)} %copy.12), channel_id=1, source_target_pairs={{0,1},{1,0},{2,3},{3,2},{4,5},{5,4},{6,7},{7,6},{8,9},{9,8},{10,11... | collective-permute-start | bytes 9984008 | tf_op jit(solution)/shard_map/ppermute | solution.py:422
  60.9 34.7 %collective-permute-start.10 = (bf16[26,50,640]{2,1,0:T(8,128)(2,1)S(1)}, bf16[26,50,640]{2,1,0:T(8,128)(2,1)S(1)}, u32[]{:S(2)}, u32[]{:S(2)}) collective-permute-start(bf16[26,50,640]{2,1,0:T(8,128)(2,1)S(1)} %copy-done.2), channel_id=1, source_target_pairs={{0,1},{1,0},{2,3},{3,2},{4,5},{5,4},{6,7},{7,6},{8,9},{9,8},{10,11... | collective-permute-start | bytes 4992008 | tf_op jit(solution)/shard_map/ppermute | solution.py:422
  61.1 8.1 %collective-permute-start.7 = (bf16[1,24,640]{2,1,0:T(8,128)(2,1)S(1)}, bf16[1,24,640]{2,1,0:T(8,128)(2,1)S(1)}, u32[]{:S(2)}, u32[]{:S(2)}) collective-permute-start(bf16[1,24,640]{2,1,0:T(8,128)(2,1)S(1)} %slice_bitcast_fusion.2), channel_id=1, source_target_pairs={{0,1},{1,2},{2,3},{4,5},{5,6},{6,7},{8,9},{9,10},{10,11},{12,13},{... | collective-permute-start | bytes 92168 | tf_op jit(solution)/shard_map/ppermute | solution.py:416
  69.2 6.1 %collective-permute-start.8 = (bf16[13,1,640]{2,1,0:T(2,128)(2,1)S(1)}, bf16[13,1,640]{2,1,0:T(2,128)(2,1)S(1)}, u32[]{:S(2)}, u32[]{:S(2)}) collective-permute-start(bf16[13,1,640]{2,1,0:T(2,128)(2,1)S(1)} %pad_maximum_fusion.5), channel_id=1, source_target_pairs={{0,4},{4,8},{8,12},{1,5},{5,9},{9,13},{2,6},{6,10},{10,14},{3,7},{... | collective-permute-start | bytes 49928 | tf_op jit(solution)/shard_map/ppermute | solution.py:416
  76.7 1.9 collective-permute-start.9
  95.7 1.2 copy-start.6
  296.9 20.7 %copy-start.5 = (bf16[288,640]{1,0:T(8,128)(2,1)S(1)}, bf16[288,640]{1,0:T(8,128)(2,1)}, u32[]{:S(2)}) copy-start(bf16[288,640]{1,0:T(8,128)(2,1)} %get-tuple-element.18) | copy-start | bytes 1105924
  296.9 21.5 %copy-start.4 = (bf16[1152,640]{1,0:T(8,128)(2,1)S(1)}, bf16[1152,640]{1,0:T(8,128)(2,1)}, u32[]{:S(2)}) copy-start(bf16[1152,640]{1,0:T(8,128)(2,1)} %get-tuple-element.19) | copy-start | bytes 4423684

commit v3 on v2

v3 whole, which is shorter than its diff:
```python
import jax
import jax.numpy as jnp
from jax import lax
from jax.sharding import PartitionSpec as P
from jax.experimental import pallas as pl
from jax.experimental.pallas import tpu as pltpu

MESH = pl.DeviceIdType.MESH
F32, BF16 = jnp.float32, jnp.bfloat16
C = 640
ROWS, COLS = 24, 48
OUT_R, OUT_C = 12, 24
PIX, OPIX = ROWS * COLS, OUT_R * OUT_C
HALF = 320
MIB = 2 ** 20
ORDERS = (('x', 'y', 'z'), ('y', 'z', 'x'), ('z', 'x', 'y'))
R1, R2, R3, A1, A2, A3A, A3B, DA, DB, DC, LA, LB, LC = range(13)


def gelu_tanh(values):
    return jax.nn.gelu(values, approximate=True)


def dot(lhs, rhs):
    return lax.dot_general(lhs, rhs, (((1,), (0,)), ((), ())), preferred_element_type=F32)


def dot_rhs_t(lhs, rhs):
    return lax.dot_general(lhs, rhs, (((1,), (1,)), ((), ())), preferred_element_type=F32)


def dot_lhs_t(lhs, rhs):
    return lax.dot_general(lhs, rhs, (((0,), (0,)), ((), ())), preferred_element_type=F32)


ANY = pl.BlockSpec(memory_space=pl.ANY)


def place():
    w, h = lax.axis_index('w'), lax.axis_index('h')
    bit = {'x': h // 2, 'c': h % 2, 'y': w % 2, 'z': w // 2}
    dev = {'x': (w, (h + 2) % 4), 'c': (w, h + 1 - 2 * (h % 2)), 'y': (w + 1 - 2 * (w % 2), h), 'z': ((w + 2) % 4, h)}
    return bit, dev


class Reducer:
    def __init__(self, index, own, land, out, sems, grants, bit, dev):
        self.index, self.own, self.land, self.out, self.sems, self.grants, self.bit, self.dev = index, own, land, out, sems, grants, bit, dev

    def starts(self, third):
        b = [self.bit[axis] for axis in ORDERS[third]]
        base2 = b[0] * 160
        base3 = base2 + b[1] * 80
        return b, base2, base3, base3 + b[2] * 40

    def copy(self, third, kind):
        b, base2, base3, base4 = self.starts(third)
        core = self.bit['c']
        far = (1 - b[0]) * 160
        src, size, axis = {
            R1: (far, 160, 0), R2: (base2 + (1 - b[1]) * 80, 80, 1), R3: (base3 + (1 - b[2]) * 40, 40, 2),
            A1: (base4, 40, 2), A2: (base3, 80, 1), A3A: (base3, 80, 0), A3B: (base2 + (1 - b[1]) * 80, 80, 0),
            DA: (base2, 160, 'c'), DB: (far + b[1] * 80, 80, 'c'), DC: (far + (1 - b[1]) * 80, 80, 'c'),
            LA: (base2, 160, None), LB: (far + b[1] * 80, 80, None), LC: (far + (1 - b[1]) * 80, 80, None),
        }[kind]
        rows = pl.ds(pl.multiple_of(src, 8), size)
        source = self.own.at[pl.ds(core + 3 * third, 3), rows]
        send, recv = (s.at[self.index, third, kind] for s in self.sems)
        if kind <= R3:
            target = self.land.at[pl.ds(3 * third, 3), pl.ds((0, 160, 240)[kind], size)]
        elif kind <= A3B:
            target = source
        else:
            target = self.out.at[pl.ds(9 * core + 3 * third, 3), rows]
        if axis is None:
            return pltpu.make_async_copy(source, target, recv)
        peer = self.dev[axis if axis == 'c' else ORDERS[third][axis]]
        return pltpu.make_async_remote_copy(src_ref=source, dst_ref=target, send_sem=send, recv_sem=recv, device_id=peer, device_id_type=MESH)

    def add(self, third, kind):
        _, base2, base3, base4 = self.starts(third)
        keep, size = ((base2, 160), (base3, 80), (base4, 40))[kind]
        land_at = (0, 160, 240)[kind]
        steps = size // 40

        def body(j, _):
            unit, row = 3 * third + j // steps, (j % steps) * 40
            rows = pl.ds(pl.multiple_of(keep + row, 8), 40)
            where = self.bit['c'] + unit
            self.own[where, rows, :] += self.land[unit, pl.ds(pl.multiple_of(land_at + row, 8), 40), :]
            return 0
        lax.fori_loop(0, 3 * steps, body, 0)

    def begin(self):
        for third in range(3):
            self.copy(third, R1).start()

    def move(self, wait_for, then, add=False):
        for third in range(3):
            self.copy(third, wait_for).wait()
            if add:
                pl.semaphore_signal(self.grants.at[self.index, third, wait_for], inc=1, device_id=self.dev[ORDERS[third][wait_for]], device_id_type=MESH)
                self.add(third, wait_for)
            for kind in then:
                if kind in (A1, A2, A3A):
                    pl.semaphore_wait(self.grants.at[self.index, third, {A1: R3, A2: R2, A3A: R1}[kind]], 1)
                self.copy(third, kind).start()

    def finish(self):
        for kind in (DA, DB, DC, LA, LB, LC):
            self.move(kind, ())


EDGE = 8
LINES = (ROWS + 2) * COLS
BLOCK = 8 * COLS
NEAR = [(dw, dh) for dw in (-1, 0, 1) for dh in (-1, 0, 1) if (dw, dh) != (0, 0)]
ABOVE = [(-1, -1), (-1, 0), (0, -1)]
BELOW = [(1, 1), (1, 0), (0, 1)]
G_AT, G_PAIR_AT, TAP_PAIR_AT = 3 * OPIX, 4 * OPIX, 5 * OPIX


def lane(k):
    return pl.ds(k * 128, 128)


def at(start, size):
    return pl.ds(pl.multiple_of(start, size), size)


class Border:
    def __init__(self, grid, row0, rows, cols, send, land, sems, send_to, take_from):
        self.grid, self.row0, self.rows, self.cols, self.sends, self.lands = grid, row0, rows, cols, send, land
        self.sems, self.send_to, self.take_from = sems, send_to, take_from
        self.w, self.h = lax.axis_index('w'), lax.axis_index('h')

    def edge(self, step, first, size, outside):
        return {-1: first - outside, 1: first + size - 1 + outside}[step]

    def copies(self):
        found = []
        for dw, dh in self.send_to:
            i = NEAR.index((dw, dh))
            if dw == 0:
                src, dst = self.sends[0].at[(dh + 1) // 2], self.lands[0].at[(1 - dh) // 2]
            elif dh == 0:
                src, dst = self.sends[1].at[(dw + 1) // 2], self.lands[1].at[(1 - dw) // 2]
            else:
                src = self.sends[2].at[2 * ((dh + 1) // 2) + (dw + 1) // 2]
                dst = self.lands[2].at[2 * ((1 - dh) // 2) + (1 - dw) // 2]
            peer = ((self.w + dw + 4) % 4, (self.h + dh + 4) % 4)
            found.append(pltpu.make_async_remote_copy(src_ref=src, dst_ref=dst, send_sem=self.sems.at[0, i], recv_sem=self.sems.at[1, i], device_id=peer, device_id_type=MESH))
        return found

    def start(self):
        grid, row0, rows, cols = self.grid, self.row0, self.rows, self.cols
        for dw, dh in self.send_to:
            r = None if dh == 0 else self.edge(dh, row0, rows, 0)
            c = None if dw == 0 else self.edge(dw, EDGE, cols, 0)
            for k in range(5):
                if dw == 0:
                    self.sends[0][(dh + 1) // 2, :, lane(k)] = grid[k, r, EDGE:EDGE + cols, :]
                elif dh == 0:
                    for row in range(rows):
                        self.sends[1][(dw + 1) // 2, row:row + 1, lane(k)] = grid[k, row0 + row, c:c + 1, :]
                else:
                    self.sends[2][2 * ((dh + 1) // 2) + (dw + 1) // 2, :, lane(k)] = jnp.broadcast_to(grid[k, r, c:c + 1, :], (8, 128))
        for copy in self.copies():
            copy.start()

    def finish(self):
        grid, row0, rows, cols = self.grid, self.row0, self.rows, self.cols
        for copy in self.copies():
            copy.wait()
        for dw, dh in self.take_from:
            r = None if dh == 0 else self.edge(dh, row0, rows, 1)
            c = None if dw == 0 else self.edge(dw, EDGE, cols, 1)
            out_w = {-1: self.w == 0, 0: False, 1: self.w == 3}[dw]
            out_h = {-1: self.h == 0, 0: False, 1: self.h == 3}[dh]
            for k in range(5):
                if dw == 0:
                    grid[k, r, EDGE:EDGE + cols, :] = jnp.where(out_h, 0.0, self.lands[0][(dh + 1) // 2, :, lane(k)])
                elif dh == 0:
                    for row in range(rows):
                        grid[k, row0 + row, c:c + 1, :] = jnp.where(out_w, 0.0, self.lands[1][(dw + 1) // 2, row:row + 1, lane(k)])
                else:
                    out = jnp.logical_or(out_w, out_h)
                    grid[k, r, c:c + 1, :] = jnp.where(out, 0.0, self.lands[2][2 * ((dh + 1) // 2) + (dw + 1) // 2, 0:1, lane(k)])


def spread(grid, xs):
    def one_row(r, _):
        for c in range(3):
            for k in range(5):
                xs[0, at(c * LINES + r * COLS, COLS), lane(k)] = grid[k, r, EDGE - 1 + c:EDGE - 1 + c + COLS, :].astype(BF16)
        return 0
    lax.fori_loop(0, ROWS + 2, one_row, 0)


def accumulate(acc, rows, part, first):
    for k in range(5):
        piece = part[:, k * 128:(k + 1) * 128]
        acc[k, 0:rows, :] = piece if first else acc[k, 0:rows, :] + piece


def block_kernel(x_in, g_in, w_first, w_down, y_out, dx_out, o_down, o_first, x_land,
                 own_d, own_f, land_d, land_f, wbuf, xs, taps, g_tile, g_grid, da, da_pair, grid, acc,
                 send_r, send_c, send_k, x_r, x_c, x_k, z_r, z_c, z_k, d_r, d_c, d_k, gs_r, gs_c, gs_k, gl_r, gl_c, gl_k,
                 load_sems, pair_sems, near_sems, out_sems, send_sems, recv_sems, grants):
    bit, dev = place()
    w, h = lax.axis_index('w'), lax.axis_index('h')
    core = bit['c']
    x_tile = xs.at[0, pl.ds(0, PIX)]
    load_x = pltpu.make_async_copy(x_in, x_tile, load_sems.at[0])
    load_g = pltpu.make_async_copy(g_in, g_tile, load_sems.at[1])
    load_w = pltpu.make_async_copy(w_first, wbuf, load_sems.at[2])
    for load in (load_x, load_g, load_w):
        load.start()
    barrier = pltpu.get_barrier_semaphore()
    for axis in 'xyzc':
        pl.semaphore_signal(barrier, inc=1, device_id=dev[axis], device_id_type=MESH)
    for dw, dh in NEAR:
        pl.semaphore_signal(barrier, inc=1, device_id=((w + dw + 4) % 4, (h + dh + 4) % 4), device_id_type=MESH)
    sends = (send_r, send_c, send_k)
    x_border = Border(grid, 1, ROWS, COLS, sends, (x_r, x_c, x_k), near_sems.at[0], NEAR, NEAR)
    z_border = Border(grid, 0, ROWS, COLS, sends, (z_r, z_c, z_k), near_sems.at[1], ABOVE, BELOW)
    d_border = Border(grid, 1, ROWS, COLS, sends, (d_r, d_c, d_k), near_sems.at[2], NEAR, NEAR)
    g_border = Border(g_grid, 1, OUT_R, OUT_C, (gs_r, gs_c, gs_k), (gl_r, gl_c, gl_k), near_sems.at[3], BELOW, ABOVE)
    sems = (send_sems, recv_sems)
    down = Reducer(0, own_d, land_d, o_down, sems, grants, bit, dev)
    first = Reducer(1, own_f, land_f, o_first, sems, grants, bit, dev)

    def to_pair(src, dst, i):
        return pltpu.make_async_remote_copy(src_ref=src, dst_ref=dst, send_sem=pair_sems.at[0, i], recv_sem=pair_sems.at[1, i], device_id=dev['c'], device_id_type=MESH)

    load_x.wait()

    def place_row(r, _):
        for k in range(5):
            grid[k, r + 1, EDGE:EDGE + COLS, :] = x_tile[at(r * COLS, COLS), lane(k)].astype(F32)
        return 0
    lax.fori_loop(0, ROWS, place_row, 0)
    pl.semaphore_wait(barrier, 12)
    x_border.start()
    load_g.wait()
    for r in range(OUT_R):
        for k in range(5):
            g_grid[k, r + 1, EDGE:EDGE + OUT_C, :] = g_tile[r, :, lane(k)].astype(F32)
    g_border.start()
    x_border.finish()
    spread(grid, xs)
    x_share = to_pair(xs.at[0], x_land, 0)
    x_share.start()
    load_w.wait()

    def pre_rows(i, _):
        for t in range(9):
            a, c = t // 3, t % 3
            rows = pl.ds(pl.multiple_of(c * LINES + i * BLOCK + a * COLS, COLS), BLOCK)
            accumulate(acc, BLOCK, dot(xs[0, rows, :], wbuf[t]), t == 0)
        for k in range(5):
            pre = acc[k].astype(BF16).astype(F32)
            acc[k] = pre
            act = gelu_tanh(pre).astype(BF16).astype(F32)
            for r in range(8):
                grid[k, 8 * i + r, EDGE:EDGE + COLS, :] = act[r * COLS:(r + 1) * COLS]
        for r in range(8):
            for cp in range(2):
                for k in range(5):
                    own_f[2 * (r % 2) + cp, pl.ds(pl.multiple_of((4 * i + r // 2) * OUT_C, 8), OUT_C), lane(k)] = acc[k, pl.ds(r * COLS + cp, OUT_C, stride=2), :]
        return 0
    lax.fori_loop(0, 3, pre_rows, 0)
    load_w2 = pltpu.make_async_copy(w_down, wbuf, load_sems.at[3])
    load_w2.start()
    z_border.start()

    g_border.finish()
    for di in range(2):
        for dj in range(2):
            for k in range(5):
                part = g_grid[k, di:di + OUT_R, EDGE - 1 + dj:EDGE - 1 + dj + OUT_C, :]
                xs[1, (2 * di + dj) * OPIX:(2 * di + dj + 1) * OPIX, lane(k)] = part.reshape(OPIX, 128).astype(BF16)
    g_share = to_pair(xs.at[1, pl.ds(G_AT, OPIX)], xs.at[1, pl.ds(G_PAIR_AT, OPIX)], 1)
    g_share.start()
    z_border.finish()

    def tap_rows(p, _):
        for t in range(9):
            a, c = t // 3, t % 3
            for k in range(5):
                cols = pl.ds(EDGE + c, OUT_C, stride=2)
                two = jnp.concatenate([grid[k, 4 * p + a, cols, :], grid[k, 4 * p + 2 + a, cols, :]], 0)
                taps[t, at(p * 2 * OUT_C, 2 * OUT_C), lane(k)] = two.astype(BF16)
        return 0
    lax.fori_loop(0, OUT_R // 2, tap_rows, 0)
    tap_shares = [to_pair(taps.at[4 * (1 - core) + j], xs.at[1, pl.ds(TAP_PAIR_AT + j * OPIX, OPIX)], 2 + j) for j in range(5)]
    for share in tap_shares:
        share.start()

    def down_tap(j, _):
        res = dot_lhs_t(taps[4 * core + j], xs[1, G_AT:G_AT + OPIX, :])
        own_d[2 * j] = res[:HALF]
        own_d[2 * j + 1] = res[HALF:]
        return 0
    lax.fori_loop(0, 5, down_tap, 0)
    g_share.wait()
    for share in tap_shares:
        share.wait()

    def down_tap_pair(j, _):
        rows = pl.ds(pl.multiple_of(TAP_PAIR_AT + j * OPIX, 32), OPIX)
        res = dot_lhs_t(xs[1, rows, :], xs[1, G_PAIR_AT:G_PAIR_AT + OPIX, :])
        own_d[2 * j] += res[:HALF]
        own_d[2 * j + 1] += res[HALF:]
        return 0
    lax.fori_loop(0, 5, down_tap_pair, 0)
    down.begin()

    load_w2.wait()
    for rp in range(2):
        for cp in range(2):
            total = None
            for a in ((0, 2), (1,))[rp]:
                for c in ((0, 2), (1,))[cp]:
                    row = (2 * (1 - a // 2) + 1 - c // 2) * OPIX
                    part = dot_rhs_t(xs[1, row:row + OPIX, :], wbuf[3 * a + c])
                    total = part if total is None else total + part
            pre = own_f[2 * rp + cp, 0:OPIX, :]
            grad = jax.vjp(gelu_tanh, pre)[1](total)[0].astype(BF16).astype(F32)
            for i in range(OUT_R):
                for k in range(5):
                    grid[k, 2 * i + rp + 1, pl.ds(EDGE + cp, OUT_C, stride=2), :] = grad[i * OUT_C:(i + 1) * OUT_C, k * 128:(k + 1) * 128]

    def pack(r, _):
        for k in range(5):
            da[at(r * COLS, COLS), lane(k)] = grid[k, r + 1, EDGE:EDGE + COLS, :].astype(BF16)
        return 0
    lax.fori_loop(0, ROWS, pack, 0)
    da_share = to_pair(da, da_pair, 7)
    da_share.start()
    d_border.start()
    x_share.wait()
    pair_load = pltpu.make_async_copy(x_land, xs.at[1], load_sems.at[4])
    pair_load.start()

    for t in range(9):
        accumulate(acc, OPIX, dot(taps[t], wbuf[t]), t == 0)
    for k in range(5):
        taps[0, :, lane(k)] = acc[k, 0:OPIX, :].astype(BF16)
    y_copy = pltpu.make_async_copy(taps.at[0], y_out, out_sems.at[0])
    y_copy.start()
    load_w1 = pltpu.make_async_copy(w_first, wbuf, load_sems.at[5])
    load_w1.start()
    pair_load.wait()
    da_share.wait()

    def first_tap(j, _):
        t = 4 * core + j
        a, c = t // 3, t % 3
        rows = pl.ds(pl.multiple_of(c * LINES + a * COLS, COLS), PIX)
        res = dot_lhs_t(xs[0, rows, :], da[...]) + dot_lhs_t(xs[1, rows, :], da_pair[...])
        own_f[2 * j] = res[:HALF]
        own_f[2 * j + 1] = res[HALF:]
        return 0
    lax.fori_loop(0, 4, first_tap, 0)
    down.move(R1, (R2,), add=True)
    first_tap(4, 0)
    first.begin()

    d_border.finish()
    spread(grid, xs)
    load_w1.wait()

    def image_rows(i, _):
        for t in range(9):
            a, c = t // 3, t % 3
            rows = pl.ds(pl.multiple_of((2 - c) * LINES + i * BLOCK + (2 - a) * COLS, COLS), BLOCK)
            accumulate(acc, BLOCK, dot_rhs_t(xs[0, rows, :], wbuf[t]), t == 0)
        for k in range(5):
            da_pair[at(i * BLOCK, BLOCK), lane(k)] = acc[k].astype(BF16)
        return 0
    lax.fori_loop(0, 3, image_rows, 0)
    dx_copy = pltpu.make_async_copy(da_pair, dx_out, out_sems.at[1])
    dx_copy.start()

    down.move(R2, (R3,), add=True)
    first.move(R1, (R2,), add=True)
    down.move(R3, (A1,), add=True)
    first.move(R2, (R3,), add=True)
    down.move(A1, (A2, A3A))
    first.move(R3, (A1,), add=True)
    down.move(A2, (A3B, DA, LA))
    first.move(A1, (A2, A3A))
    down.move(A3A, (DB, LB))
    first.move(A2, (A3B, DA, LA))
    down.move(A3B, (DC, LC))
    first.move(A3A, (DB, LB))
    first.move(A3B, (DC, LC))
    y_copy.wait()
    dx_copy.wait()
    down.finish()
    first.finish()


def block_call(image, grad_out, w_first, w_down):
    total = jax.ShapeDtypeStruct((18, HALF, C), F32)
    dma = pltpu.SemaphoreType.DMA
    edges = [pltpu.VMEM((2, COLS, C), F32), pltpu.VMEM((2, ROWS, C), F32), pltpu.VMEM((4, 8, C), F32)]
    small = [pltpu.VMEM((2, OUT_C, C), F32), pltpu.VMEM((2, OUT_R, C), F32), pltpu.VMEM((4, 8, C), F32)]
    return pl.pallas_call(
        block_kernel,
        out_shape=[jax.ShapeDtypeStruct((OPIX, C), BF16), jax.ShapeDtypeStruct((PIX, C), BF16), total, total,
                   jax.ShapeDtypeStruct((3 * LINES, C), BF16)],
        in_specs=[ANY] * 4, out_specs=[ANY] * 5,
        scratch_shapes=[pltpu.VMEM((10, HALF, C), F32)] * 2 + [pltpu.VMEM((9, 280, C), F32)] * 2
        + [pltpu.VMEM((9, C, C), BF16), pltpu.VMEM((2, 3 * LINES, C), BF16), pltpu.VMEM((9, OPIX, C), BF16)]
        + [pltpu.VMEM((OUT_R, OUT_C, C), BF16), pltpu.VMEM((5, OUT_R + 1, OUT_C + EDGE, 128), F32)]
        + [pltpu.VMEM((PIX, C), BF16)] * 2
        + [pltpu.VMEM((5, ROWS + 2, COLS + 2 * EDGE, 128), F32), pltpu.VMEM((5, BLOCK, 128), F32)]
        + edges * 4 + small * 2
        + [dma((6,)), dma((2, 8)), dma((4, 2, 8)), dma((2,)), dma((2, 3, 13)), dma((2, 3, 13)), pltpu.SemaphoreType.REGULAR((2, 3, 3))],
        compiler_params=pltpu.CompilerParams(collective_id=1, has_side_effects=True, vmem_limit_bytes=67043328),
        cost_estimate=pl.CostEstimate(flops=2 * PIX * 90 * C * C, bytes_accessed=64 * MIB, transcendentals=0),
    )(image.reshape(PIX, C), grad_out, w_first, w_down)


def settle_kernel(in_a, in_b, out_a, out_b, buf, load_sems, store_sems):
    loads, stores = [], []
    for i, (src, dst) in enumerate(((in_a, out_a), (in_b, out_b))):
        for part in range(9):
            span = pl.ds(2 * part, 2)
            loads.append(pltpu.make_async_copy(src.at[span], buf.at[i, span], load_sems.at[i, part]))
            stores.append(pltpu.make_async_copy(buf.at[i, span], dst.at[span], store_sems.at[i, part]))
    for load in loads:
        load.start()
    for load, store in zip(loads, stores):
        load.wait()
        store.start()
    for store in stores:
        store.wait()


def settle(sum_a, sum_b):
    shape = jax.ShapeDtypeStruct((18, HALF, C), F32)
    return pl.pallas_call(
        settle_kernel, out_shape=[shape, shape], in_specs=[ANY] * 2, out_specs=[ANY] * 2,
        scratch_shapes=[pltpu.VMEM((2, 18, HALF, C), F32), pltpu.SemaphoreType.DMA((2, 9)), pltpu.SemaphoreType.DMA((2, 9))],
        compiler_params=pltpu.CompilerParams(vmem_limit_bytes=56 * MIB),
    )(sum_a, sum_b)


def solution(mesh):
    def block_step(image, w_first, w_down, grad_out):
        block_out, grad_image, sum_down, sum_first, _ = block_call(image[0], grad_out[0], w_first.reshape(9, C, C), w_down.reshape(9, C, C))
        grad_w_down, grad_w_first = settle(sum_down, sum_first)
        return (block_out.reshape(1, OUT_R, OUT_C, C), grad_image.reshape(1, ROWS, COLS, C),
                grad_w_first.reshape(3, 3, C, C), grad_w_down.reshape(3, 3, C, C))

    img_spec = P(None, 'h', 'w', None)
    return jax.shard_map(block_step, mesh=mesh, in_specs=(img_spec, P(), P(), img_spec), out_specs=(img_spec, img_spec, P(), P()), check_vma=False)
```

time: 320 us -> 257 us (0.80)
  waiting for transfers between devices: 26.3 us -> 0 us
  starting transfers between devices: 20.9 us -> 0 us
  local copies, waits for them, and re-layouts: 11.5 us -> 1.86 us
  other arithmetic: 7.7 us -> 0 us
    ppermute x11 -> x0, waiting for transfers between devices: 26.3 us -> none  [the longest x4 16.4 us: from_next(): lax.ppermute(edge, axis, [(i + 1, i) for i in range(axis_len[axis] - 1)])]
    ppermute x11 -> x0, starting transfers between devices: 20.9 us -> none  [the longest x4 12.9 us: from_prev(): lax.ppermute(edge, axis, [(i, i + 1) for i in range(axis_len[axis] - 1)])]
    concatenate x5 -> x0, other arithmetic: 6.53 us -> none  [the longest x1 3.77 us: frame(): jnp.concatenate([from_prev(rows[:, -1:], 'w'), rows, from_next(rows[:, :1...]
    pallas_call x3 -> x1, Pallas kernels: 232 us -> 234 us  [block_call(): pl.pallas_call(block_kernel, out_shape=[jax.ShapeDtypeStruct((OPIX, C), B...]
  transfers between devices with their start and end apart: 11 -> 0, of which waited for: 8 -> 0; matrix products, arithmetic and copies ran while one was open for 2% -> 0% of each run, Pallas kernels for 4% -> 0%
where the time goes in v3:
time: 257 us
  Pallas kernels  255 us (99%)
    pallas_call x1, Pallas kernels, block_call(): pl.pallas_call(block_kernel, out_shape=[jax.ShapeDtypeStruct((OPIX, C), B...  234 us
    pallas_call x1, Pallas kernels, settle(): pl.pallas_call(settle_kernel, out_shape=[shape, shape], in_specs=[ANY] *...  20.7 us

profile of v3, /device:TPU:0, one launch (start us, length us, event | category | flops | bytes accessed | tf_op | source)
XLA Modules:
  0.0 257.3 jit_solution(5184506014119694102)
XLA Ops:
  0.6 234.0 %shard_map.75 = (bf16[288,640]{1,0:T(8,128)(2,1)}, bf16[1152,640]{1,0:T(8,128)(2,1)}, f32[18,320,640]{2,1,0:T(8,128)}, f32[18,320,640]{2,1,0:T(8,128)}, bf16[3744,640]{1,0:T(8,128)(2,1)}) custom-call(bf16[1152,640]{1,0:T(8,128)(2,1)} %bitcast.14, bf16[12,24,640]{2,1,0:T(8,128)(2,1)} %bitcast.15, bf16[9,640,640]{2,1,0:T(8,128)(2,1)} %bitcast.12, ...), custom_call_target="tpu_custom_call" | custom-call | flops 84934656000 | bytes 67108864 | tf_op jit(solution)/shard_map/pallas_call | solution.py:410
  234.7 0.0 copy-start.1
  234.7 0.0 copy-start
  234.7 20.7 %shard_map.76 = (f32[18,320,640]{2,1,0:T(8,128)}, f32[18,320,640]{2,1,0:T(8,128)}) custom-call(f32[18,320,640]{2,1,0:T(8,128)} %get-tuple-element.12.in_a, f32[18,320,640]{2,1,0:T(8,128)} %get-tuple-element.13.in_b), custom_call_target="tpu_custom_call" | custom-call | tf_op jit(solution)/shard_map/pallas_call | solution.py:445
  255.4 0.0 copy-done.1
  255.4 0.7 copy.10
  256.2 0.0 copy-done
  256.2 1.1 copy.11
Async XLA Ops:
  234.7 20.7 %copy-start.1 = (bf16[288,640]{1,0:T(8,128)(2,1)S(1)}, bf16[288,640]{1,0:T(8,128)(2,1)}, u32[]{:S(2)}) copy-start(bf16[288,640]{1,0:T(8,128)(2,1)} %get-tuple-element.10) | copy-start | bytes 1105924
  234.7 21.5 %copy-start = (bf16[1152,640]{1,0:T(8,128)(2,1)S(1)}, bf16[1152,640]{1,0:T(8,128)(2,1)}, u32[]{:S(2)}) copy-start(bf16[1152,640]{1,0:T(8,128)(2,1)} %get-tuple-element.11) | copy-start | bytes 4423684

commit v4 on v3

v4 whole, which is shorter than its diff:
```python
import jax
import jax.numpy as jnp
from jax import lax
from jax.sharding import PartitionSpec as P
from jax.experimental import pallas as pl
from jax.experimental.pallas import tpu as pltpu

MESH = pl.DeviceIdType.MESH
F32, BF16 = jnp.float32, jnp.bfloat16
C = 640
ROWS, COLS = 24, 48
OUT_R, OUT_C = 12, 24
PIX, OPIX = ROWS * COLS, OUT_R * OUT_C
HALF = 320
MIB = 2 ** 20
OWN_SPACE = 50462720
ORDERS = (('x', 'y', 'z'), ('y', 'z', 'x'), ('z', 'x', 'y'))
R1, R2, R3, A1, A2, A3A, A3B, DA, DB, DC = range(10)
QUARTER = HALF // 2
EIGHTH = QUARTER // 2
LEAST = EIGHTH // 2
LAND_AT = (0, QUARTER, QUARTER + EIGHTH)
LANES = range(C // 128)
TAPS = [(t, t // 3, t % 3) for t in range(9)]
THIRDS = range(3)


def gelu_tanh(values):
    return jax.nn.gelu(values, approximate=True)


def dot(lhs, rhs):
    return lax.dot_general(lhs, rhs, (((1,), (0,)), ((), ())), preferred_element_type=F32)


def dot_rhs_t(lhs, rhs):
    return lax.dot_general(lhs, rhs, (((1,), (1,)), ((), ())), preferred_element_type=F32)


def dot_lhs_t(lhs, rhs):
    return lax.dot_general(lhs, rhs, (((0,), (0,)), ((), ())), preferred_element_type=F32)


ANY = pl.BlockSpec(memory_space=pl.ANY)


def place():
    w, h = lax.axis_index('w'), lax.axis_index('h')
    bit = {'x': h // 2, 'c': h % 2, 'y': w % 2, 'z': w // 2}
    dev = {'x': (w, (h + 2) % 4), 'c': (w, h + 1 - 2 * (h % 2)), 'y': (w + 1 - 2 * (w % 2), h), 'z': ((w + 2) % 4, h)}
    return bit, dev


class Reducer:
    def __init__(self, index, own, land, out, sems, grants, bit, dev):
        self.index, self.own, self.land, self.out, self.sems, self.grants, self.bit, self.dev = index, own, land, out, sems, grants, bit, dev

    def starts(self, third):
        b = [self.bit[axis] for axis in ORDERS[third]]
        base2 = b[0] * QUARTER
        base3 = base2 + b[1] * EIGHTH
        return b, base2, base3, base3 + b[2] * LEAST

    def copy(self, third, kind):
        (b0, b1, b2), base2, base3, base4 = self.starts(third)
        axis0, axis1, axis2 = ORDERS[third]
        far = (1 - b0) * QUARTER
        near1, far1 = b1 * EIGHTH, (1 - b1) * EIGHTH
        src, size, axis = {
            R1: (far, QUARTER, axis0), R2: (base2 + far1, EIGHTH, axis1), R3: (base3 + (1 - b2) * LEAST, LEAST, axis2),
            A1: (base4, LEAST, axis2), A2: (base3, EIGHTH, axis1), A3A: (base3, EIGHTH, axis0), A3B: (base2 + far1, EIGHTH, axis0),
            DA: (base2, QUARTER, 'c'), DB: (far + near1, EIGHTH, 'c'), DC: (far + far1, EIGHTH, 'c'),
        }[kind]
        rows = pl.ds(pl.multiple_of(src, 8), size)
        units = pl.ds(3 * third, 3)
        source = self.own.at[pl.ds(self.bit['c'] + 3 * third, 3), rows]
        send, recv = (s.at[self.index, third, kind] for s in self.sems)
        if kind <= R3:
            target = self.land.at[units, pl.ds(LAND_AT[kind], size)]
        elif kind <= A3B:
            target = source
        else:
            target = self.out.at[units, rows]
        return pltpu.make_async_remote_copy(src_ref=source, dst_ref=target, send_sem=send, recv_sem=recv, device_id=self.dev[axis], device_id_type=MESH)

    def add(self, third, kind):
        _, base2, base3, base4 = self.starts(third)
        keep, size = ((base2, QUARTER), (base3, EIGHTH), (base4, LEAST))[kind]
        steps = size // LEAST

        def body(j):
            unit, row = 3 * third + j // steps, (j % steps) * LEAST
            rows = pl.ds(pl.multiple_of(keep + row, 8), LEAST)
            self.own[self.bit['c'] + unit, rows, :] += self.land[unit, pl.ds(pl.multiple_of(LAND_AT[kind] + row, 8), LEAST), :]
        run(3 * steps, body)

    def begin(self):
        for third in THIRDS:
            self.copy(third, R1).start()

    def move(self, wait_for, then, add=False):
        for third in THIRDS:
            self.copy(third, wait_for).wait()
            if add:
                pl.semaphore_signal(self.grants.at[self.index, third, wait_for], inc=1, device_id=self.dev[ORDERS[third][wait_for]], device_id_type=MESH)
                self.add(third, wait_for)
            for kind in then:
                if kind in (A1, A2, A3A):
                    pl.semaphore_wait(self.grants.at[self.index, third, {A1: R3, A2: R2, A3A: R1}[kind]], 1)
                self.copy(third, kind).start()

    def finish(self):
        for kind in (DA, DB, DC):
            self.move(kind, ())


EDGE = 8
LINES = (ROWS + 2) * COLS
BLOCK = 8 * COLS
NEAR = [(dw, dh) for dw in (-1, 0, 1) for dh in (-1, 0, 1) if (dw, dh) != (0, 0)]
ABOVE = [(-1, -1), (-1, 0), (0, -1)]
BELOW = [(1, 1), (1, 0), (0, 1)]
G_AT, G_PAIR_AT, TAP_PAIR_AT = 3 * OPIX, 4 * OPIX, 5 * OPIX


def lane(k):
    return slice(k * 128, k * 128 + 128)


def run(steps, body):
    lax.fori_loop(0, steps, lambda i, _: body(i), None)


def clear_of(flag, value):
    return jnp.where(flag, 0.0, value)


def at(start, size):
    return pl.ds(pl.multiple_of(start, size), size)


class Border:
    def __init__(self, grid, row0, rows, cols, send, land, sems, send_to, take_from):
        self.grid, self.row0, self.rows, self.cols, self.sends, self.lands = grid, row0, rows, cols, send, land
        self.sems, self.send_to, self.take_from = sems, send_to, take_from
        self.w, self.h = lax.axis_index('w'), lax.axis_index('h')

    def edge(self, step, first, size, outside):
        return {-1: first - outside, 1: first + size - 1 + outside}[step]

    def copies(self):
        found = []
        for dw, dh in self.send_to:
            i = NEAR.index((dw, dh))
            if dw == 0:
                src, dst = self.sends[0].at[(dh + 1) // 2], self.lands[0].at[(1 - dh) // 2]
            elif dh == 0:
                src, dst = self.sends[1].at[(dw + 1) // 2], self.lands[1].at[(1 - dw) // 2]
            else:
                src = self.sends[2].at[2 * ((dh + 1) // 2) + (dw + 1) // 2]
                dst = self.lands[2].at[2 * ((1 - dh) // 2) + (1 - dw) // 2]
            peer = ((self.w + dw + 4) % 4, (self.h + dh + 4) % 4)
            found.append(pltpu.make_async_remote_copy(src_ref=src, dst_ref=dst, send_sem=self.sems.at[0, i], recv_sem=self.sems.at[1, i], device_id=peer, device_id_type=MESH))
        return found

    def start(self):
        grid, row0, rows, cols = self.grid, self.row0, self.rows, self.cols
        for dw, dh in self.send_to:
            r = None if dh == 0 else self.edge(dh, row0, rows, 0)
            c = None if dw == 0 else self.edge(dw, EDGE, cols, 0)
            for k in LANES:
                if dw == 0:
                    self.sends[0][(dh + 1) // 2, :, lane(k)] = grid[k, r, EDGE:EDGE + cols, :]
                elif dh == 0:
                    for row in range(rows):
                        self.sends[1][(dw + 1) // 2, row:row + 1, lane(k)] = grid[k, row0 + row, c:c + 1, :]
                else:
                    self.sends[2][2 * ((dh + 1) // 2) + (dw + 1) // 2, :, lane(k)] = jnp.broadcast_to(grid[k, r, c:c + 1, :], (8, 128))
        for copy in self.copies():
            copy.start()

    def finish(self):
        grid, row0, rows, cols = self.grid, self.row0, self.rows, self.cols
        for copy in self.copies():
            copy.wait()
        for dw, dh in self.take_from:
            r = None if dh == 0 else self.edge(dh, row0, rows, 1)
            c = None if dw == 0 else self.edge(dw, EDGE, cols, 1)
            out_w = {-1: self.w == 0, 0: False, 1: self.w == 3}[dw]
            out_h = {-1: self.h == 0, 0: False, 1: self.h == 3}[dh]
            for k in LANES:
                if dw == 0:
                    grid[k, r, EDGE:EDGE + cols, :] = clear_of(out_h, self.lands[0][(dh + 1) // 2, :, lane(k)])
                elif dh == 0:
                    for row in range(rows):
                        grid[k, row0 + row, c:c + 1, :] = clear_of(out_w, self.lands[1][(dw + 1) // 2, row:row + 1, lane(k)])
                else:
                    out = jnp.logical_or(out_w, out_h)
                    grid[k, r, c:c + 1, :] = clear_of(out, self.lands[2][2 * ((dh + 1) // 2) + (dw + 1) // 2, 0:1, lane(k)])


def spread(grid, xs):
    def one_row(r):
        for c in range(3):
            for k in LANES:
                xs[0, at(c * LINES + r * COLS, COLS), lane(k)] = grid[k, r, EDGE - 1 + c:EDGE - 1 + c + COLS, :].astype(BF16)
    run(ROWS + 2, one_row)


def accumulate(acc, rows, part, first):
    for k in LANES:
        piece = part[:, lane(k)]
        acc[k, 0:rows, :] = piece if first else acc[k, 0:rows, :] + piece


def block_kernel(x_in, g_in, w_first, w_down, y_out, dx_out, own_d, own_f, o_down, o_first, x_land,
                 land_d, land_f, wbuf, xs, taps, g_tile, g_grid, da, da_pair, grid, acc,
                 send_r, send_c, send_k, x_r, x_c, x_k, z_r, z_c, z_k, d_r, d_c, d_k, gs_r, gs_c, gs_k, gl_r, gl_c, gl_k,
                 load_sems, pair_sems, near_sems, out_sems, send_sems, recv_sems, grants):
    bit, dev = place()
    w, h = lax.axis_index('w'), lax.axis_index('h')
    core = bit['c']
    x_tile = xs.at[0, pl.ds(0, PIX)]
    load_x = pltpu.make_async_copy(x_in, x_tile, load_sems.at[0])
    load_g = pltpu.make_async_copy(g_in, g_tile, load_sems.at[1])
    load_w = pltpu.make_async_copy(w_first, wbuf, load_sems.at[2])
    for load in (load_x, load_g, load_w):
        load.start()
    barrier = pltpu.get_barrier_semaphore()
    for axis in 'xyzc':
        pl.semaphore_signal(barrier, inc=1, device_id=dev[axis], device_id_type=MESH)
    for dw, dh in NEAR:
        pl.semaphore_signal(barrier, inc=1, device_id=((w + dw + 4) % 4, (h + dh + 4) % 4), device_id_type=MESH)
    sends = (send_r, send_c, send_k)
    x_border = Border(grid, 1, ROWS, COLS, sends, (x_r, x_c, x_k), near_sems.at[0], NEAR, NEAR)
    z_border = Border(grid, 0, ROWS, COLS, sends, (z_r, z_c, z_k), near_sems.at[1], ABOVE, BELOW)
    d_border = Border(grid, 1, ROWS, COLS, sends, (d_r, d_c, d_k), near_sems.at[2], NEAR, NEAR)
    g_border = Border(g_grid, 1, OUT_R, OUT_C, (gs_r, gs_c, gs_k), (gl_r, gl_c, gl_k), near_sems.at[3], BELOW, ABOVE)
    sems = (send_sems, recv_sems)
    down = Reducer(0, own_d, land_d, o_down, sems, grants, bit, dev)
    first = Reducer(1, own_f, land_f, o_first, sems, grants, bit, dev)

    def to_pair(src, dst, i):
        return pltpu.make_async_remote_copy(src_ref=src, dst_ref=dst, send_sem=pair_sems.at[0, i], recv_sem=pair_sems.at[1, i], device_id=dev['c'], device_id_type=MESH)

    load_x.wait()

    def place_row(r):
        for k in LANES:
            grid[k, r + 1, EDGE:EDGE + COLS, :] = x_tile[at(r * COLS, COLS), lane(k)].astype(F32)
    run(ROWS, place_row)
    pl.semaphore_wait(barrier, 12)
    x_border.start()
    load_g.wait()
    for r in range(OUT_R):
        for k in LANES:
            g_grid[k, r + 1, EDGE:EDGE + OUT_C, :] = g_tile[r, :, lane(k)].astype(F32)
    g_border.start()
    x_border.finish()
    spread(grid, xs)
    x_share = to_pair(xs.at[0], x_land, 0)
    x_share.start()
    load_w.wait()

    def pre_rows(i):
        for t, a, c in TAPS:
            rows = pl.ds(pl.multiple_of(c * LINES + i * BLOCK + a * COLS, COLS), BLOCK)
            accumulate(acc, BLOCK, dot(xs[0, rows, :], wbuf[t]), t == 0)
        for k in LANES:
            pre = acc[k].astype(BF16).astype(F32)
            acc[k] = pre
            act = gelu_tanh(pre).astype(BF16).astype(F32)
            for r in range(8):
                grid[k, 8 * i + r, EDGE:EDGE + COLS, :] = act[r * COLS:(r + 1) * COLS]
        for r in range(8):
            for cp in range(2):
                for k in LANES:
                    own_f[2 * (r % 2) + cp, pl.ds(pl.multiple_of((4 * i + r // 2) * OUT_C, 8), OUT_C), lane(k)] = acc[k, pl.ds(r * COLS + cp, OUT_C, stride=2), :]
    run(3, pre_rows)
    load_w2 = pltpu.make_async_copy(w_down, wbuf, load_sems.at[3])
    load_w2.start()
    z_border.start()

    g_border.finish()
    for di in range(2):
        for dj in range(2):
            for k in LANES:
                part = g_grid[k, di:di + OUT_R, EDGE - 1 + dj:EDGE - 1 + dj + OUT_C, :]
                xs[1, (2 * di + dj) * OPIX:(2 * di + dj + 1) * OPIX, lane(k)] = part.reshape(OPIX, 128).astype(BF16)
    g_share = to_pair(xs.at[1, pl.ds(G_AT, OPIX)], xs.at[1, pl.ds(G_PAIR_AT, OPIX)], 1)
    g_share.start()
    z_border.finish()

    def tap_rows(p):
        for t, a, c in TAPS:
            for k in LANES:
                cols = pl.ds(EDGE + c, OUT_C, stride=2)
                two = jnp.concatenate([grid[k, 4 * p + a, cols, :], grid[k, 4 * p + 2 + a, cols, :]], 0)
                taps[t, at(p * 2 * OUT_C, 2 * OUT_C), lane(k)] = two.astype(BF16)
    run(OUT_R // 2, tap_rows)
    tap_shares = [to_pair(taps.at[4 * (1 - core) + j], xs.at[1, pl.ds(TAP_PAIR_AT + j * OPIX, OPIX)], 2 + j) for j in range(5)]
    for share in tap_shares:
        share.start()

    def down_tap(j):
        res = dot_lhs_t(taps[4 * core + j], xs[1, G_AT:G_AT + OPIX, :])
        own_d[2 * j] = res[:HALF]
        own_d[2 * j + 1] = res[HALF:]
    run(5, down_tap)
    g_share.wait()
    for share in tap_shares:
        share.wait()

    def down_tap_pair(j):
        rows = pl.ds(pl.multiple_of(TAP_PAIR_AT + j * OPIX, 32), OPIX)
        res = dot_lhs_t(xs[1, rows, :], xs[1, G_PAIR_AT:G_PAIR_AT + OPIX, :])
        own_d[2 * j] += res[:HALF]
        own_d[2 * j + 1] += res[HALF:]
    run(5, down_tap_pair)
    down.begin()

    load_w2.wait()
    for rp in range(2):
        for cp in range(2):
            total = None
            for a in ((0, 2), (1,))[rp]:
                for c in ((0, 2), (1,))[cp]:
                    row = (2 * (1 - a // 2) + 1 - c // 2) * OPIX
                    part = dot_rhs_t(xs[1, row:row + OPIX, :], wbuf[3 * a + c])
                    total = part if total is None else total + part
            pre = own_f[2 * rp + cp, 0:OPIX, :]
            grad = jax.vjp(gelu_tanh, pre)[1](total)[0].astype(BF16).astype(F32)
            for i in range(OUT_R):
                for k in LANES:
                    grid[k, 2 * i + rp + 1, pl.ds(EDGE + cp, OUT_C, stride=2), :] = grad[i * OUT_C:(i + 1) * OUT_C, lane(k)]

    def pack(r):
        for k in LANES:
            da[at(r * COLS, COLS), lane(k)] = grid[k, r + 1, EDGE:EDGE + COLS, :].astype(BF16)
    run(ROWS, pack)
    da_share = to_pair(da, da_pair, 7)
    da_share.start()
    d_border.start()
    x_share.wait()
    pair_load = pltpu.make_async_copy(x_land, xs.at[1], load_sems.at[4])
    pair_load.start()

    for t in range(9):
        accumulate(acc, OPIX, dot(taps[t], wbuf[t]), t == 0)
    for k in LANES:
        taps[0, :, lane(k)] = acc[k, 0:OPIX, :].astype(BF16)
    y_copy = pltpu.make_async_copy(taps.at[0], y_out, out_sems.at[0])
    y_copy.start()
    load_w1 = pltpu.make_async_copy(w_first, wbuf, load_sems.at[5])
    load_w1.start()
    pair_load.wait()
    da_share.wait()

    def first_tap(j):
        t = 4 * core + j
        a, c = t // 3, t % 3
        rows = pl.ds(pl.multiple_of(c * LINES + a * COLS, COLS), PIX)
        res = dot_lhs_t(xs[0, rows, :], da[...]) + dot_lhs_t(xs[1, rows, :], da_pair[...])
        own_f[2 * j] = res[:HALF]
        own_f[2 * j + 1] = res[HALF:]
    run(4, first_tap)
    down.move(R1, (R2,), add=True)
    first_tap(4)
    first.begin()

    d_border.finish()
    spread(grid, xs)
    load_w1.wait()

    def image_rows(i):
        for t, a, c in TAPS:
            rows = pl.ds(pl.multiple_of((2 - c) * LINES + i * BLOCK + (2 - a) * COLS, COLS), BLOCK)
            accumulate(acc, BLOCK, dot_rhs_t(xs[0, rows, :], wbuf[t]), t == 0)
        for k in LANES:
            da_pair[at(i * BLOCK, BLOCK), lane(k)] = acc[k].astype(BF16)
    run(3, image_rows)
    dx_copy = pltpu.make_async_copy(da_pair, dx_out, out_sems.at[1])
    dx_copy.start()

    down.move(R2, (R3,), add=True)
    first.move(R1, (R2,), add=True)
    down.move(R3, (A1,), add=True)
    first.move(R2, (R3,), add=True)
    down.move(A1, (A2, A3A))
    first.move(R3, (A1,), add=True)
    down.move(A2, (A3B, DA))
    first.move(A1, (A2, A3A))
    down.move(A3A, (DB,))
    first.move(A2, (A3B, DA))
    down.move(A3B, (DC,))
    first.move(A3A, (DB,))
    first.move(A3B, (DC,))
    y_copy.wait()
    dx_copy.wait()
    down.finish()
    first.finish()


def block_call(image, grad_out, w_first, w_down):
    total = jax.ShapeDtypeStruct((9, HALF, C), F32)
    kept = pltpu.VMEM((10, HALF, C), F32)
    dma = pltpu.SemaphoreType.DMA
    edges = [pltpu.VMEM((2, COLS, C), F32), pltpu.VMEM((2, ROWS, C), F32), pltpu.VMEM((4, 8, C), F32)]
    small = [pltpu.VMEM((2, OUT_C, C), F32), pltpu.VMEM((2, OUT_R, C), F32), pltpu.VMEM((4, 8, C), F32)]
    return pl.pallas_call(
        block_kernel,
        out_shape=[jax.ShapeDtypeStruct((OPIX, C), BF16), jax.ShapeDtypeStruct((PIX, C), BF16), kept, kept, total, total,
                   jax.ShapeDtypeStruct((3 * LINES, C), BF16)],
        in_specs=[ANY] * 4, out_specs=[ANY] * 2 + [pl.BlockSpec(memory_space=pltpu.VMEM)] * 2 + [ANY] * 3,
        scratch_shapes=[pltpu.VMEM((9, 280, C), F32)] * 2
        + [pltpu.VMEM((9, C, C), BF16), pltpu.VMEM((2, 3 * LINES, C), BF16), pltpu.VMEM((9, OPIX, C), BF16)]
        + [pltpu.VMEM((OUT_R, OUT_C, C), BF16), pltpu.VMEM((5, OUT_R + 1, OUT_C + EDGE, 128), F32)]
        + [pltpu.VMEM((PIX, C), BF16)] * 2
        + [pltpu.VMEM((5, ROWS + 2, COLS + 2 * EDGE, 128), F32), pltpu.VMEM((5, BLOCK, 128), F32)]
        + edges * 4 + small * 2
        + [dma((6,)), dma((2, 8)), dma((4, 2, 8)), dma((2,)), dma((2, 3, 10)), dma((2, 3, 10)), pltpu.SemaphoreType.REGULAR((2, 3, 3))],
        compiler_params=pltpu.CompilerParams(collective_id=1, has_side_effects=True, vmem_limit_bytes=OWN_SPACE),
        cost_estimate=pl.CostEstimate(flops=2 * PIX * 90 * C * C, bytes_accessed=64 * MIB, transcendentals=0),
    )(image.reshape(PIX, C), grad_out, w_first, w_down)


def settle_kernel(y_in, dx_in, own_d, own_f, pair_d, pair_f, y_out, dx_out, down_out, first_out, y_buf, dx_buf, buf, load_sems, store_sems):
    core = lax.axis_index('h') % 2
    loads, stores = [], []
    for i, (src, via, dst) in enumerate(((y_in, y_buf, y_out), (dx_in, dx_buf, dx_out))):
        loads.append(pltpu.make_async_copy(src, via, load_sems.at[2, i]))
        stores.append(pltpu.make_async_copy(via, dst, store_sems.at[2, i]))
    kept = []
    for i, (own, pair, out) in enumerate(((own_d, pair_d, down_out), (own_f, pair_f, first_out))):
        kept.append(pltpu.make_async_copy(own.at[pl.ds(core, 9)], out.at[pl.ds(9 * core, 9)], store_sems.at[i, 9]))
        for part in range(9):
            loads.append(pltpu.make_async_copy(pair.at[part], buf.at[i, part], load_sems.at[i, part]))
            stores.append(pltpu.make_async_copy(buf.at[i, part], out.at[9 * (1 - core) + part], store_sems.at[i, part]))
    for copy in loads + kept:
        copy.start()
    for load, store in zip(loads, stores):
        load.wait()
        store.start()
    for copy in kept + stores:
        copy.wait()


def settle(*made):
    total = jax.ShapeDtypeStruct((18, HALF, C), F32)
    dma = pltpu.SemaphoreType.DMA
    return pl.pallas_call(
        settle_kernel, out_shape=[jax.ShapeDtypeStruct((OPIX, C), BF16), jax.ShapeDtypeStruct((PIX, C), BF16), total, total],
        in_specs=[pl.BlockSpec(memory_space=pltpu.HBM)] * 2 + [pl.BlockSpec(memory_space=pltpu.VMEM)] * 2 + [pl.BlockSpec(memory_space=pltpu.HBM)] * 2,
        out_specs=[ANY] * 4,
        scratch_shapes=[pltpu.VMEM((OPIX, C), BF16), pltpu.VMEM((PIX, C), BF16), pltpu.VMEM((2, 9, HALF, C), F32), dma((3, 9)), dma((3, 10))],
        compiler_params=pltpu.CompilerParams(vmem_limit_bytes=OWN_SPACE),
    )(*made[:2], *(pltpu.with_memory_space_constraint(own, pltpu.VMEM) for own in made[2:4]), *made[4:])


def solution(mesh):
    def block_step(image, w_first, w_down, grad_out):
        made = block_call(image[0], grad_out[0], w_first.reshape(9, C, C), w_down.reshape(9, C, C))
        block_out, grad_image, grad_w_down, grad_w_first = settle(*made[:6])
        return (block_out.reshape(1, OUT_R, OUT_C, C), grad_image.reshape(1, ROWS, COLS, C),
                grad_w_first.reshape(3, 3, C, C), grad_w_down.reshape(3, 3, C, C))

    img_spec = P(None, 'h', 'w', None)
    return jax.shard_map(block_step, mesh=mesh, in_specs=(img_spec, P(), P(), img_spec), out_specs=(img_spec, img_spec, P(), P()), check_vma=False)
```

time: 257 us -> 252 us (0.981)
  Pallas kernels: 255 us -> 251 us
    pallas_call x1, Pallas kernels: 20.7 us -> 17 us  [settle(): pl.pallas_call(settle_kernel, out_shape=[jax.ShapeDtypeStruct((OPIX, C),...]
where the time goes in v4:
time: 252 us
  Pallas kernels  251 us (100%)
    pallas_call x1, Pallas kernels, block_call(): pl.pallas_call(block_kernel, out_shape=[jax.ShapeDtypeStruct((OPIX, C), B...  234 us
    pallas_call x1, Pallas kernels, settle(): pl.pallas_call(settle_kernel, out_shape=[jax.ShapeDtypeStruct((OPIX, C),...  17 us

profile of v4, /device:TPU:0, one launch (start us, length us, event | category | flops | bytes accessed | tf_op | source)
XLA Modules:
  0.0 251.5 jit_solution(18037786857987741797)
XLA Ops:
  0.6 233.7 %shard_map.75 = (bf16[288,640]{1,0:T(8,128)(2,1)}, bf16[1152,640]{1,0:T(8,128)(2,1)}, f32[10,320,640]{2,1,0:T(8,128)S(1)}, f32[10,320,640]{2,1,0:T(8,128)S(1)}, ...) custom-call(bf16[1152,640]{1,0:T(8,128)(2,1)} %bitcast.12, ...), custom_call_target="tpu_custom_call" | custom-call | flops 84934656000 | bytes 67108864 | tf_op jit(solution)/shard_map/pallas_call | solution.py:410
  234.3 17.0 %shard_map.76 = (bf16[288,640]{1,0:T(8,128)(2,1)}, bf16[1152,640]{1,0:T(8,128)(2,1)}, f32[18,320,640]{2,1,0:T(8,128)}, f32[18,320,640]{2,1,0:T(8,128)}) custom-call(bf16[288,640]{1,0:T(8,128)(2,1)} %get-tuple-element.14.y_in, bf16[1152,640]{1,0:T(8,128)(2,1)} %get-tuple-element.15.dx_in, f32[10,320,640]{2,1,0:T(8,128)S(1)} %get-tuple-element.16.own_d, ...), custom_call_target="tpu_custom_call" | custom-call | tf_op jit(solution)/shard_map/pallas_call | solution.py:451

commit v5 on v4

--- a/solution.py
+++ b/solution.py
@@ -13,7 +13,7 @@
 PIX, OPIX = ROWS * COLS, OUT_R * OUT_C
 HALF = 320
 MIB = 2 ** 20
-OWN_SPACE = 50462720
+SCRATCH = 36000000
 ORDERS = (('x', 'y', 'z'), ('y', 'z', 'x'), ('z', 'x', 'y'))
 R1, R2, R3, A1, A2, A3A, A3B, DA, DB, DC = range(10)
 QUARTER = HALF // 2
@@ -42,6 +42,7 @@
 
 
 ANY = pl.BlockSpec(memory_space=pl.ANY)
+VM = pl.BlockSpec(memory_space=pltpu.VMEM)
 
 
 def place():
@@ -52,8 +53,8 @@
 
 
 class Reducer:
-    def __init__(self, index, own, land, out, sems, grants, bit, dev):
-        self.index, self.own, self.land, self.out, self.sems, self.grants, self.bit, self.dev = index, own, land, out, sems, grants, bit, dev
+    def __init__(self, index, own, pair, sems, grants, bit, dev):
+        self.index, self.own, self.pair, self.sems, self.grants, self.bit, self.dev = index, own, pair, sems, grants, bit, dev
 
     def starts(self, third):
         b = [self.bit[axis] for axis in ORDERS[third]]
@@ -73,14 +74,14 @@
         }[kind]
         rows = pl.ds(pl.multiple_of(src, 8), size)
         units = pl.ds(3 * third, 3)
-        source = self.own.at[pl.ds(self.bit['c'] + 3 * third, 3), rows]
+        source = self.own.at[units, rows]
         send, recv = (s.at[self.index, third, kind] for s in self.sems)
         if kind <= R3:
-            target = self.land.at[units, pl.ds(LAND_AT[kind], size)]
+            target = self.pair.at[units, pl.ds(LAND_AT[kind], size)]
         elif kind <= A3B:
             target = source
         else:
-            target = self.out.at[units, rows]
+            target = self.pair.at[units, rows]
         return pltpu.make_async_remote_copy(src_ref=source, dst_ref=target, send_sem=send, recv_sem=recv, device_id=self.dev[axis], device_id_type=MESH)
 
     def add(self, third, kind):
@@ -91,7 +92,7 @@
         def body(j):
             unit, row = 3 * third + j // steps, (j % steps) * LEAST
             rows = pl.ds(pl.multiple_of(keep + row, 8), LEAST)
-            self.own[self.bit['c'] + unit, rows, :] += self.land[unit, pl.ds(pl.multiple_of(LAND_AT[kind] + row, 8), LEAST), :]
+            self.own[unit, rows, :] += self.pair[unit, pl.ds(pl.multiple_of(LAND_AT[kind] + row, 8), LEAST), :]
         run(3 * steps, body)
 
     def begin(self):
@@ -104,7 +105,11 @@
             if add:
                 pl.semaphore_signal(self.grants.at[self.index, third, wait_for], inc=1, device_id=self.dev[ORDERS[third][wait_for]], device_id_type=MESH)
                 self.add(third, wait_for)
+            if wait_for == R3 and third == THIRDS[-1]:
+                pl.semaphore_signal(self.grants.at[self.index, 0, 3], inc=1, device_id=self.dev['c'], device_id_type=MESH)
             for kind in then:
+                if kind == DA and third == 0:
+                    pl.semaphore_wait(self.grants.at[self.index, 0, 3], 1)
                 if kind in (A1, A2, A3A):
                     pl.semaphore_wait(self.grants.at[self.index, third, {A1: R3, A2: R2, A3A: R1}[kind]], 1)
                 self.copy(third, kind).start()
@@ -116,7 +121,8 @@
 
 EDGE = 8
 LINES = (ROWS + 2) * COLS
-BLOCK = 8 * COLS
+BLOCK_ROWS = 6
+BLOCK = BLOCK_ROWS * COLS
 NEAR = [(dw, dh) for dw in (-1, 0, 1) for dh in (-1, 0, 1) if (dw, dh) != (0, 0)]
 ABOVE = [(-1, -1), (-1, 0), (0, -1)]
 BELOW = [(1, 1), (1, 0), (0, 1)]
@@ -213,8 +219,8 @@
         acc[k, 0:rows, :] = piece if first else acc[k, 0:rows, :] + piece
 
 
-def block_kernel(x_in, g_in, w_first, w_down, y_out, dx_out, own_d, own_f, o_down, o_first, x_land,
-                 land_d, land_f, wbuf, xs, taps, g_tile, g_grid, da, da_pair, grid, acc,
+def block_kernel(x_in, g_in, w_first, w_down, y_out, da_pair, own_d, own_f, other_d, other_f, x_land,
+                 wbuf, xs, taps, g_tile, g_grid, da, grid, acc,
                  send_r, send_c, send_k, x_r, x_c, x_k, z_r, z_c, z_k, d_r, d_c, d_k, gs_r, gs_c, gs_k, gl_r, gl_c, gl_k,
                  load_sems, pair_sems, near_sems, out_sems, send_sems, recv_sems, grants):
     bit, dev = place()
@@ -237,11 +243,20 @@
     d_border = Border(grid, 1, ROWS, COLS, sends, (d_r, d_c, d_k), near_sems.at[2], NEAR, NEAR)
     g_border = Border(g_grid, 1, OUT_R, OUT_C, (gs_r, gs_c, gs_k), (gl_r, gl_c, gl_k), near_sems.at[3], BELOW, ABOVE)
     sems = (send_sems, recv_sems)
-    down = Reducer(0, own_d, land_d, o_down, sems, grants, bit, dev)
-    first = Reducer(1, own_f, land_f, o_first, sems, grants, bit, dev)
+    down = Reducer(0, own_d, other_d, sems, grants, bit, dev)
+    first = Reducer(1, own_f, other_f, sems, grants, bit, dev)
 
     def to_pair(src, dst, i):
         return pltpu.make_async_remote_copy(src_ref=src, dst_ref=dst, send_sem=pair_sems.at[0, i], recv_sem=pair_sems.at[1, i], device_id=dev['c'], device_id_type=MESH)
+
+    def put(own, j, res, more):
+        for side in range(2):
+            unit = 2 * j + side - core
+            part = res[side * HALF:(side + 1) * HALF]
+
+            @pl.when(jnp.logical_and(unit >= 0, unit < 9))
+            def _():
+                own[unit] = own[unit] + part if more else part
 
     load_x.wait()
 
@@ -270,13 +285,13 @@
             pre = acc[k].astype(BF16).astype(F32)
             acc[k] = pre
             act = gelu_tanh(pre).astype(BF16).astype(F32)
-            for r in range(8):
-                grid[k, 8 * i + r, EDGE:EDGE + COLS, :] = act[r * COLS:(r + 1) * COLS]
-        for r in range(8):
+            for r in range(BLOCK_ROWS):
+                grid[k, BLOCK_ROWS * i + r, EDGE:EDGE + COLS, :] = act[r * COLS:(r + 1) * COLS]
+        for r in range(BLOCK_ROWS):
             for cp in range(2):
                 for k in LANES:
-                    own_f[2 * (r % 2) + cp, pl.ds(pl.multiple_of((4 * i + r // 2) * OUT_C, 8), OUT_C), lane(k)] = acc[k, pl.ds(r * COLS + cp, OUT_C, stride=2), :]
-    run(3, pre_rows)
+                    own_f[2 * (r % 2) + cp, pl.ds(pl.multiple_of((BLOCK_ROWS // 2 * i + r // 2) * OUT_C, 8), OUT_C), lane(k)] = acc[k, pl.ds(r * COLS + cp, OUT_C, stride=2), :]
+    run(ROWS // BLOCK_ROWS, pre_rows)
     load_w2 = pltpu.make_async_copy(w_down, wbuf, load_sems.at[3])
     load_w2.start()
     z_border.start()
@@ -304,8 +319,7 @@
 
     def down_tap(j):
         res = dot_lhs_t(taps[4 * core + j], xs[1, G_AT:G_AT + OPIX, :])
-        own_d[2 * j] = res[:HALF]
-        own_d[2 * j + 1] = res[HALF:]
+        put(own_d, j, res, False)
     run(5, down_tap)
     g_share.wait()
     for share in tap_shares:
@@ -314,8 +328,7 @@
     def down_tap_pair(j):
         rows = pl.ds(pl.multiple_of(TAP_PAIR_AT + j * OPIX, 32), OPIX)
         res = dot_lhs_t(xs[1, rows, :], xs[1, G_PAIR_AT:G_PAIR_AT + OPIX, :])
-        own_d[2 * j] += res[:HALF]
-        own_d[2 * j + 1] += res[HALF:]
+        put(own_d, j, res, True)
     run(5, down_tap_pair)
     down.begin()
 
@@ -361,8 +374,7 @@
         a, c = t // 3, t % 3
         rows = pl.ds(pl.multiple_of(c * LINES + a * COLS, COLS), PIX)
         res = dot_lhs_t(xs[0, rows, :], da[...]) + dot_lhs_t(xs[1, rows, :], da_pair[...])
-        own_f[2 * j] = res[:HALF]
-        own_f[2 * j + 1] = res[HALF:]
+        put(own_f, j, res, False)
     run(4, first_tap)
     down.move(R1, (R2,), add=True)
     first_tap(4)
@@ -378,9 +390,7 @@
             accumulate(acc, BLOCK, dot_rhs_t(xs[0, rows, :], wbuf[t]), t == 0)
         for k in LANES:
             da_pair[at(i * BLOCK, BLOCK), lane(k)] = acc[k].astype(BF16)
-    run(3, image_rows)
-    dx_copy = pltpu.make_async_copy(da_pair, dx_out, out_sems.at[1])
-    dx_copy.start()
+    run(ROWS // BLOCK_ROWS, image_rows)
 
     down.move(R2, (R3,), add=True)
     first.move(R1, (R2,), add=True)
@@ -396,52 +406,47 @@
     first.move(A3A, (DB,))
     first.move(A3B, (DC,))
     y_copy.wait()
-    dx_copy.wait()
     down.finish()
     first.finish()
 
 
 def block_call(image, grad_out, w_first, w_down):
-    total = jax.ShapeDtypeStruct((9, HALF, C), F32)
-    kept = pltpu.VMEM((10, HALF, C), F32)
+    kept = pltpu.VMEM((9, HALF, C), F32)
     dma = pltpu.SemaphoreType.DMA
     edges = [pltpu.VMEM((2, COLS, C), F32), pltpu.VMEM((2, ROWS, C), F32), pltpu.VMEM((4, 8, C), F32)]
     small = [pltpu.VMEM((2, OUT_C, C), F32), pltpu.VMEM((2, OUT_R, C), F32), pltpu.VMEM((4, 8, C), F32)]
     return pl.pallas_call(
         block_kernel,
-        out_shape=[jax.ShapeDtypeStruct((OPIX, C), BF16), jax.ShapeDtypeStruct((PIX, C), BF16), kept, kept, total, total,
+        out_shape=[jax.ShapeDtypeStruct((OPIX, C), BF16), pltpu.VMEM((PIX, C), BF16), kept, kept, kept, kept,
                    jax.ShapeDtypeStruct((3 * LINES, C), BF16)],
-        in_specs=[ANY] * 4, out_specs=[ANY] * 2 + [pl.BlockSpec(memory_space=pltpu.VMEM)] * 2 + [ANY] * 3,
-        scratch_shapes=[pltpu.VMEM((9, 280, C), F32)] * 2
-        + [pltpu.VMEM((9, C, C), BF16), pltpu.VMEM((2, 3 * LINES, C), BF16), pltpu.VMEM((9, OPIX, C), BF16)]
+        in_specs=[ANY] * 4, out_specs=[ANY] + [VM] * 5 + [ANY],
+        scratch_shapes=[pltpu.VMEM((9, C, C), BF16), pltpu.VMEM((2, 3 * LINES, C), BF16), pltpu.VMEM((9, OPIX, C), BF16)]
         + [pltpu.VMEM((OUT_R, OUT_C, C), BF16), pltpu.VMEM((5, OUT_R + 1, OUT_C + EDGE, 128), F32)]
-        + [pltpu.VMEM((PIX, C), BF16)] * 2
+        + [pltpu.VMEM((PIX, C), BF16)]
         + [pltpu.VMEM((5, ROWS + 2, COLS + 2 * EDGE, 128), F32), pltpu.VMEM((5, BLOCK, 128), F32)]
         + edges * 4 + small * 2
-        + [dma((6,)), dma((2, 8)), dma((4, 2, 8)), dma((2,)), dma((2, 3, 10)), dma((2, 3, 10)), pltpu.SemaphoreType.REGULAR((2, 3, 3))],
-        compiler_params=pltpu.CompilerParams(collective_id=1, has_side_effects=True, vmem_limit_bytes=OWN_SPACE),
+        + [dma((6,)), dma((2, 8)), dma((4, 2, 8)), dma((2,)), dma((2, 3, 10)), dma((2, 3, 10)), pltpu.SemaphoreType.REGULAR((2, 3, 4))],
+        compiler_params=pltpu.CompilerParams(collective_id=1, has_side_effects=True, vmem_limit_bytes=SCRATCH),
         cost_estimate=pl.CostEstimate(flops=2 * PIX * 90 * C * C, bytes_accessed=64 * MIB, transcendentals=0),
     )(image.reshape(PIX, C), grad_out, w_first, w_down)
 
 
-def settle_kernel(y_in, dx_in, own_d, own_f, pair_d, pair_f, y_out, dx_out, down_out, first_out, y_buf, dx_buf, buf, load_sems, store_sems):
+def settle_kernel(y_in, dx_in, own_d, own_f, other_d, other_f, y_out, dx_out, down_out, first_out, y_buf, load_sem, sems):
     core = lax.axis_index('h') % 2
-    loads, stores = [], []
-    for i, (src, via, dst) in enumerate(((y_in, y_buf, y_out), (dx_in, dx_buf, dx_out))):
-        loads.append(pltpu.make_async_copy(src, via, load_sems.at[2, i]))
-        stores.append(pltpu.make_async_copy(via, dst, store_sems.at[2, i]))
-    kept = []
-    for i, (own, pair, out) in enumerate(((own_d, pair_d, down_out), (own_f, pair_f, first_out))):
-        kept.append(pltpu.make_async_copy(own.at[pl.ds(core, 9)], out.at[pl.ds(9 * core, 9)], store_sems.at[i, 9]))
-        for part in range(9):
-            loads.append(pltpu.make_async_copy(pair.at[part], buf.at[i, part], load_sems.at[i, part]))
-            stores.append(pltpu.make_async_copy(buf.at[i, part], out.at[9 * (1 - core) + part], store_sems.at[i, part]))
-    for copy in loads + kept:
+    load = pltpu.make_async_copy(y_in, y_buf, load_sem)
+    load.start()
+    pieces = [(dx_in, dx_out)]
+    for own, other, out in ((own_d, other_d, down_out), (own_f, other_f, first_out)):
+        for part in THIRDS:
+            for side, src in ((core, own), (1 - core, other)):
+                pieces.append((src.at[pl.ds(3 * part, 3)], out.at[pl.ds(9 * side + 3 * part, 3)]))
+    copies = [pltpu.make_async_copy(src, dst, sems.at[i]) for i, (src, dst) in enumerate(pieces)]
+    for copy in copies:
         copy.start()
-    for load, store in zip(loads, stores):
-        load.wait()
-        store.start()
-    for copy in kept + stores:
+    load.wait()
+    last = pltpu.make_async_copy(y_buf, y_out, sems.at[len(copies)])
+    last.start()
+    for copy in copies + [last]:
         copy.wait()
 
 
@@ -450,11 +455,10 @@
     dma = pltpu.SemaphoreType.DMA
     return pl.pallas_call(
         settle_kernel, out_shape=[jax.ShapeDtypeStruct((OPIX, C), BF16), jax.ShapeDtypeStruct((PIX, C), BF16), total, total],
-        in_specs=[pl.BlockSpec(memory_space=pltpu.HBM)] * 2 + [pl.BlockSpec(memory_space=pltpu.VMEM)] * 2 + [pl.BlockSpec(memory_space=pltpu.HBM)] * 2,
-        out_specs=[ANY] * 4,
-        scratch_shapes=[pltpu.VMEM((OPIX, C), BF16), pltpu.VMEM((PIX, C), BF16), pltpu.VMEM((2, 9, HALF, C), F32), dma((3, 9)), dma((3, 10))],
-        compiler_params=pltpu.CompilerParams(vmem_limit_bytes=OWN_SPACE),
-    )(*made[:2], *(pltpu.with_memory_space_constraint(own, pltpu.VMEM) for own in made[2:4]), *made[4:])
+        in_specs=[pl.BlockSpec(memory_space=pltpu.HBM)] + [VM] * 5, out_specs=[ANY] * 4,
+        scratch_shapes=[pltpu.VMEM((OPIX, C), BF16), dma, dma((14,))],
+        compiler_params=pltpu.CompilerParams(vmem_limit_bytes=SCRATCH),
+    )(made[0], *(pltpu.with_memory_space_constraint(one, pltpu.VMEM) for one in made[1:]))
 
 
 def solution(mesh):

time: 252 us -> 246 us (0.976)
  Pallas kernels: 251 us -> 245 us
    pallas_call x1, Pallas kernels: 17 us -> 10.4 us  [settle(): pl.pallas_call(settle_kernel, out_shape=[jax.ShapeDtypeStruct((OPIX, C),...]
where the time goes in v5:
time: 246 us
  Pallas kernels  245 us (100%)
    pallas_call x1, Pallas kernels, block_call(): pl.pallas_call(block_kernel, out_shape=[jax.ShapeDtypeStruct((OPIX, C), B...  235 us
    pallas_call x1, Pallas kernels, settle(): pl.pallas_call(settle_kernel, out_shape=[jax.ShapeDtypeStruct((OPIX, C),...  10.4 us

profile of v5, /device:TPU:0, one launch (start us, length us, event | category | flops | bytes accessed | tf_op | source)
XLA Modules:
  0.0 246.0 jit_solution(2735363126662780179)
XLA Ops:
  0.6 234.8 %shard_map.75 = (bf16[288,640]{1,0:T(8,128)(2,1)}, bf16[1152,640]{1,0:T(8,128)(2,1)S(1)}, f32[9,320,640]{2,1,0:T(8,128)S(1)}, f32[9,320,640]{2,1,0:T(8,128)S(1)}...) custom-call(bf16[1152,640]{1,0:T(8,128)(2,1)} %bitcast.12, ...), custom_call_target="tpu_custom_call" | custom-call | flops 84934656000 | bytes 67108864 | tf_op jit(solution)/shard_map/pallas_call | solution.py:418
  235.5 10.4 %shard_map.76 = (bf16[288,640]{1,0:T(8,128)(2,1)}, bf16[1152,640]{1,0:T(8,128)(2,1)}, f32[18,320,640]{2,1,0:T(8,128)}, f32[18,320,640]{2,1,0:T(8,128)}) custom-call(bf16[288,640]{1,0:T(8,128)(2,1)} %get-tuple-element.14.y_in, bf16[1152,640]{1,0:T(8,128)(2,1)S(1)} %get-tuple-element.15.dx_in, f32[9,320,640]{2,1,0:T(8,128)S(1)} %get-tuple-element.16.own_d, ...), custom_call_target="tpu_custom_call" | custom-call | tf_op jit(solution)/shard_map/pallas_call | solution.py:456

commit v6 on v5

--- a/solution.py
+++ b/solution.py
@@ -146,63 +146,75 @@
 
 
 class Border:
-    def __init__(self, grid, row0, rows, cols, send, land, sems, send_to, take_from):
+    def __init__(self, grid, row0, rows, cols, send, land, sems, send_to, take_from, row_sources=None):
         self.grid, self.row0, self.rows, self.cols, self.sends, self.lands = grid, row0, rows, cols, send, land
-        self.sems, self.send_to, self.take_from = sems, send_to, take_from
+        self.sems, self.send_to, self.take_from, self.row_sources = sems, send_to, take_from, row_sources
         self.w, self.h = lax.axis_index('w'), lax.axis_index('h')
 
     def edge(self, step, first, size, outside):
         return {-1: first - outside, 1: first + size - 1 + outside}[step]
 
-    def copies(self):
-        found = []
-        for dw, dh in self.send_to:
-            i = NEAR.index((dw, dh))
-            if dw == 0:
-                src, dst = self.sends[0].at[(dh + 1) // 2], self.lands[0].at[(1 - dh) // 2]
-            elif dh == 0:
-                src, dst = self.sends[1].at[(dw + 1) // 2], self.lands[1].at[(1 - dw) // 2]
-            else:
-                src = self.sends[2].at[2 * ((dh + 1) // 2) + (dw + 1) // 2]
-                dst = self.lands[2].at[2 * ((1 - dh) // 2) + (1 - dw) // 2]
-            peer = ((self.w + dw + 4) % 4, (self.h + dh + 4) % 4)
-            found.append(pltpu.make_async_remote_copy(src_ref=src, dst_ref=dst, send_sem=self.sems.at[0, i], recv_sem=self.sems.at[1, i], device_id=peer, device_id_type=MESH))
-        return found
-
-    def start(self):
+    def inside(self, dw, dh):
+        w, h = self.w + dw, self.h + dh
+        return jnp.logical_and(jnp.logical_and(w >= 0, w < 4), jnp.logical_and(h >= 0, h < 4))
+
+    def copy(self, dw, dh):
+        i, up, side = NEAR.index((dw, dh)), (dh + 1) // 2, (dw + 1) // 2
+        if dw == 0:
+            src = self.row_sources[up] if self.row_sources else self.sends[0].at[up]
+            dst = self.lands[0].at[1 - up]
+        elif dh == 0:
+            src, dst = self.sends[1].at[side], self.lands[1].at[1 - side]
+        else:
+            src, dst = self.sends[2].at[2 * up + side], self.lands[2].at[2 * (1 - up) + 1 - side]
+        peer = ((self.w + dw + 4) % 4, (self.h + dh + 4) % 4)
+        return pltpu.make_async_remote_copy(src_ref=src, dst_ref=dst, send_sem=self.sems.at[0, i], recv_sem=self.sems.at[1, i], device_id=peer, device_id_type=MESH)
+
+    def start(self, straight):
         grid, row0, rows, cols = self.grid, self.row0, self.rows, self.cols
         for dw, dh in self.send_to:
+            if (dw == 0) != straight:
+                continue
+            up, side = (dh + 1) // 2, (dw + 1) // 2
             r = None if dh == 0 else self.edge(dh, row0, rows, 0)
             c = None if dw == 0 else self.edge(dw, EDGE, cols, 0)
             for k in LANES:
                 if dw == 0:
-                    self.sends[0][(dh + 1) // 2, :, lane(k)] = grid[k, r, EDGE:EDGE + cols, :]
+                    if not self.row_sources:
+                        self.sends[0][up, :, lane(k)] = grid[k, r, EDGE:EDGE + cols, :].astype(self.sends[0].dtype)
                 elif dh == 0:
                     for row in range(rows):
-                        self.sends[1][(dw + 1) // 2, row:row + 1, lane(k)] = grid[k, row0 + row, c:c + 1, :]
+                        self.sends[1][side, row:row + 1, lane(k)] = grid[k, row0 + row, c:c + 1, :]
                 else:
-                    self.sends[2][2 * ((dh + 1) // 2) + (dw + 1) // 2, :, lane(k)] = jnp.broadcast_to(grid[k, r, c:c + 1, :], (8, 128))
-        for copy in self.copies():
-            copy.start()
+                    self.sends[2][2 * up + side, :, lane(k)] = jnp.broadcast_to(grid[k, r, c:c + 1, :], (8, 128))
+
+            @pl.when(self.inside(dw, dh))
+            def _():
+                self.copy(dw, dh).start()
 
     def finish(self):
         grid, row0, rows, cols = self.grid, self.row0, self.rows, self.cols
-        for copy in self.copies():
-            copy.wait()
+        for dw, dh in self.send_to:
+            @pl.when(self.inside(dw, dh))
+            def _():
+                self.copy(dw, dh).wait_send()
+
+            @pl.when(self.inside(-dw, -dh))
+            def _():
+                self.copy(dw, dh).wait_recv()
         for dw, dh in self.take_from:
+            up, side = (dh + 1) // 2, (dw + 1) // 2
             r = None if dh == 0 else self.edge(dh, row0, rows, 1)
             c = None if dw == 0 else self.edge(dw, EDGE, cols, 1)
-            out_w = {-1: self.w == 0, 0: False, 1: self.w == 3}[dw]
-            out_h = {-1: self.h == 0, 0: False, 1: self.h == 3}[dh]
+            out = jnp.logical_not(self.inside(dw, dh))
             for k in LANES:
                 if dw == 0:
-                    grid[k, r, EDGE:EDGE + cols, :] = clear_of(out_h, self.lands[0][(dh + 1) // 2, :, lane(k)])
+                    grid[k, r, EDGE:EDGE + cols, :] = clear_of(out, self.lands[0][up, :, lane(k)].astype(F32))
                 elif dh == 0:
                     for row in range(rows):
-                        grid[k, row0 + row, c:c + 1, :] = clear_of(out_w, self.lands[1][(dw + 1) // 2, row:row + 1, lane(k)])
+                        grid[k, row0 + row, c:c + 1, :] = clear_of(out, self.lands[1][side, row:row + 1, lane(k)])
                 else:
-                    out = jnp.logical_or(out_w, out_h)
-                    grid[k, r, c:c + 1, :] = clear_of(out, self.lands[2][2 * ((dh + 1) // 2) + (dw + 1) // 2, 0:1, lane(k)])
+                    grid[k, r, c:c + 1, :] = clear_of(out, self.lands[2][2 * up + side, 0:1, lane(k)])
 
 
 def spread(grid, xs):
@@ -238,7 +250,8 @@
     for dw, dh in NEAR:
         pl.semaphore_signal(barrier, inc=1, device_id=((w + dw + 4) % 4, (h + dh + 4) % 4), device_id_type=MESH)
     sends = (send_r, send_c, send_k)
-    x_border = Border(grid, 1, ROWS, COLS, sends, (x_r, x_c, x_k), near_sems.at[0], NEAR, NEAR)
+    x_border = Border(grid, 1, ROWS, COLS, sends, (x_r, x_c, x_k), near_sems.at[0], NEAR, NEAR,
+                      [x_tile.at[pl.ds(0, COLS)], x_tile.at[pl.ds(PIX - COLS, COLS)]])
     z_border = Border(grid, 0, ROWS, COLS, sends, (z_r, z_c, z_k), near_sems.at[1], ABOVE, BELOW)
     d_border = Border(grid, 1, ROWS, COLS, sends, (d_r, d_c, d_k), near_sems.at[2], NEAR, NEAR)
     g_border = Border(g_grid, 1, OUT_R, OUT_C, (gs_r, gs_c, gs_k), (gl_r, gl_c, gl_k), near_sems.at[3], BELOW, ABOVE)
@@ -259,18 +272,20 @@
                 own[unit] = own[unit] + part if more else part
 
     load_x.wait()
+    pl.semaphore_wait(barrier, 12)
+    x_border.start(True)
 
     def place_row(r):
         for k in LANES:
             grid[k, r + 1, EDGE:EDGE + COLS, :] = x_tile[at(r * COLS, COLS), lane(k)].astype(F32)
     run(ROWS, place_row)
-    pl.semaphore_wait(barrier, 12)
-    x_border.start()
+    x_border.start(False)
     load_g.wait()
     for r in range(OUT_R):
         for k in LANES:
             g_grid[k, r + 1, EDGE:EDGE + OUT_C, :] = g_tile[r, :, lane(k)].astype(F32)
-    g_border.start()
+    g_border.start(True)
+    g_border.start(False)
     x_border.finish()
     spread(grid, xs)
     x_share = to_pair(xs.at[0], x_land, 0)
@@ -294,7 +309,8 @@
     run(ROWS // BLOCK_ROWS, pre_rows)
     load_w2 = pltpu.make_async_copy(w_down, wbuf, load_sems.at[3])
     load_w2.start()
-    z_border.start()
+    z_border.start(True)
+    z_border.start(False)
 
     g_border.finish()
     for di in range(2):
@@ -353,7 +369,8 @@
     run(ROWS, pack)
     da_share = to_pair(da, da_pair, 7)
     da_share.start()
-    d_border.start()
+    d_border.start(True)
+    d_border.start(False)
     x_share.wait()
     pair_load = pltpu.make_async_copy(x_land, xs.at[1], load_sems.at[4])
     pair_load.start()
@@ -413,7 +430,7 @@
 def block_call(image, grad_out, w_first, w_down):
     kept = pltpu.VMEM((9, HALF, C), F32)
     dma = pltpu.SemaphoreType.DMA
-    edges = [pltpu.VMEM((2, COLS, C), F32), pltpu.VMEM((2, ROWS, C), F32), pltpu.VMEM((4, 8, C), F32)]
+    edges = [pltpu.VMEM((2, COLS, C), BF16), pltpu.VMEM((2, ROWS, C), F32), pltpu.VMEM((4, 8, C), F32)]
     small = [pltpu.VMEM((2, OUT_C, C), F32), pltpu.VMEM((2, OUT_R, C), F32), pltpu.VMEM((4, 8, C), F32)]
     return pl.pallas_call(
         block_kernel,

time: 246 us -> 245 us (level)
  no operation moved by 1% of the time
where the time goes in v6:
time: 245 us; the launch traced here: 244 us
  Pallas kernels  244 us (100%)
    pallas_call x1, Pallas kernels, block_call(): pl.pallas_call(block_kernel, out_shape=[jax.ShapeDtypeStruct((OPIX, C), B...  233 us
    pallas_call x1, Pallas kernels, settle(): pl.pallas_call(settle_kernel, out_shape=[jax.ShapeDtypeStruct((OPIX, C),...  10.4 us

profile of v6, /device:TPU:0, one launch (start us, length us, event | category | flops | bytes accessed | tf_op | source)
XLA Modules:
  0.0 244.4 jit_solution(6239881827359631829)
XLA Ops:
  0.6 233.2 %shard_map.75 = (bf16[288,640]{1,0:T(8,128)(2,1)}, bf16[1152,640]{1,0:T(8,128)(2,1)S(1)}, f32[9,320,640]{2,1,0:T(8,128)S(1)}, f32[9,320,640]{2,1,0:T(8,128)S(1)}...) custom-call(bf16[1152,640]{1,0:T(8,128)(2,1)} %bitcast.12, ...), custom_call_target="tpu_custom_call" | custom-call | flops 84934656000 | bytes 67108864 | tf_op jit(solution)/shard_map/pallas_call | solution.py:435
  233.9 10.4 %shard_map.76 = (bf16[288,640]{1,0:T(8,128)(2,1)}, bf16[1152,640]{1,0:T(8,128)(2,1)}, f32[18,320,640]{2,1,0:T(8,128)}, f32[18,320,640]{2,1,0:T(8,128)}) custom-call(bf16[288,640]{1,0:T(8,128)(2,1)} %get-tuple-element.14.y_in, bf16[1152,640]{1,0:T(8,128)(2,1)S(1)} %get-tuple-element.15.dx_in, f32[9,320,640]{2,1,0:T(8,128)S(1)} %get-tuple-element.16.own_d, ...), custom_call_target="tpu_custom_call" | custom-call | tf_op jit(solution)/shard_map/pallas_call | solution.py:473

commit v7 on v6

--- a/solution.py
+++ b/solution.py
@@ -120,6 +120,7 @@
 
 
 EDGE = 8
+ALL_PARTS = ROW, COLUMN, CORNER = range(3)
 LINES = (ROWS + 2) * COLS
 BLOCK_ROWS = 6
 BLOCK = BLOCK_ROWS * COLS
@@ -170,11 +171,12 @@
         peer = ((self.w + dw + 4) % 4, (self.h + dh + 4) % 4)
         return pltpu.make_async_remote_copy(src_ref=src, dst_ref=dst, send_sem=self.sems.at[0, i], recv_sem=self.sems.at[1, i], device_id=peer, device_id_type=MESH)
 
-    def start(self, straight):
+    def chosen(self, ways, parts):
+        return [(dw, dh) for dw, dh in ways if (ROW if dw == 0 else COLUMN if dh == 0 else CORNER) in parts]
+
+    def start(self, *parts):
         grid, row0, rows, cols = self.grid, self.row0, self.rows, self.cols
-        for dw, dh in self.send_to:
-            if (dw == 0) != straight:
-                continue
+        for dw, dh in self.chosen(self.send_to, parts):
             up, side = (dh + 1) // 2, (dw + 1) // 2
             r = None if dh == 0 else self.edge(dh, row0, rows, 0)
             c = None if dw == 0 else self.edge(dw, EDGE, cols, 0)
@@ -192,9 +194,9 @@
             def _():
                 self.copy(dw, dh).start()
 
-    def finish(self):
+    def finish(self, *parts):
         grid, row0, rows, cols = self.grid, self.row0, self.rows, self.cols
-        for dw, dh in self.send_to:
+        for dw, dh in self.chosen(self.send_to, parts):
             @pl.when(self.inside(dw, dh))
             def _():
                 self.copy(dw, dh).wait_send()
@@ -202,7 +204,7 @@
             @pl.when(self.inside(-dw, -dh))
             def _():
                 self.copy(dw, dh).wait_recv()
-        for dw, dh in self.take_from:
+        for dw, dh in self.chosen(self.take_from, parts):
             up, side = (dh + 1) // 2, (dw + 1) // 2
             r = None if dh == 0 else self.edge(dh, row0, rows, 1)
             c = None if dw == 0 else self.edge(dw, EDGE, cols, 1)
@@ -273,20 +275,19 @@
 
     load_x.wait()
     pl.semaphore_wait(barrier, 12)
-    x_border.start(True)
+    x_border.start(ROW)
 
     def place_row(r):
         for k in LANES:
             grid[k, r + 1, EDGE:EDGE + COLS, :] = x_tile[at(r * COLS, COLS), lane(k)].astype(F32)
     run(ROWS, place_row)
-    x_border.start(False)
+    x_border.start(COLUMN, CORNER)
     load_g.wait()
     for r in range(OUT_R):
         for k in LANES:
             g_grid[k, r + 1, EDGE:EDGE + OUT_C, :] = g_tile[r, :, lane(k)].astype(F32)
-    g_border.start(True)
-    g_border.start(False)
-    x_border.finish()
+    g_border.start(*ALL_PARTS)
+    x_border.finish(*ALL_PARTS)
     spread(grid, xs)
     x_share = to_pair(xs.at[0], x_land, 0)
     x_share.start()
@@ -306,13 +307,14 @@
             for cp in range(2):
                 for k in LANES:
                     own_f[2 * (r % 2) + cp, pl.ds(pl.multiple_of((BLOCK_ROWS // 2 * i + r // 2) * OUT_C, 8), OUT_C), lane(k)] = acc[k, pl.ds(r * COLS + cp, OUT_C, stride=2), :]
-    run(ROWS // BLOCK_ROWS, pre_rows)
+    pre_rows(0)
+    z_border.start(ROW, CORNER)
+    run(ROWS // BLOCK_ROWS - 1, lambda i: pre_rows(i + 1))
+    z_border.start(COLUMN)
     load_w2 = pltpu.make_async_copy(w_down, wbuf, load_sems.at[3])
     load_w2.start()
-    z_border.start(True)
-    z_border.start(False)
-
-    g_border.finish()
+
+    g_border.finish(*ALL_PARTS)
     for di in range(2):
         for dj in range(2):
             for k in LANES:
@@ -320,23 +322,38 @@
                 xs[1, (2 * di + dj) * OPIX:(2 * di + dj + 1) * OPIX, lane(k)] = part.reshape(OPIX, 128).astype(BF16)
     g_share = to_pair(xs.at[1, pl.ds(G_AT, OPIX)], xs.at[1, pl.ds(G_PAIR_AT, OPIX)], 1)
     g_share.start()
-    z_border.finish()
-
-    def tap_rows(p):
+
+    def tap_rows(p, columns):
         for t, a, c in TAPS:
-            for k in LANES:
-                cols = pl.ds(EDGE + c, OUT_C, stride=2)
-                two = jnp.concatenate([grid[k, 4 * p + a, cols, :], grid[k, 4 * p + 2 + a, cols, :]], 0)
-                taps[t, at(p * 2 * OUT_C, 2 * OUT_C), lane(k)] = two.astype(BF16)
-    run(OUT_R // 2, tap_rows)
-    tap_shares = [to_pair(taps.at[4 * (1 - core) + j], xs.at[1, pl.ds(TAP_PAIR_AT + j * OPIX, OPIX)], 2 + j) for j in range(5)]
-    for share in tap_shares:
+            if c in columns:
+                for k in LANES:
+                    cols = pl.ds(EDGE + c, OUT_C, stride=2)
+                    two = jnp.concatenate([grid[k, 4 * p + a, cols, :], grid[k, 4 * p + 2 + a, cols, :]], 0)
+                    taps[t, at(p * 2 * OUT_C, 2 * OUT_C), lane(k)] = two.astype(BF16)
+
+    def early(n, core):
+        return n + n // 2 + core * (n % 2)
+
+    def late(n, core):
+        return 4 - 2 * n + core * (5 * n - 3)
+
+    def share_tap(j, i):
+        rows = pl.ds(pl.multiple_of(TAP_PAIR_AT + j * OPIX, 32), OPIX)
+        share = to_pair(taps.at[4 * (1 - core) + j], xs.at[1, rows], 2 + i)
         share.start()
+        return share
 
     def down_tap(j):
-        res = dot_lhs_t(taps[4 * core + j], xs[1, G_AT:G_AT + OPIX, :])
-        put(own_d, j, res, False)
-    run(5, down_tap)
+        put(own_d, j, dot_lhs_t(taps[4 * core + j], xs[1, G_AT:G_AT + OPIX, :]), False)
+
+    z_border.finish(ROW)
+    run(OUT_R // 2, lambda p: tap_rows(p, (0, 1)))
+    tap_shares = [share_tap(early(n, 1 - core), n) for n in range(3)]
+    run(3, lambda n: down_tap(early(n, core)))
+    z_border.finish(COLUMN, CORNER)
+    run(OUT_R // 2, lambda p: tap_rows(p, (2,)))
+    tap_shares += [share_tap(late(n, 1 - core), 3 + n) for n in range(2)]
+    run(2, lambda n: down_tap(late(n, core)))
     g_share.wait()
     for share in tap_shares:
         share.wait()
@@ -369,8 +386,7 @@
     run(ROWS, pack)
     da_share = to_pair(da, da_pair, 7)
     da_share.start()
-    d_border.start(True)
-    d_border.start(False)
+    d_border.start(*ALL_PARTS)
     x_share.wait()
     pair_load = pltpu.make_async_copy(x_land, xs.at[1], load_sems.at[4])
     pair_load.start()
@@ -397,7 +413,7 @@
     first_tap(4)
     first.begin()
 
-    d_border.finish()
+    d_border.finish(*ALL_PARTS)
     spread(grid, xs)
     load_w1.wait()
 

time: 245 us -> 242 us (0.988)
  Pallas kernels: 244 us -> 241 us
where the time goes in v7:
time: 242 us
  Pallas kernels  241 us (100%)
    pallas_call x1, Pallas kernels, block_call(): pl.pallas_call(block_kernel, out_shape=[jax.ShapeDtypeStruct((OPIX, C), B...  231 us
    pallas_call x1, Pallas kernels, settle(): pl.pallas_call(settle_kernel, out_shape=[jax.ShapeDtypeStruct((OPIX, C),...  10.4 us

profile of v7, /device:TPU:0, one launch (start us, length us, event | category | flops | bytes accessed | tf_op | source)
XLA Modules:
  0.0 242.2 jit_solution(12023895918973424745)
XLA Ops:
  0.6 231.0 %shard_map.75 = (bf16[288,640]{1,0:T(8,128)(2,1)}, bf16[1152,640]{1,0:T(8,128)(2,1)S(1)}, f32[9,320,640]{2,1,0:T(8,128)S(1)}, f32[9,320,640]{2,1,0:T(8,128)S(1)}...) custom-call(bf16[1152,640]{1,0:T(8,128)(2,1)} %bitcast.12, ...), custom_call_target="tpu_custom_call" | custom-call | flops 84934656000 | bytes 67108864 | tf_op jit(solution)/shard_map/pallas_call | solution.py:451
  231.7 10.4 %shard_map.76 = (bf16[288,640]{1,0:T(8,128)(2,1)}, bf16[1152,640]{1,0:T(8,128)(2,1)}, f32[18,320,640]{2,1,0:T(8,128)}, f32[18,320,640]{2,1,0:T(8,128)}) custom-call(bf16[288,640]{1,0:T(8,128)(2,1)} %get-tuple-element.14.y_in, bf16[1152,640]{1,0:T(8,128)(2,1)S(1)} %get-tuple-element.15.dx_in, f32[9,320,640]{2,1,0:T(8,128)S(1)} %get-tuple-element.16.own_d, ...), custom_call_target="tpu_custom_call" | custom-call | tf_op jit(solution)/shard_map/pallas_call | solution.py:489

commit v8 on v7

--- a/solution.py
+++ b/solution.py
@@ -15,7 +15,7 @@
 MIB = 2 ** 20
 SCRATCH = 36000000
 ORDERS = (('x', 'y', 'z'), ('y', 'z', 'x'), ('z', 'x', 'y'))
-R1, R2, R3, A1, A2, A3A, A3B, DA, DB, DC = range(10)
+R1, R2, R3, A1, A2, A3A, A3B, A3C, DA, DB, DC, DD = range(12)
 QUARTER = HALF // 2
 EIGHTH = QUARTER // 2
 LEAST = EIGHTH // 2
@@ -69,8 +69,8 @@
         near1, far1 = b1 * EIGHTH, (1 - b1) * EIGHTH
         src, size, axis = {
             R1: (far, QUARTER, axis0), R2: (base2 + far1, EIGHTH, axis1), R3: (base3 + (1 - b2) * LEAST, LEAST, axis2),
-            A1: (base4, LEAST, axis2), A2: (base3, EIGHTH, axis1), A3A: (base3, EIGHTH, axis0), A3B: (base2 + far1, EIGHTH, axis0),
-            DA: (base2, QUARTER, 'c'), DB: (far + near1, EIGHTH, 'c'), DC: (far + far1, EIGHTH, 'c'),
+            A1: (base4, LEAST, axis2), A2: (base3, EIGHTH, axis1), A3A: (base3, EIGHTH, axis0), A3B: (base2 + far1, LEAST, axis0), A3C: (base2 + far1 + LEAST, LEAST, axis0),
+            DA: (base2, QUARTER, 'c'), DB: (far + near1, EIGHTH, 'c'), DC: (far + far1, LEAST, 'c'), DD: (far + far1 + LEAST, LEAST, 'c'),
         }[kind]
         rows = pl.ds(pl.multiple_of(src, 8), size)
         units = pl.ds(3 * third, 3)
@@ -78,7 +78,7 @@
         send, recv = (s.at[self.index, third, kind] for s in self.sems)
         if kind <= R3:
             target = self.pair.at[units, pl.ds(LAND_AT[kind], size)]
-        elif kind <= A3B:
+        elif kind <= A3C:
             target = source
         else:
             target = self.pair.at[units, rows]
@@ -95,8 +95,8 @@
             self.own[unit, rows, :] += self.pair[unit, pl.ds(pl.multiple_of(LAND_AT[kind] + row, 8), LEAST), :]
         run(3 * steps, body)
 
-    def begin(self):
-        for third in THIRDS:
+    def begin(self, *thirds):
+        for third in thirds:
             self.copy(third, R1).start()
 
     def move(self, wait_for, then, add=False):
@@ -115,7 +115,7 @@
                 self.copy(third, kind).start()
 
     def finish(self):
-        for kind in (DA, DB, DC):
+        for kind in (DA, DB, DC, DD):
             self.move(kind, ())
 
 
@@ -359,11 +359,12 @@
         share.wait()
 
     def down_tap_pair(j):
-        rows = pl.ds(pl.multiple_of(TAP_PAIR_AT + j * OPIX, 32), OPIX)
+        rows = pl.ds(TAP_PAIR_AT + j * OPIX, OPIX)
         res = dot_lhs_t(xs[1, rows, :], xs[1, G_PAIR_AT:G_PAIR_AT + OPIX, :])
         put(own_d, j, res, True)
-    run(5, down_tap_pair)
-    down.begin()
+    for j in range(5):
+        down_tap_pair(j)
+        down.begin(*{1: (0,), 3: (1,), 4: (2,)}.get(j, ()))
 
     load_w2.wait()
     for rp in range(2):
@@ -411,7 +412,7 @@
     run(4, first_tap)
     down.move(R1, (R2,), add=True)
     first_tap(4)
-    first.begin()
+    first.begin(*THIRDS)
 
     d_border.finish(*ALL_PARTS)
     spread(grid, xs)
@@ -431,13 +432,15 @@
     first.move(R2, (R3,), add=True)
     down.move(A1, (A2, A3A))
     first.move(R3, (A1,), add=True)
-    down.move(A2, (A3B, DA))
+    down.move(A2, (A3B, A3C, DA))
     first.move(A1, (A2, A3A))
     down.move(A3A, (DB,))
-    first.move(A2, (A3B, DA))
+    first.move(A2, (A3B, A3C, DA))
     down.move(A3B, (DC,))
+    down.move(A3C, (DD,))
     first.move(A3A, (DB,))
     first.move(A3B, (DC,))
+    first.move(A3C, (DD,))
     y_copy.wait()
     down.finish()
     first.finish()
@@ -458,7 +461,7 @@
         + [pltpu.VMEM((PIX, C), BF16)]
         + [pltpu.VMEM((5, ROWS + 2, COLS + 2 * EDGE, 128), F32), pltpu.VMEM((5, BLOCK, 128), F32)]
         + edges * 4 + small * 2
-        + [dma((6,)), dma((2, 8)), dma((4, 2, 8)), dma((2,)), dma((2, 3, 10)), dma((2, 3, 10)), pltpu.SemaphoreType.REGULAR((2, 3, 4))],
+        + [dma((6,)), dma((2, 8)), dma((4, 2, 8)), dma((2,)), dma((2, 3, 12)), dma((2, 3, 12)), pltpu.SemaphoreType.REGULAR((2, 3, 4))],
         compiler_params=pltpu.CompilerParams(collective_id=1, has_side_effects=True, vmem_limit_bytes=SCRATCH),
         cost_estimate=pl.CostEstimate(flops=2 * PIX * 90 * C * C, bytes_accessed=64 * MIB, transcendentals=0),
     )(image.reshape(PIX, C), grad_out, w_first, w_down)

time: 242 us -> 241 us (level)
  no operation moved by 1% of the time
where the time goes in v8:
time: 241 us
  Pallas kernels  240 us (100%)
    pallas_call x1, Pallas kernels, block_call(): pl.pallas_call(block_kernel, out_shape=[jax.ShapeDtypeStruct((OPIX, C), B...  230 us
    pallas_call x1, Pallas kernels, settle(): pl.pallas_call(settle_kernel, out_shape=[jax.ShapeDtypeStruct((OPIX, C),...  10.4 us

profile of v8, /device:TPU:0, one launch (start us, length us, event | category | flops | bytes accessed | tf_op | source)
XLA Modules:
  0.0 240.7 jit_solution(8071269634692705589)
XLA Ops:
  0.6 229.5 %shard_map.75 = (bf16[288,640]{1,0:T(8,128)(2,1)}, bf16[1152,640]{1,0:T(8,128)(2,1)S(1)}, f32[9,320,640]{2,1,0:T(8,128)S(1)}, f32[9,320,640]{2,1,0:T(8,128)S(1)}...) custom-call(bf16[1152,640]{1,0:T(8,128)(2,1)} %bitcast.12, ...), custom_call_target="tpu_custom_call" | custom-call | flops 84934656000 | bytes 67108864 | tf_op jit(solution)/shard_map/pallas_call | solution.py:454
  230.2 10.4 %shard_map.76 = (bf16[288,640]{1,0:T(8,128)(2,1)}, bf16[1152,640]{1,0:T(8,128)(2,1)}, f32[18,320,640]{2,1,0:T(8,128)}, f32[18,320,640]{2,1,0:T(8,128)}) custom-call(bf16[288,640]{1,0:T(8,128)(2,1)} %get-tuple-element.14.y_in, bf16[1152,640]{1,0:T(8,128)(2,1)S(1)} %get-tuple-element.15.dx_in, f32[9,320,640]{2,1,0:T(8,128)S(1)} %get-tuple-element.16.own_d, ...), custom_call_target="tpu_custom_call" | custom-call | tf_op jit(solution)/shard_map/pallas_call | solution.py:492

commit v9 on v8

--- a/solution.py
+++ b/solution.py
@@ -349,11 +349,13 @@
     z_border.finish(ROW)
     run(OUT_R // 2, lambda p: tap_rows(p, (0, 1)))
     tap_shares = [share_tap(early(n, 1 - core), n) for n in range(3)]
-    run(3, lambda n: down_tap(early(n, core)))
+    for n in range(3):
+        down_tap(early(n, core))
     z_border.finish(COLUMN, CORNER)
     run(OUT_R // 2, lambda p: tap_rows(p, (2,)))
     tap_shares += [share_tap(late(n, 1 - core), 3 + n) for n in range(2)]
-    run(2, lambda n: down_tap(late(n, core)))
+    for n in range(2):
+        down_tap(late(n, core))
     g_share.wait()
     for share in tap_shares:
         share.wait()

time: 241 us -> 241 us (level)
  no operation moved by 1% of the time
where the time goes in v9:
time: 241 us
  Pallas kernels  240 us (100%)
    pallas_call x1, Pallas kernels, block_call(): pl.pallas_call(block_kernel, out_shape=[jax.ShapeDtypeStruct((OPIX, C), B...  230 us
    pallas_call x1, Pallas kernels, settle(): pl.pallas_call(settle_kernel, out_shape=[jax.ShapeDtypeStruct((OPIX, C),...  10.4 us

profile of v9, /device:TPU:0, one launch (start us, length us, event | category | flops | bytes accessed | tf_op | source)
XLA Modules:
  0.0 240.9 jit_solution(13348030518821003942)
XLA Ops:
  0.6 229.7 %shard_map.75 = (bf16[288,640]{1,0:T(8,128)(2,1)}, bf16[1152,640]{1,0:T(8,128)(2,1)S(1)}, f32[9,320,640]{2,1,0:T(8,128)S(1)}, f32[9,320,640]{2,1,0:T(8,128)S(1)}...) custom-call(bf16[1152,640]{1,0:T(8,128)(2,1)} %bitcast.12, ...), custom_call_target="tpu_custom_call" | custom-call | flops 84934656000 | bytes 67108864 | tf_op jit(solution)/shard_map/pallas_call | solution.py:456
  230.4 10.4 %shard_map.76 = (bf16[288,640]{1,0:T(8,128)(2,1)}, bf16[1152,640]{1,0:T(8,128)(2,1)}, f32[18,320,640]{2,1,0:T(8,128)}, f32[18,320,640]{2,1,0:T(8,128)}) custom-call(bf16[288,640]{1,0:T(8,128)(2,1)} %get-tuple-element.14.y_in, bf16[1152,640]{1,0:T(8,128)(2,1)S(1)} %get-tuple-element.15.dx_in, f32[9,320,640]{2,1,0:T(8,128)S(1)} %get-tuple-element.16.own_d, ...), custom_call_target="tpu_custom_call" | custom-call | tf_op jit(solution)/shard_map/pallas_call | solution.py:494
